TPU v7x, 256 devices: a whole 4x4x8 slice. The times are simulated.
256 devices in a mesh: band: 64 (over x, z, y_hi), img: 4 (over y_lo, core).
Axes of the slice: x: 4, y: 4 (y_hi: 2, y_lo: 2; y = y_hi * 2 + y_lo), z: 8, core: 2. Of those that a mesh axis runs over, the one named last changes fastest.
Arguments:
- pixels: bfloat16 [2048, 256, 180], P(('img', 'band')), parts along dimension 0, may hold values from -12 to 12
- keep_mask: int32 [256, 32], P(('img', 'band')), parts along dimension 0, may hold values from 0 to 1, as said below
- band_counts: int32 [256], P(('img', 'band')), parts along dimension 0, may hold values from 0 to 32, as said below
- plan_dest: int32 [256, 16], P(('img', 'band')), parts along dimension 0, may hold values from 0 to 63, as said below
- plan_slot: int32 [256, 16], P(('img', 'band')), parts along dimension 0, may hold values from 0 to 8, as said below
- bias_table: float32 [225, 6], replicated, may hold values from -4 to 4
- gain_attn: float32 [180], replicated, may hold values from 0.25 to 1.75
- qkv_weight: bfloat16 [180, 540], replicated, may hold values from -5 to 5
- proj_weight: bfloat16 [180, 180], replicated, may hold values from -0.4375 to 0.4375
- gain_mlp: float32 [180], replicated, may hold values from 0.25 to 1.75
- hidden_weight: bfloat16 [180, 360], replicated, may hold values from -0.4375 to 0.4375
- output_weight: bfloat16 [360, 180], replicated, may hold values from -0.3125 to 0.3125
Outputs:
- restored: bfloat16 [2048, 256, 180], P(('img', 'band')), parts along dimension 0
- work_tiles: bfloat16 [2048, 128, 180], P(('img', 'band')), parts along dimension 0
There are 4 independent parts, one for each index of `img`. A program takes and returns all parts, laid end to end along the dimension named above; an argument that names none is the same for every part. Nothing has to cross between parts.
Inputs may be any that keep to these rules, and one draw needn't show every extreme that they name: `keep_mask`: the number of ones in a band varies strongly from band to band. band_counts[b] equals the number of ones among band b's windows in keep_mask. A band's live tiles are those with 2 t < band_counts[b]; their number summed over bands lies between 449 and 512, and some band has all 16 tiles live. `plan_dest`: within each aligned group of 64 consecutive tiles of a band (equal t // 64) the destinations are all different. `plan_slot`: 8 for tiles that are not live; a live tile has a slot below 8, no two live tiles of the image share destination and slot, and some destination receives 8 live tiles.
All inputs are finite; a program needn't handle non-finite values.
Results may differ from a plain program's by a relative error of at most 0.0044.
Values may be sent and summed in bfloat16 or wider, within the bound.
No kernel may reach another device: no remote copies, remote signals or barrier semaphores. Data moves between devices by JAX's collectives and lax.ppermute only.
A program may use at most 64 MiB of HBM per device.

v0:
```python
import jax
import jax.numpy as jnp
from jax import lax
from jax.sharding import PartitionSpec as P

CHAN = 180
HEADS = 6
WIN = 8
TILE = 2
SHIFT = 4
CAP = 8


EPSILON = 1e-05


def from_behind(value, axis, steps):
    count = lax.axis_size(axis)
    pairs = [(source, (source + steps) % count) for source in range(count)]
    return lax.ppermute(value, axis, pairs)


def layer_norm(values, gain_vec):
    values = values.astype(jnp.float32)
    center = values - jnp.mean(values, axis=-1, keepdims=True)
    spread = jnp.mean(center * center, axis=-1, keepdims=True)
    return center * lax.rsqrt(spread + EPSILON) * gain_vec


def position_bias(bias_table):
    coords = jnp.arange(WIN * WIN, dtype=jnp.int32)
    row_pos = coords // WIN
    col_pos = coords % WIN
    table_index = (row_pos[:, None] - row_pos[None, :] + WIN - 1) * (2 * WIN - 1) + (
        col_pos[:, None] - col_pos[None, :] + WIN - 1
    )
    entries = bias_table.shape[0]
    onehot = (table_index.reshape(-1, 1) == jnp.arange(entries, dtype=jnp.int32)[None, :]).astype(
        jnp.float32
    )
    looked = jnp.dot(onehot, bias_table, precision=lax.Precision.HIGHEST)
    return jnp.transpose(looked.reshape(WIN * WIN, WIN * WIN, -1), (2, 0, 1))


def region_codes(first_row, row_count, height, col_count):
    rows_global = first_row + jnp.arange(row_count, dtype=jnp.int32)
    row_region = (rows_global >= height - WIN).astype(jnp.int32) + (
        rows_global >= height - SHIFT
    ).astype(jnp.int32)
    col_global = jnp.arange(col_count, dtype=jnp.int32)
    col_region = (col_global >= col_count - WIN).astype(jnp.int32) + (
        col_global >= col_count - SHIFT
    ).astype(jnp.int32)
    return 3 * row_region[:, None] + col_region[None, :]


def attend(windows, window_codes, head_bias, gain_attn, qkv_weight, proj_weight):
    window_count = windows.shape[0]
    head_dim = CHAN // HEADS
    normed = layer_norm(windows, gain_attn).astype(jnp.bfloat16).reshape(-1, CHAN)
    mixed_all = jnp.dot(normed, qkv_weight, preferred_element_type=jnp.float32).reshape(
        window_count, WIN * WIN, 3, HEADS, head_dim
    )
    queries = mixed_all[:, :, 0] * head_dim ** (-0.5)
    key_part = mixed_all[:, :, 1]
    value_part = mixed_all[:, :, 2].astype(jnp.bfloat16)
    scores = jnp.einsum("wqhd,wkhd->whqk", queries, key_part, precision=lax.Precision.HIGHEST)
    differ = window_codes[:, :, None] != window_codes[:, None, :]
    scores = scores + head_bias[None] + jnp.where(differ, -100.0, 0.0)[:, None]
    weights = jax.nn.softmax(scores, axis=-1).astype(jnp.bfloat16)
    mixed = jnp.einsum("whqk,wkhd->wqhd", weights, value_part, preferred_element_type=jnp.float32)
    mixed = mixed.reshape(-1, CHAN).astype(jnp.bfloat16)
    projected = jnp.dot(mixed, proj_weight, preferred_element_type=jnp.float32)
    summed = windows.reshape(-1, CHAN).astype(jnp.float32) + projected
    return summed.astype(jnp.bfloat16).reshape(window_count, WIN * WIN, CHAN)


def feed(states, gain_mlp, hidden_weight, output_weight):
    flat_rows = states.reshape(-1, CHAN)
    normed = layer_norm(flat_rows, gain_mlp).astype(jnp.bfloat16)
    inner_act = jax.nn.gelu(
        jnp.dot(normed, hidden_weight, preferred_element_type=jnp.float32)
    ).astype(jnp.bfloat16)
    summed = flat_rows.astype(jnp.float32) + jnp.dot(
        inner_act, output_weight, preferred_element_type=jnp.float32
    )
    return summed.astype(jnp.bfloat16).reshape(states.shape)


def shards(
    pixels,
    keep_mask,
    band_counts,
    plan_dest,
    plan_slot,
    bias_table,
    gain_attn,
    qkv_weight,
    proj_weight,
    gain_mlp,
    hidden_weight,
    output_weight,
):
    band_total = lax.axis_size("band")
    band_index = lax.axis_index("band")
    row_count, col_count, channels = pixels.shape
    win_rows = row_count // WIN
    win_cols = col_count // WIN
    window_total = win_rows * win_cols
    tile_total = window_total // TILE
    tile_tokens = TILE * WIN * WIN
    pair_slots = -(-tile_total // band_total)
    lower_rows = from_behind(pixels[:SHIFT], "band", -1)
    shifted = jnp.roll(jnp.concatenate([pixels[SHIFT:], lower_rows], axis=0), -SHIFT, axis=1)
    windows = (
        shifted.reshape(win_rows, WIN, win_cols, WIN, channels)
        .transpose(0, 2, 1, 3, 4)
        .reshape(window_total, WIN * WIN, channels)
    )
    region_map = region_codes(band_index * row_count, row_count, band_total * row_count, col_count)
    window_codes = (
        region_map.reshape(win_rows, WIN, win_cols, WIN)
        .transpose(0, 2, 1, 3)
        .reshape(window_total, WIN * WIN)
    )
    band_keep = keep_mask.reshape(window_total)
    kept_count = band_counts[0]
    packed_order = jnp.cumsum(band_keep) - 1
    active = (band_keep == 1) & (packed_order < kept_count)
    target = jnp.where(active, packed_order, window_total)
    packed = (
        jnp.zeros((window_total + 1, WIN * WIN, channels), jnp.bfloat16)
        .at[target]
        .set(windows)[:window_total]
    )
    packed_codes = (
        jnp.zeros((window_total + 1, WIN * WIN), jnp.bfloat16)
        .at[target]
        .set(window_codes.astype(jnp.bfloat16))[:window_total]
    )
    tile_ids = jnp.arange(tile_total, dtype=jnp.int32)
    tile_live = tile_ids * TILE < kept_count
    destinations = plan_dest[0]
    pair_index = tile_ids // band_total
    sent_slot = jnp.where(tile_live, plan_slot[0], CAP).astype(jnp.bfloat16)
    outgoing_slots = (
        jnp.full((band_total, pair_slots), CAP, jnp.bfloat16)
        .at[destinations, pair_index]
        .set(sent_slot)
    )
    head_bias = position_bias(bias_table)
    own_attended = attend(packed, packed_codes, head_bias, gain_attn, qkv_weight, proj_weight)
    flat_done = feed(own_attended, gain_mlp, hidden_weight, output_weight)
    outgoing = (
        jnp.zeros((band_total, pair_slots, tile_tokens, channels), jnp.bfloat16)
        .at[destinations, pair_index]
        .set(own_attended.reshape(tile_total, tile_tokens, channels))
    )
    incoming, incoming_slots = (
        lax.all_to_all(outgoing, "band", split_axis=0, concat_axis=0, tiled=True),
        lax.all_to_all(outgoing_slots, "band", split_axis=0, concat_axis=0, tiled=True),
    )
    arrived_slot = incoming_slots.reshape(-1).astype(jnp.int32)
    attended = (
        jnp.zeros((CAP, tile_tokens, channels), jnp.bfloat16)
        .at[arrived_slot]
        .set(incoming.reshape(-1, tile_tokens, channels), mode="drop")
    )
    gathered = flat_done[jnp.clip(packed_order, 0, window_total - 1)]
    result = jnp.where(active[:, None, None], gathered, windows)
    band_shifted = (
        result.reshape(win_rows, win_cols, WIN, WIN, channels)
        .transpose(0, 2, 1, 3, 4)
        .reshape(row_count, col_count, channels)
    )
    band_shifted = jnp.roll(band_shifted, SHIFT, axis=1)
    upper_rows = from_behind(band_shifted[row_count - SHIFT :], "band", 1)
    restored = jnp.concatenate([upper_rows, band_shifted[: row_count - SHIFT]], axis=0)
    return (restored, attended)


def solution(mesh):
    in_specs = (
        P(("img", "band"), None, None),
        P(("img", "band"), None),
        P(("img", "band")),
        P(("img", "band"), None),
        P(("img", "band"), None),
        P(),
        P(),
        P(),
        P(),
        P(),
        P(),
        P(),
    )
    out_specs = (P(("img", "band"), None, None), P(("img", "band"), None, None))
    return jax.shard_map(shards, mesh=mesh, in_specs=in_specs, out_specs=out_specs, check_vma=False)
```

profile of v0, /device:TPU:1, one launch (start us, length us, event | category | flops | bytes accessed | tf_op | source)
XLA Modules:
  0.0 172.8 jit_solution(14152191948323769649)
XLA Ops:
  0.7 1.7 fusion.72
  2.7 11.3 %collective-permute-start = (bf16[4,256,180]{2,1,0:T(8,128)(2,1)S(1)}, bf16[4,256,180]{2,1,0:T(8,128)(2,1)S(1)}, u32[]{:S(2)}, u32[]{:S(2)}) collective-permute-start(bf16[4,256,180]{2,1,0:T(8,128)(2,1)S(1)} %copy.93), channel_id=1, source_target_pairs={{0,252},{4,0},{8,4},{12,8},{16,12},{20,16},{24,20},{28,24},{32,28}... | collective-permute-start | bytes 1105928 | tf_op jit(solution)/shard_map/ppermute | solution.py:20
  16.1 5.3 %all-to-all-start = ((bf16[64,1,1]{2,1,0:T(2,128)(2,1)}), bf16[64,1,1]{2,1,0:T(2,128)(2,1)}, u32[]{:S(2)}, u32[]{:S(2)}) async-start(bf16[64,1,1]{2,1,0:T(2,128)(2,1)} %copy.85), calls=%async_computation | async-start | bytes 65536 | tf_op jit(solution)/shard_map/all_to_all | solution.py:161
  22.0 0.8 reshape.421
  24.1 2.6 %fusion.2 = f32[4096,6]{0,1:T(8,128)S(1)} fusion(f32[225,6]{0,1:T(8,128)S(1)} %copy-done.13, s32[4096]{0:T(1024)S(1)} %add.237), kind=kOutput, calls=%fused_computation.13 | convolution fusion | flops 67276800 | bytes 120088 | tf_op jit(solution)/shard_map/dot_general | solution.py:41
  26.9 1.3 compare_select_fusion
  28.5 1.4 copy_bitcast_fusion
  30.0 3.8 %scatter_fusion = bf16[33,64,180]{2,1,0:T(8,128)(2,1)S(1)} fusion(bf16[33,64,180]{2,1,0:T(8,128)(2,1)S(1)} %broadcast_in_dim.32, s32[32]{0:T(128)S(1)} %get-tuple-element.13, bf16[32,64,180]{2,1,0:T(8,128)(2,1)} %copy_bitcast_fusion), kind=kCustom, calls=%fused_computation.1 | custom fusion | bytes 2211968 | tf_op jit(solution)/shard_map/scatter | solution.py:134
  35.1 1.5 fusion.33
  36.6 10.5 %fusion.3 = f32[32,6,64,64]{2,3,1,0:T(8,128)S(1)} fusion(f32[32,64,3,6,30]{1,4,3,2,0:T(8,128)S(1)} %fusion.33), kind=kOutput, calls=%fused_computation.15 | convolution fusion | flops 283484160 | bytes 9437184 | tf_op jit(solution)/shard_map/wqhd,wkhd->whqk/dot_general | solution.py:67
  47.1 3.7 %fusion.73 = (f32[32,6,64]{2,1,0:T(8,128)S(1)}, f32[32,6,64,64]{2,3,1,0:T(8,128)}) fusion(f32[32,6,64,64]{2,3,1,0:T(8,128)S(1)} %fusion.3, f32[32,64,64]{1,2,0:T(8,128)S(1)} %copy-done.7, f32[6,64,64]{1,2,0:T(8,128)S(1)} %bitcast.92), kind=kOutput, calls=%fused_computation.124 | output fusion | flops 4718655 | bytes 6963200 | tf_op jit(solution)/shard_map/sub | solution.py:70
  50.9 3.8 %fusion.29 = bf16[32,64,6,30]{1,3,2,0:T(8,128)(2,1)S(1)} fusion(f32[32,6,64,64]{2,3,1,0:T(8,128)} %get-tuple-element.17, f32[32,6,64]{2,1,0:T(8,128)S(1)} %get-tuple-element.16, f32[32,64,3,6,30]{1,4,3,2,0:T(8,128)S(1)} %fusion.33), kind=kOutput, calls=%fused_computation.48 | convolution fusion | flops 49127424 | bytes 5586944 | tf_op jit(solution)/shard_map/whqk,wkhd->wqhd/dot_general | solution.py:71
  54.7 2.1 %copy.81 = bf16[32,64,6,30]{1,0,3,2:T(8,128)(2,1)} copy(bf16[32,64,6,30]{1,3,2,0:T(8,128)(2,1)S(1)} %fusion.29) | data formatting | bytes 1474560 | tf_op jit(solution)/shard_map/convert_element_type | solution.py:72
  56.8 2.6 %convert_element_type.113 = bf16[2048,180]{0,1:T(8,128)(2,1)S(1)} reshape(bf16[32,64,6,30]{1,0,3,2:T(8,128)(2,1)} %copy.81) | data formatting | bytes 1474560 | tf_op jit(solution)/shard_map/convert_element_type | solution.py:72
  59.5 1.7 copy.82
  61.1 1.8 %convert_reduce_fusion = (f32[2048]{0:T(1024)S(1)}, bf16[2048,180]{0,1:T(8,128)(2,1)S(1)}) fusion(f32[2048,180]{0,1:T(8,128)} %copy.82, bf16[2048,180]{0,1:T(8,128)(2,1)S(1)} %convert_element_type.113, bf16[180,180]{1,0:T(8,128)(2,1)S(1)} %copy-done.9), kind=kOutput, calls=%fused_computation.35 | convolution fusion | flops 134182912 | bytes 3022112 | tf_op jit(solution)/shard_map/dot_general | solution.py:73
  63.8 1.1 copy.86
  65.3 2.2 %scatter_fusion.1 = bf16[64,128,180]{1,2,0:T(8,128)(2,1)S(1)} fusion(bf16[64,128,180]{1,2,0:T(8,128)(2,1)S(1)} %broadcast.482, s32[16]{0:T(128)S(1)} %fusion.63, bf16[16,128,180]{1,2,0:T(8,128)(2,1)} %copy.86), kind=kCustom, calls=%fused_computation.4 | custom fusion | bytes 2211904 | tf_op jit(solution)/shard_map/scatter | solution.py:157
  67.5 1.6 copy-done.1
  69.1 12.2 %all-to-all-start.1 = ((bf16[64,1,128,180]{2,3,1,0:T(8,128)(2,1)}), bf16[64,1,128,180]{2,3,1,0:T(8,128)(2,1)S(1)}, u32[]{:S(2)}, u32[]{:S(2)}) async-start(bf16[64,1,128,180]{2,3,1,0:T(8,128)(2,1)} %bitcast.84), calls=%async_computation.1 | async-start | bytes 6029312 | tf_op jit(solution)/shard_map/all_to_all | solution.py:160
  81.5 1.3 fusion.26
  82.9 3.7 %fusion.18 = bf16[2048,180]{0,1:T(8,128)(2,1)} fusion(bf16[360,180]{0,1:T(8,128)(2,1)S(1)} %copy-done, bf16[2048,180]{0,1:T(8,128)(2,1)} %copy-done.4, bf16[180,360]{1,0:T(8,128)(2,1)S(1)} %copy-done.12, f32[180]{0:T(256)S(1)} %copy-done.14, f32[2048]{0:T(1024)S(1)} %add_rsqrt_fusion.1, f32[2048]{0:T(1024)S(1)} %broadcast_multiply_fusion.1), kind=kOutput, calls=%fused_computation.33 | convolution fusion | flops 540426240 | bytes 1750864 | tf_op jit(solution)/shard_map/dot_general | solution.py:84
  86.6 2.2 %copy.83 = bf16[2048,180]{1,0:T(8,128)(2,1)} copy(bf16[2048,180]{0,1:T(8,128)(2,1)} %fusion.18) | data formatting | bytes 1474560 | tf_op jit(solution)/shard_map/convert_element_type | solution.py:87
  88.8 2.8 %gather_fusion = bf16[32,64,180]{2,1,0:T(8,128)(2,1)} fusion(bf16[32,64,180]{2,1,0:T(8,128)(2,1)} %bitcast.89, s32[1024]{0:T(1024)S(1)} %pad_clamp_fusion), kind=kCustom, calls=%fused_computation | custom fusion | bytes 1474688 | tf_op jit(solution)/shard_map/gather | solution.py:169
  91.6 1.9 %fusion.38 = bf16[8,256,180]{2,1,0:T(8,128)(2,1)S(1)} fusion(pred[32]{0:T(512)(128)(4,1)S(1)} %bitcast_and_fusion, bf16[4,256,180]{2,1,0:T(8,128)(2,1)} %copy-done.5, bf16[4,256,180]{2,1,0:T(8,128)(2,1)} %copy-done.3, bf16[8,252,180]{2,1,0:T(8,128)(2,1)} %copy-done.2, bf16[32,64,180]{2,1,0:T(8,128)(2,1)} %gather_fusion), kind=kLoop, calls=%fused_computation.60 | loop fusion | flops 2580480 | bytes 2937632 | tf_op jit(solution)/shard_map/reshape | solution.py:174
  93.7 2.6 %collective-permute-start.1 = (bf16[4,256,180]{2,1,0:T(8,128)(2,1)S(1)}, bf16[4,256,180]{2,1,0:T(8,128)(2,1)S(1)}, u32[]{:S(2)}, u32[]{:S(2)}) collective-permute-start(bf16[4,256,180]{2,1,0:T(8,128)(2,1)S(1)} %fusion.51), channel_id=1, source_target_pairs={{0,4},{4,8},{8,12},{12,16},{16,20},{20,24},{24,28},{28,32},{32,36}... | collective-permute-start | bytes 1105928 | tf_op jit(solution)/shard_map/ppermute | solution.py:20
  96.3 2.0 %convert_reduce_fusion.2 = s32[64]{0:T(128)S(1)} fusion(bf16[64,1,1]{2,1,0:T(2,128)(2,1)} %all-to-all-done), kind=kLoop, calls=%fused_computation.75 | loop fusion | flops 64 | bytes 384 | tf_op jit(solution)/shard_map/convert_element_type | solution.py:163
  98.3 66.0 %collective-permute-done.1 = bf16[4,256,180]{2,1,0:T(8,128)(2,1)S(1)} collective-permute-done((bf16[4,256,180]{2,1,0:T(8,128)(2,1)S(1)}, bf16[4,256,180]{2,1,0:T(8,128)(2,1)S(1)}, u32[]{:S(2)}, u32[]{:S(2)}) %collective-permute-start.1) | collective-permute-done | bytes 368672 | tf_op jit(solution)/shard_map/ppermute | solution.py:20
  164.3 1.2 fusion.35
  165.5 2.3 %copy.88 = bf16[8,256,180]{1,0,2:T(8,128)(2,1)} copy(bf16[8,256,180]{2,1,0:T(8,128)(2,1)} %fusion.35) | data formatting | bytes 1474560
  167.9 4.1 %scatter_fusion.2 = bf16[8,128,180]{1,2,0:T(8,128)(2,1)S(1)} fusion(bf16[8,128,180]{1,2,0:T(8,128)(2,1)S(1)} %broadcast_in_dim.37, s32[64]{0:T(128)S(1)} %fusion.64, bf16[64,128,180]{1,2,0:T(8,128)(2,1)S(1)} %bitcast.83), kind=kCustom, calls=%fused_computation.5 | custom fusion | bytes 8847616 | tf_op jit(solution)/shard_map/scatter | solution.py:167
  172.0 0.8 copy.89
  (76 shorter events, 7.0 us)
Async XLA Ops:
  0.6 82.2 %copy-start = (bf16[360,180]{0,1:T(8,128)(2,1)S(1)}, bf16[360,180]{0,1:T(8,128)(2,1)}, u32[]{:S(2)}) copy-start(bf16[360,180]{0,1:T(8,128)(2,1)} %param.23) | copy-start | bytes 388804
  0.6 14.0 %copy-start.15 = (s32[1,16]{1,0:T(1,128)S(1)}, s32[1,16]{1,0:T(1,128)}, u32[]{:S(2)}) copy-start(s32[1,16]{1,0:T(1,128)} %param.15) | copy-start | bytes 196
  0.7 14.0 %copy-start.16 = (s32[1,16]{1,0:T(1,128)S(1)}, s32[1,16]{1,0:T(1,128)}, u32[]{:S(2)}) copy-start(s32[1,16]{1,0:T(1,128)} %param.16) | copy-start | bytes 196
  0.7 21.1 %copy-start.11 = (s32[1,32]{1,0:T(1,128)S(1)}, s32[1,32]{1,0:T(1,128)}, u32[]{:S(2)}) copy-start(s32[1,32]{1,0:T(1,128)} %param.13) | copy-start | bytes 388
  0.7 21.2 %copy-start.8 = (bf16[180,540]{1,0:T(8,128)(2,1)S(1)}, bf16[180,540]{1,0:T(8,128)(2,1)}, u32[]{:S(2)}) copy-start(bf16[180,540]{1,0:T(8,128)(2,1)} %param.19) | copy-start | bytes 583204
  0.7 23.4 %copy-start.13 = (f32[225,6]{0,1:T(8,128)S(1)}, f32[225,6]{0,1:T(8,128)}, u32[]{:S(2)}) copy-start(f32[225,6]{0,1:T(8,128)} %param.17) | copy-start | bytes 16204
  2.7 25.5 %collective-permute-start = (bf16[4,256,180]{2,1,0:T(8,128)(2,1)S(1)}, bf16[4,256,180]{2,1,0:T(8,128)(2,1)S(1)}, u32[]{:S(2)}, u32[]{:S(2)}) collective-permute-start(bf16[4,256,180]{2,1,0:T(8,128)(2,1)S(1)} %copy.93), channel_id=1, source_target_pairs={{0,252},{4,0},{8,4},{12,8},{16,12},{20,16},{24,20},{28,24},{32,28}... | collective-permute-start | bytes 1105928 | tf_op jit(solution)/shard_map/ppermute | solution.py:20
  16.1 51.4 %all-to-all-start = ((bf16[64,1,1]{2,1,0:T(2,128)(2,1)}), bf16[64,1,1]{2,1,0:T(2,128)(2,1)}, u32[]{:S(2)}, u32[]{:S(2)}) async-start(bf16[64,1,1]{2,1,0:T(2,128)(2,1)} %copy.85), calls=%async_computation | async-start | bytes 65536 | tf_op jit(solution)/shard_map/all_to_all | solution.py:161
  21.8 6.7 %copy-start.3 = (bf16[4,256,180]{2,1,0:T(8,128)(2,1)}, bf16[4,256,180]{2,1,0:T(8,128)(2,1)S(1)}, u32[]{:S(2)}) copy-start(bf16[4,256,180]{2,1,0:T(8,128)(2,1)S(1)} %copy.92) | copy-start | bytes 1105924
  28.2 1.7 copy-start.5
  28.5 1.4 copy-start.2
  34.1 1.0 copy-start.6
  34.1 1.0 copy-start.10
  36.6 10.5 %copy-start.7 = (f32[32,64,64]{1,2,0:T(8,128)S(1)}, f32[32,64,64]{1,2,0:T(8,128)}, u32[]{:S(2)}) copy-start(f32[32,64,64]{1,2,0:T(8,128)} %compare_select_fusion) | copy-start | bytes 1572868
  59.4 1.7 copy-start.9
  63.0 0.9 copy-start.4
  67.5 1.6 copy-start.1
  69.1 13.8 %copy-start.12 = (bf16[180,360]{1,0:T(8,128)(2,1)S(1)}, bf16[180,360]{1,0:T(8,128)(2,1)}, u32[]{:S(2)}) copy-start(bf16[180,360]{1,0:T(8,128)(2,1)} %param.22) | copy-start | bytes 388804
  69.1 13.8 %copy-start.14 = (f32[180]{0:T(256)S(1)}, f32[180]{0:T(256)}, u32[]{:S(2)}) copy-start(f32[180]{0:T(256)} %param.21) | copy-start | bytes 2164
  69.1 98.7 %all-to-all-start.1 = ((bf16[64,1,128,180]{2,3,1,0:T(8,128)(2,1)}), bf16[64,1,128,180]{2,3,1,0:T(8,128)(2,1)S(1)}, u32[]{:S(2)}, u32[]{:S(2)}) async-start(bf16[64,1,128,180]{2,3,1,0:T(8,128)(2,1)} %bitcast.84), calls=%async_computation.1 | async-start | bytes 6029312 | tf_op jit(solution)/shard_map/all_to_all | solution.py:160
  93.7 70.6 %collective-permute-start.1 = (bf16[4,256,180]{2,1,0:T(8,128)(2,1)S(1)}, bf16[4,256,180]{2,1,0:T(8,128)(2,1)S(1)}, u32[]{:S(2)}, u32[]{:S(2)}) collective-permute-start(bf16[4,256,180]{2,1,0:T(8,128)(2,1)S(1)} %fusion.51), channel_id=1, source_target_pairs={{0,4},{4,8},{8,12},{12,16},{16,20},{20,24},{24,28},{28,32},{32,36}... | collective-permute-start | bytes 1105928 | tf_op jit(solution)/shard_map/ppermute | solution.py:20
where the time goes:
time: 174 us; the launch traced here: 173 us
  waiting for transfers between devices  66 us (38%)
  local copies, waits for them, and re-layouts  34.5 us (20%)
  starting transfers between devices  31.5 us (18%)
  matrix products  23.9 us (14%)
  other arithmetic  15.1 us (9%)
  between operations  1.78 us (1%)
    ppermute x2, waiting for transfers between devices, from_behind(): return lax.ppermute(value, axis, pairs)  66 us
    ppermute x2, starting transfers between devices, from_behind(): return lax.ppermute(value, axis, pairs)  13.9 us
    all_to_all x1, starting transfers between devices, shards(): lax.all_to_all(outgoing, 'band', split_axis=0, concat_axis=0, tiled=True)  12.2 us
    dot_general x1, matrix products, attend(): jnp.einsum('wqhd,wkhd->whqk', queries, key_part, precision=lax.Precision....  10.5 us
    unnamed x39, local copies, waits for them, and re-layouts  6.07 us
    all_to_all x1, starting transfers between devices, shards(): lax.all_to_all(outgoing_slots, 'band', split_axis=0, concat_axis=0, tiled...  5.33 us
    convert_element_type x2, local copies, waits for them, and re-layouts, attend(): mixed = mixed.reshape(-1, CHAN).astype(jnp.bfloat16)  4.7 us
    scatter x1, local copies, waits for them, and re-layouts, shards(): attended = jnp.zeros((CAP, tile_tokens, channels), jnp.bfloat16).at[arriv...  4.13 us
  transfers between devices with their start and end apart: 4, of which 1 were waited for; matrix products, arithmetic and copies ran while one was open for 37% of the time, Pallas kernels for 0%

commit v1 on v0

v1 whole, which is shorter than its diff:
```python
import functools

import jax
import jax.numpy as jnp
from jax import lax
from jax.experimental import pallas as pl
from jax.experimental.pallas import tpu as pltpu
from jax.sharding import PartitionSpec as P

CHAN = 180
HEADS = 6
HEAD_DIM = CHAN // HEADS
HEAD_PAD = 32
WIN = 8
TOKENS = WIN * WIN
TILE = 2
PAIR = TILE * TOKENS
SHIFT = 4
CAP = 8
TAIL = CHAN - 128
EPSILON = 1e-05

F32 = jnp.float32
BF16 = jnp.bfloat16


def dot(left, right, left_dim=1, right_dim=0):
    return lax.dot_general(
        left,
        right,
        (((left_dim,), (right_dim,)), ((), ())),
        preferred_element_type=F32,
    )


def layer_norm(values, gain):
    center = values - jnp.sum(values, axis=-1, keepdims=True) * (1.0 / CHAN)
    spread = jnp.sum(center * center, axis=-1, keepdims=True) * (1.0 / CHAN)
    return center * lax.rsqrt(spread + EPSILON) * gain


def region_mask(row_flag, col_flags):
    shape = (TOKENS, PAIR)
    key = lax.broadcasted_iota(jnp.int32, shape, 0)
    lane = lax.broadcasted_iota(jnp.int32, shape, 1)
    first = lane < TOKENS
    row_differs = ((key >> 5) & 1) ^ ((lane >> 5) & 1)
    col_differs = ((key >> 2) & 1) ^ ((lane >> 2) & 1)
    row_on = jnp.where(first, row_flag[0], row_flag[1])
    col_on = jnp.where(first, col_flags[0], col_flags[1])
    differs = (row_differs & row_on) | (col_differs & col_on)
    return jnp.where(differs == 1, -100.0, 0.0).astype(F32)


def attend(x, mask, bias_ref, gain, wqv_ref, wk_ref, proj_ref):
    normed = layer_norm(x, gain).astype(BF16)
    qv = dot(wqv_ref[...], normed, 1, 1)
    keys = dot(normed, wk_ref[...])
    lane = lax.broadcasted_iota(jnp.int32, (PAIR, PAIR), 1)
    key_low = (lane & 64) != 0
    first_lane = lax.broadcasted_iota(jnp.int32, (TOKENS, PAIR), 1) < TOKENS
    half = HEADS * HEAD_PAD
    mixed = []
    for head in range(HEADS):
        q = qv[head * HEAD_PAD : (head + 1) * HEAD_PAD] * (HEAD_DIM ** (-0.5))
        q_high = q.astype(BF16)
        q_low = (q - q_high.astype(F32)).astype(BF16)
        q_four = jnp.concatenate([q_high, q_low, q_high, q_low], axis=0)
        k = keys[:, head * PAIR : (head + 1) * PAIR]
        k_four = (k - jnp.where(key_low, k.astype(BF16).astype(F32), 0.0)).astype(BF16)
        scores = dot(k_four, q_four)
        scores = jnp.where(first_lane, scores[:TOKENS], scores[TOKENS:])
        scores = scores + bias_ref[head] + mask
        peak = jnp.max(scores, axis=0, keepdims=True)
        weights = jnp.exp(scores - peak)
        weights = weights * (1.0 / jnp.sum(weights, axis=0, keepdims=True))
        split = jnp.concatenate(
            [jnp.where(first_lane, weights, 0.0), jnp.where(first_lane, 0.0, weights)], axis=0
        ).astype(BF16)
        v = qv[half + head * HEAD_PAD : half + (head + 1) * HEAD_PAD].astype(BF16)
        mixed.append(dot(v, split))
    mixed = jnp.concatenate(mixed, axis=0).astype(BF16)
    return x + dot(mixed, proj_ref[...], 0, 0)


def feed(states, gain, hidden_ref, output_ref):
    normed = layer_norm(states, gain).astype(BF16)
    inner = jax.nn.gelu(dot(normed, hidden_ref[...]), approximate=True).astype(BF16)
    return states + dot(inner, output_ref[...])


def own_kernel(
    flags_ref,
    active_ref,
    x_ref,
    bias_ref,
    gain_attn_ref,
    wqv_ref,
    wk_ref,
    proj_ref,
    gain_mlp_ref,
    hidden_ref,
    output_ref,
    out_ref,
):
    step = pl.program_id(0)
    pairs = x_ref.shape[1] // (TILE * WIN)
    last = pl.num_programs(0) * pairs - 1
    for pair in range(pairs):
        columns = pl.ds(pair * TILE * WIN, TILE * WIN)
        block = x_ref[:, columns, :].astype(F32)
        x = jnp.concatenate(
            [
                block[:, w * WIN : (w + 1) * WIN].reshape(TOKENS, CHAN)
                for w in range(TILE)
            ],
            axis=0,
        )
        at_end = jnp.where(step * pairs + pair == last, 1, 0)
        row_flag = flags_ref[0]
        mask = region_mask((row_flag, row_flag), (0, at_end))
        attended = attend(x, mask, bias_ref, gain_attn_ref[...], wqv_ref, wk_ref, proj_ref)
        attended = attended.astype(BF16).astype(F32)
        done = feed(attended, gain_mlp_ref[...], hidden_ref, output_ref)
        parts = []
        for w in range(TILE):
            on = active_ref[(step * pairs + pair) * TILE + w]
            rows = slice(w * TOKENS, (w + 1) * TOKENS)
            parts.append(jnp.where(on == 1, done[rows], x[rows]).reshape(WIN, WIN, CHAN))
        out_ref[:, columns, :] = jnp.concatenate(parts, axis=1).astype(BF16)


def own_path(shifted, flags, active, bias, gain_attn, wqv, wk, proj, gain_mlp, hidden, output):
    rows, columns, _ = shifted.shape
    per_step = 2 * TILE * WIN
    whole = pl.BlockSpec(memory_space=pltpu.VMEM)
    scalars = pl.BlockSpec(memory_space=pltpu.SMEM)
    block = pl.BlockSpec((rows, per_step, CHAN), lambda i: (0, i, 0))
    return pl.pallas_call(
        own_kernel,
        grid=(columns // per_step,),
        in_specs=[scalars, scalars, block] + [whole] * 8,
        out_specs=block,
        out_shape=jax.ShapeDtypeStruct(shifted.shape, BF16),
        cost_estimate=pl.CostEstimate(
            flops=6_000_000_000, bytes_accessed=3_000_000, transcendentals=2_000_000
        ),
        name="own_path",
    )(flags, active, shifted, bias, gain_attn, wqv, wk, proj, gain_mlp, hidden, output)


def spread_kernel(pixels_ref, codes_ref, out_ref, heads, tails):
    rows, columns, _ = pixels_ref.shape
    tails[...] = jnp.zeros(tails.shape, F32)
    for row in range(rows):
        values = pixels_ref[row].astype(F32)
        heads[row, 0:columns, :] = values[:, 0:128]
        tails[row, 0:columns, 0:TAIL] = values[:, 128:CHAN]
        heads[row, columns : columns + WIN, :] = values[0:WIN, 0:128]
        tails[row, columns : columns + WIN, 0:TAIL] = values[0:WIN, 128:CHAN]
    codes = codes_ref[...]
    windows = columns // WIN
    half = windows // 2
    for token in range(TOKENS):
        row = (token // WIN + SHIFT) % rows
        picked = pl.ds(token % WIN + SHIFT, windows, stride=WIN)
        head = heads[row, picked, :]
        tail = tails[row, picked, :]
        packed = tail[:half] + pltpu.roll(tail[half:], TAIL, 1) + codes
        out_ref[token, :, 0:128] = head[:half].astype(BF16)
        out_ref[token, :, 128:256] = head[half:].astype(BF16)
        out_ref[token, :, 256:384] = packed.astype(BF16)


def spread(pixels, codes):
    rows, columns, _ = pixels.shape
    half = columns // WIN // 2
    return pl.pallas_call(
        spread_kernel,
        in_specs=[pl.BlockSpec(memory_space=pltpu.VMEM)] * 2,
        out_specs=pl.BlockSpec(memory_space=pltpu.VMEM),
        out_shape=jax.ShapeDtypeStruct((TOKENS, half, 384), BF16),
        scratch_shapes=[pltpu.VMEM((rows, columns + WIN, 128), F32)] * 2,
        cost_estimate=pl.CostEstimate(
            flops=100_000_000, bytes_accessed=2_000_000, transcendentals=0
        ),
        name="spread",
    )(pixels, codes)


def route_kernel(flags_ref, got_ref, out_ref):
    bands, half, _ = got_ref.shape
    slots = out_ref.shape[0] * out_ref.shape[1]
    sources = bands * half
    got = got_ref[...].reshape(sources, 384)
    tails = got[:, 256:384]
    row = lax.broadcasted_iota(jnp.int32, (8, 128), 0)
    lane = lax.broadcasted_iota(jnp.int32, (8, 128), 1) - 2 * TAIL - 2 * row
    pick = jnp.where(row < 2, jnp.where(lane == 0, 16.0, jnp.where(lane == 1, 1.0, 0.0)), 0.0)
    codes = dot(pick.astype(BF16), tails, 1, 1)
    codes = jnp.where(flags_ref[1] == 1, pltpu.roll(codes, half, 1), codes)
    low, high = codes[0:1].astype(jnp.int32), codes[1:2].astype(jnp.int32)
    chunk = 128
    lane_out = lax.broadcasted_iota(jnp.int32, (chunk, 128), 1)
    for start in range(0, slots, chunk):
        target = (lax.broadcasted_iota(jnp.int32, (chunk, sources), 0) + start) * TILE
        heads, tail_parts = [], []
        for place in range(TILE):
            pick_low = jnp.where(target + place == low, 1.0, 0.0).astype(BF16)
            pick_high = jnp.where(target + place == high, 1.0, 0.0).astype(BF16)
            first = jnp.concatenate([got[:, 0:128], tails], axis=1)
            second = jnp.concatenate([got[:, 128:256], tails], axis=1)
            from_low = dot(pick_low, first)
            from_high = dot(pick_high, second)
            heads.append(from_low[:, 0:128] + from_high[:, 0:128])
            low_tail, high_tail = from_low[:, 128:256], from_high[:, 128:256]
            high_moved = pltpu.roll(high_tail, 128 - TAIL, 1)
            tail = jnp.where(lane_out < TAIL, low_tail + high_moved, 0.0)
            kind_low = jnp.where(lane_out == 2 * TAIL + 4, low_tail, 0.0)
            kind_high = jnp.where(
                lane_out == 2 * TAIL + 4, pltpu.roll(high_tail, 127, 1), 0.0
            )
            kind = kind_low + kind_high
            if place:
                tail = pltpu.roll(tail, TAIL, 1)
                kind = pltpu.roll(kind, 1, 1)
            tail_parts.append(tail + kind)
        out = out_ref.at[start // CAP : (start + chunk) // CAP]
        blocks = chunk // CAP
        out[:, :, 0:128] = heads[0].reshape(blocks, CAP, 128).astype(BF16)
        out[:, :, 128:256] = heads[1].reshape(blocks, CAP, 128).astype(BF16)
        both = tail_parts[0] + tail_parts[1]
        out[:, :, 256:384] = both.reshape(blocks, CAP, 128).astype(BF16)


def route(got, flags):
    bands = got.shape[0]
    return pl.pallas_call(
        route_kernel,
        in_specs=[
            pl.BlockSpec(memory_space=pltpu.SMEM),
            pl.BlockSpec(memory_space=pltpu.VMEM),
        ],
        out_specs=pl.BlockSpec(memory_space=pltpu.VMEM),
        out_shape=jax.ShapeDtypeStruct((bands, CAP, 384), BF16),
        cost_estimate=pl.CostEstimate(
            flops=1_200_000_000, bytes_accessed=1_200_000, transcendentals=0
        ),
        name="route",
    )(flags, got)


def work_kernel(got_ref, kinds_ref, bias_ref, gain_ref, wqv_ref, wk_ref, proj_ref, out_ref, held):
    step = pl.program_id(0)

    @pl.when(step == 0)
    def _():
        for part in range(held.shape[0]):
            values = got_ref[:, :, part * 128 : (part + 1) * 128].astype(F32)
            held[part] = values.reshape(TOKENS * CAP, 128)

    slots = out_ref.shape[0]
    for index in range(slots):
        slot = step * slots + index
        rows = pl.ds(slot, TOKENS, stride=CAP)
        tail = held[TILE, rows, :]
        parts = []
        for place in range(TILE):
            head = held[place, rows, :]
            moved = pltpu.roll(tail, 128 - TAIL, 1) if place else tail
            parts.append(jnp.concatenate([head, moved], axis=1)[:, :CHAN])
        x = jnp.concatenate(parts, axis=0)
        kinds = [kinds_ref[slot * TILE + place] for place in range(TILE)]
        mask = region_mask([k & 1 for k in kinds], [k >> 1 for k in kinds])
        attended = attend(x, mask, bias_ref, gain_ref[...], wqv_ref, wk_ref, proj_ref)
        out_ref[index] = attended.astype(BF16)


def work_path(got, kinds, bias, gain, wqv, wk, proj):
    whole = pl.BlockSpec(memory_space=pltpu.VMEM)
    per_step = 2
    return pl.pallas_call(
        work_kernel,
        grid=(CAP // per_step,),
        in_specs=[whole, pl.BlockSpec(memory_space=pltpu.SMEM)] + [whole] * 5,
        out_specs=pl.BlockSpec((per_step, PAIR, CHAN), lambda i: (i, 0, 0)),
        out_shape=jax.ShapeDtypeStruct((CAP, PAIR, CHAN), BF16),
        scratch_shapes=[pltpu.VMEM((TILE + 1, TOKENS * CAP, 128), F32)],
        cost_estimate=pl.CostEstimate(
            flops=2_000_000_000, bytes_accessed=2_000_000, transcendentals=1_000_000
        ),
        name="work_path",
    )(got, kinds, bias, gain, wqv, wk, proj)


def from_behind(value, axis, steps):
    count = lax.axis_size(axis)
    pairs = [(source, (source + steps) % count) for source in range(count)]
    return lax.ppermute(value, axis, pairs)


def position_bias(bias_table):
    coords = jnp.arange(WIN, dtype=jnp.int32)
    offset = coords[None, :] - coords[:, None] + WIN - 1
    reach = 2 * WIN - 1
    onehot = (offset[:, :, None] == jnp.arange(reach)).astype(F32)
    table = bias_table.reshape(reach, reach, HEADS)
    looked = jnp.einsum(
        "kqa,abh->hkqb", onehot, table, precision=lax.Precision.HIGHEST
    )
    looked = jnp.einsum(
        "hkqb,cdb->hkcqd", looked, onehot, precision=lax.Precision.HIGHEST
    )
    looked = looked.reshape(HEADS, TOKENS, TOKENS)
    return jnp.concatenate([looked, looked], axis=2)


def pad_heads(weight):
    weight = weight.reshape(CHAN, HEADS, HEAD_DIM)
    return jnp.pad(weight, ((0, 0), (0, 0), (0, HEAD_PAD - HEAD_DIM)))


def shards(
    pixels,
    keep_mask,
    band_counts,
    plan_dest,
    plan_slot,
    bias_table,
    gain_attn,
    qkv_weight,
    proj_weight,
    gain_mlp,
    hidden_weight,
    output_weight,
):
    band_total = lax.axis_size("band")
    band_index = lax.axis_index("band")
    row_count, col_count, channels = pixels.shape
    window_total = (row_count // WIN) * (col_count // WIN)
    half = window_total // 2

    lower_rows = from_behind(pixels[:SHIFT], "band", -1)

    keep = keep_mask.reshape(window_total)
    position = jnp.cumsum(keep) - 1
    active = (keep == 1) & (position < band_counts[0])
    tile = position // TILE
    tile_onehot = tile[:, None] == jnp.arange(window_total // TILE)[None, :]
    dest = jnp.sum(jnp.where(tile_onehot, plan_dest, 0), axis=1)
    slot = jnp.sum(jnp.where(tile_onehot, plan_slot, 0), axis=1)
    placed = active & (slot < CAP)
    dest = jnp.where(placed, dest, band_total)
    place = jnp.where(placed, slot * TILE + position % TILE, 0)
    last_band = (band_index == band_total - 1).astype(jnp.int32)
    last_column = (jnp.arange(window_total) % (col_count // WIN) == col_count // WIN - 1)
    kind = last_band + 2 * last_column.astype(jnp.int32)
    codes = jnp.stack(
        [dest[:half], place[:half], dest[half:], place[half:], kind[:half], kind[half:]], axis=1
    )
    codes = jnp.pad(codes.astype(F32), ((0, 0), (2 * TAIL, 128 - 2 * TAIL - 6)))

    flags = jnp.stack([last_band, (band_index >= TOKENS // 2).astype(jnp.int32)])
    outgoing = spread(pixels, codes)
    gathered = lax.all_to_all(outgoing, "band", split_axis=0, concat_axis=0, tiled=True)

    bias = position_bias(bias_table)
    wq = pad_heads(qkv_weight[:, :CHAN]).reshape(CHAN, -1)
    wv = pad_heads(qkv_weight[:, 2 * CHAN :]).reshape(CHAN, -1)
    wqv = jnp.concatenate([wq, wv], axis=1).T
    wk = pad_heads(qkv_weight[:, CHAN : 2 * CHAN])
    wk = jnp.broadcast_to(wk[:, :, None, :], (CHAN, HEADS, 4, HEAD_PAD)).reshape(CHAN, -1)
    proj = jnp.pad(
        proj_weight.reshape(HEADS, HEAD_DIM, CHAN), ((0, 0), (0, HEAD_PAD - HEAD_DIM), (0, 0))
    ).reshape(HEADS * HEAD_PAD, CHAN)
    gain_one = gain_attn[None]

    shifted = jnp.roll(
        jnp.concatenate([pixels[SHIFT:], lower_rows], axis=0), -SHIFT, axis=1
    )
    band_shifted = own_path(
        shifted,
        flags,
        active.astype(jnp.int32),
        bias,
        gain_one,
        wqv,
        wk,
        proj,
        gain_mlp[None],
        hidden_weight,
        output_weight,
    )

    routed = route(gathered, flags)
    incoming = lax.all_to_all(routed, "band", split_axis=0, concat_axis=0, tiled=True)
    kinds = incoming[0, :, 256 + 2 * TAIL + 4 : 256 + 2 * TAIL + 6]
    kinds = kinds.astype(jnp.int32).reshape(CAP * TILE)
    work_tiles = work_path(incoming, kinds, bias, gain_one, wqv, wk, proj)

    band_shifted = jnp.roll(band_shifted, SHIFT, axis=1)
    upper_rows = from_behind(band_shifted[row_count - SHIFT :], "band", 1)
    restored = jnp.concatenate([upper_rows, band_shifted[: row_count - SHIFT]], axis=0)
    return (restored, work_tiles)


def solution(mesh):
    in_specs = (
        P(("img", "band"), None, None),
        P(("img", "band"), None),
        P(("img", "band")),
        P(("img", "band"), None),
        P(("img", "band"), None),
        P(),
        P(),
        P(),
        P(),
        P(),
        P(),
        P(),
    )
    out_specs = (P(("img", "band"), None, None), P(("img", "band"), None, None))
    return jax.shard_map(shards, mesh=mesh, in_specs=in_specs, out_specs=out_specs, check_vma=False)
```

time: 174 us -> 129 us (0.74)
  waiting for transfers between devices: 66 us -> 25.9 us
  Pallas kernels: 0 us -> 38 us
  matrix products: 23.9 us -> 2.11 us
  local copies, waits for them, and re-layouts: 34.5 us -> 14.6 us
  other arithmetic: 15.1 us -> 7.76 us
  starting transfers between devices: 31.5 us -> 38.8 us
    ppermute x2, waiting for transfers between devices: 66 us -> 25.9 us  [from_behind(): return lax.ppermute(value, axis, pairs)]
    pallas_call x0 -> x4, Pallas kernels: none -> 38 us  [the longest x1 22.9 us: own_path(): pl.pallas_call(own_kernel, grid=(columns // per_step,), in_specs=[scalars...]
    dot_general x6 -> x2, matrix products: 23.9 us -> 2.11 us  [the longest x1 1.84 us: position_bias(): jnp.einsum('hkqb,cdb->hkcqd', looked, onehot, precision=lax.Precision.HIG...]
    scatter x5 -> x0, local copies, waits for them, and re-layouts: 11.4 us -> none  [the longest x1 4.13 us: shards(): attended = jnp.zeros((CAP, tile_tokens, channels), jnp.bfloat16).at[arriv...]
    all_to_all x1, starting transfers between devices: 5.33 us -> 13.7 us  [shards(): lax.all_to_all(routed, 'band', split_axis=0, concat_axis=0, tiled=True)]
    convert_element_type x5 -> x1, local copies, waits for them, and re-layouts: 8.68 us -> 0.67 us  [shards(): kinds = kinds.astype(jnp.int32).reshape(CAP * TILE)]
    ppermute x2, starting transfers between devices: 13.9 us -> 9.57 us  [from_behind(): return lax.ppermute(value, axis, pairs)]
    sub x1 -> x2, other arithmetic: 3.74 us -> 0.12 us  [the longest x1 0.11 us: shards(): position = jnp.cumsum(keep) - 1]
  transfers between devices with their start and end apart: 4 -> 4, of which waited for: 1 -> 2; matrix products, arithmetic and copies ran while one was open for 37% -> 13% of each run, Pallas kernels for 0% -> 18%
where the time goes in v1:
time: 129 us
  starting transfers between devices  38.8 us (30%)
  Pallas kernels  38 us (29%)
  waiting for transfers between devices  25.9 us (20%)
  local copies, waits for them, and re-layouts  14.6 us (11%)
  other arithmetic  7.76 us (6%)
  matrix products  2.11 us (2%)
  between operations  1.56 us (1%)
    ppermute x2, waiting for transfers between devices, from_behind(): return lax.ppermute(value, axis, pairs)  25.9 us
    pallas_call x1, Pallas kernels, own_path(): pl.pallas_call(own_kernel, grid=(columns // per_step,), in_specs=[scalars...  22.9 us
    all_to_all x1, starting transfers between devices, shards(): lax.all_to_all(outgoing, 'band', split_axis=0, concat_axis=0, tiled=True)  15.5 us
    all_to_all x1, starting transfers between devices, shards(): lax.all_to_all(routed, 'band', split_axis=0, concat_axis=0, tiled=True)  13.7 us
    ppermute x2, starting transfers between devices, from_behind(): return lax.ppermute(value, axis, pairs)  9.57 us
    pallas_call x1, Pallas kernels, work_path(): pl.pallas_call(work_kernel, grid=(CAP // per_step,), in_specs=[whole, pl....  8.81 us
    unnamed x26, local copies, waits for them, and re-layouts  6.62 us
    pallas_call x1, Pallas kernels, route(): pl.pallas_call(route_kernel, in_specs=[pl.BlockSpec(memory_space=pltpu.SM...  3.53 us
  transfers between devices with their start and end apart: 4, of which 2 were waited for; matrix products, arithmetic and copies ran while one was open for 13% of the time, Pallas kernels for 18%

profile of v1, /device:TPU:1, one launch (start us, length us, event | category | flops | bytes accessed | tf_op | source)
XLA Modules:
  0.0 128.7 jit_solution(14587255227983076464)
XLA Ops:
  0.7 0.8 copy.49
  2.3 2.4 %copy.50.pixels_ref = bf16[8,256,180]{2,1,0:T(8,128)(2,1)} copy(bf16[8,256,180]{1,0,2:T(8,128)(2,1)} %param.12) | data formatting | bytes 1474560 | tf_op args[0]
  5.6 0.7 pad.22.codes_ref
  6.3 2.8 %spread.1 = bf16[64,16,384]{2,1,0:T(8,128)(2,1)} custom-call(bf16[8,256,180]{2,1,0:T(8,128)(2,1)} %copy.50.pixels_ref, f32[16,128]{1,0:T(8,128)} %pad.22.codes_ref), custom_call_target="tpu_custom_call" | custom-call | flops 100000000 | bytes 2000000 | tf_op jit(solution)/shard_map/spread/pallas_call | solution.py:178
  9.0 15.5 %all-to-all-start = ((bf16[64,16,384]{2,1,0:T(8,128)(2,1)}), bf16[64,16,384]{2,1,0:T(8,128)(2,1)}, u32[]{:S(2)}, u32[]{:S(2)}) async-start(bf16[64,16,384]{2,1,0:T(8,128)(2,1)} %spread.1), calls=%async_computation | async-start | bytes 1572864 | tf_op jit(solution)/shard_map/all_to_all | solution.py:365
  24.5 1.0 fusion.13
  25.6 7.0 %collective-permute-start = (bf16[4,256,180]{2,1,0:T(8,128)(2,1)}, bf16[4,256,180]{2,1,0:T(8,128)(2,1)}, u32[]{:S(2)}, u32[]{:S(2)}) collective-permute-start(bf16[4,256,180]{2,1,0:T(8,128)(2,1)} %get-tuple-element.13), channel_id=1, source_target_pairs={{0,252},{4,0},{8,4},{12,8},{16,12},{20,16},{24,20},{28,24},{32,28}... | collective-permute-start | bytes 1105928 | tf_op jit(solution)/shard_map/ppermute | solution.py:299
  32.6 0.3 convolution_bitcast_fusion.1
  32.9 1.8 %convolution_bitcast_fusion = f32[6,8,8,8,8]{3,4,1,0,2:T(8,128)S(1)} fusion(f32[6,8,8,15,1]{3,2,1,0,4:T(8,128)S(1)} %convolution_bitcast_fusion.1, s32[8,8]{1,0:T(8,128)S(1)} %subtract_add_fusion), kind=kOutput, calls=%fused_computation | convolution fusion | flops 4424640 | bytes 121600 | tf_op jit(solution)/shard_map/hkqb,cdb->hkcqd/dot_general | solution.py:311
  34.9 0.6 convert_element_type.28.active_ref
  35.5 0.5 copy.52
  36.0 0.4 reshape.92
  37.0 0.9 copy.56.wk_ref
  37.9 0.7 pad.21
  38.5 0.8 copy.57.output_ref
  39.4 0.6 pad_add_fusion.flags_ref
  40.0 0.8 pad_maximum_fusion.2.bias_ref
  40.8 0.7 maximum_bitcast_fusion.wqv_ref
  41.5 10.3 %collective-permute-done = bf16[4,256,180]{2,1,0:T(8,128)(2,1)} collective-permute-done((bf16[4,256,180]{2,1,0:T(8,128)(2,1)}, bf16[4,256,180]{2,1,0:T(8,128)(2,1)}, u32[]{:S(2)}, u32[]{:S(2)}) %collective-permute-start) | collective-permute-done | bytes 368672 | tf_op jit(solution)/shard_map/ppermute | solution.py:299
  51.8 1.3 %slice_maximum_fusion = bf16[8,252,180]{2,1,0:T(8,128)(2,1)S(1)} fusion(bf16[4,256,180]{2,1,0:T(8,128)(2,1)} %collective-permute-done, bf16[4,256,180]{2,1,0:T(8,128)(2,1)S(1)} %copy-done.1), kind=kLoop, calls=%fused_computation.6 | loop fusion | flops 362880 | bytes 1463040 | tf_op jit(solution)/shard_map/concatenate | solution.py:379
  53.2 1.9 %fusion.1.x_ref = bf16[8,256,180]{2,1,0:T(8,128)(2,1)} fusion(bf16[4,256,180]{2,1,0:T(8,128)(2,1)} %collective-permute-done, bf16[4,256,180]{2,1,0:T(8,128)(2,1)S(1)} %copy-done.1, bf16[8,252,180]{2,1,0:T(8,128)(2,1)S(1)} %slice_maximum_fusion), kind=kLoop, calls=%fused_computation.5 | loop fusion | flops 2211840 | bytes 2200320 | tf_op jit(solution)/shard_map/jit(_roll_static)/concatenate | solution.py:378
  55.1 3.5 %route.1 = bf16[64,8,384]{2,1,0:T(8,128)(2,1)} custom-call(s32[2]{0:T(128)} %pad_add_fusion.flags_ref, bf16[64,16,384]{2,1,0:T(8,128)(2,1)} %all-to-all-done.got_ref), custom_call_target="tpu_custom_call" | custom-call | flops 1200000000 | bytes 1200000 | tf_op jit(solution)/shard_map/route/pallas_call | solution.py:238
  58.6 13.7 %all-to-all-start.1 = ((bf16[64,8,384]{2,1,0:T(8,128)(2,1)}), bf16[64,8,384]{2,1,0:T(8,128)(2,1)S(1)}, u32[]{:S(2)}, u32[]{:S(2)}) async-start(bf16[64,8,384]{2,1,0:T(8,128)(2,1)} %route.1), calls=%async_computation.1 | async-start | bytes 786432 | tf_op jit(solution)/shard_map/all_to_all | solution.py:396
  72.3 22.9 %own_path.1 = bf16[8,256,180]{2,1,0:T(8,128)(2,1)} custom-call(s32[2]{0:T(128)} %pad_add_fusion.flags_ref, s32[32]{0:T(128)} %convert_element_type.28.active_ref, bf16[8,256,180]{2,1,0:T(8,128)(2,1)} %fusion.1.x_ref, f32[6,64,128]{2,1,0:T(8,128)} %pad_maximum_fusion.2.bias_ref, f32[1,180]{1,0:T(1,128)} %bitcast.70, ...), custom_call_target="tpu_custom_call" | custom-call | flops 6000000000 | bytes 3000000 | tf_op jit(solution)/shard_map/own_path/pallas_call | solution.py:139
  95.2 0.9 slice.80
  96.1 1.2 fusion.2
  97.3 2.6 %collective-permute-start.1 = (bf16[4,256,180]{2,1,0:T(8,128)(2,1)S(1)}, bf16[4,256,180]{2,1,0:T(8,128)(2,1)S(1)}, u32[]{:S(2)}, u32[]{:S(2)}) collective-permute-start(bf16[4,256,180]{2,1,0:T(8,128)(2,1)S(1)} %fusion.2), channel_id=1, source_target_pairs={{0,4},{4,8},{8,12},{12,16},{16,20},{20,24},{24,28},{28,32},{32,36}... | collective-permute-start | bytes 1105928 | tf_op jit(solution)/shard_map/ppermute | solution.py:299
  99.9 15.6 %collective-permute-done.1 = bf16[4,256,180]{2,1,0:T(8,128)(2,1)S(1)} collective-permute-done((bf16[4,256,180]{2,1,0:T(8,128)(2,1)S(1)}, bf16[4,256,180]{2,1,0:T(8,128)(2,1)S(1)}, u32[]{:S(2)}, u32[]{:S(2)}) %collective-permute-start.1) | collective-permute-done | bytes 368672 | tf_op jit(solution)/shard_map/ppermute | solution.py:299
  115.7 1.4 %copy.66 = bf16[8,256,180]{1,0,2:T(8,128)(2,1)} copy(bf16[8,256,180]{2,1,0:T(8,128)(2,1)S(1)} %fusion) | data formatting | bytes 1474560
  117.1 0.7 reshape.102.kinds_ref
  117.8 8.8 %work_path.1 = bf16[8,128,180]{2,1,0:T(8,128)(2,1)} custom-call(bf16[64,8,384]{2,1,0:T(8,128)(2,1)} %copy-done.3, s32[16]{0:T(128)} %reshape.102.kinds_ref, f32[6,64,128]{2,1,0:T(8,128)} %pad_maximum_fusion.2.bias_ref, f32[1,180]{1,0:T(1,128)} %bitcast.71, bf16[384,180]{1,0:T(8,128)(2,1)} %maximum_bitcast_fusion.wqv_ref, bf16[180,768]{1,0:T(8,128)(2,1)} %copy.56.wk_ref, ...), custom_call_target="tpu_custom_call" | custom-call | flops 2000000000 | bytes 2000000 | tf_op jit(solution)/shard_map/work_path/pallas_call | solution.py:282
  126.6 2.0 %copy.67 = bf16[8,128,180]{1,0,2:T(8,128)(2,1)} copy(bf16[8,128,180]{2,1,0:T(8,128)(2,1)} %work_path.1) | data formatting | bytes 737280
  (58 shorter events, 2.2 us)
Async XLA Ops:
  0.6 4.1 %copy-start.8 = (s32[1,32]{1,0:T(1,128)S(1)}, s32[1,32]{1,0:T(1,128)}, u32[]{:S(2)}) copy-start(s32[1,32]{1,0:T(1,128)} %param.13) | copy-start | bytes 388
  0.6 4.0 %copy-start.9 = (s32[1,16]{1,0:T(1,128)S(1)}, s32[1,16]{1,0:T(1,128)}, u32[]{:S(2)}) copy-start(s32[1,16]{1,0:T(1,128)} %param.16) | copy-start | bytes 196
  0.7 4.0 %copy-start.10 = (s32[1,16]{1,0:T(1,128)S(1)}, s32[1,16]{1,0:T(1,128)}, u32[]{:S(2)}) copy-start(s32[1,16]{1,0:T(1,128)} %param.15) | copy-start | bytes 196
  6.3 18.2 %copy-start = (bf16[8,256,180]{2,1,0:T(8,128)(2,1)S(1)}, bf16[8,256,180]{2,1,0:T(8,128)(2,1)}, u32[]{:S(2)}) copy-start(bf16[8,256,180]{2,1,0:T(8,128)(2,1)} %copy.50.pixels_ref) | copy-start | bytes 2211844
  9.0 23.5 %copy-start.7 = (f32[225,6]{0,1:T(8,128)S(1)}, f32[225,6]{0,1:T(8,128)}, u32[]{:S(2)}) copy-start(f32[225,6]{0,1:T(8,128)} %param.17) | copy-start | bytes 16204
  9.0 46.0 %all-to-all-start = ((bf16[64,16,384]{2,1,0:T(8,128)(2,1)}), bf16[64,16,384]{2,1,0:T(8,128)(2,1)}, u32[]{:S(2)}, u32[]{:S(2)}) async-start(bf16[64,16,384]{2,1,0:T(8,128)(2,1)} %spread.1), calls=%async_computation | async-start | bytes 1572864 | tf_op jit(solution)/shard_map/all_to_all | solution.py:365
  24.5 10.3 %copy-start.4 = (bf16[180,540]{1,0:T(8,128)(2,1)S(1)}, bf16[180,540]{1,0:T(8,128)(2,1)}, u32[]{:S(2)}) copy-start(bf16[180,540]{1,0:T(8,128)(2,1)} %param.19) | copy-start | bytes 583204
  25.6 26.3 %collective-permute-start = (bf16[4,256,180]{2,1,0:T(8,128)(2,1)}, bf16[4,256,180]{2,1,0:T(8,128)(2,1)}, u32[]{:S(2)}, u32[]{:S(2)}) collective-permute-start(bf16[4,256,180]{2,1,0:T(8,128)(2,1)} %get-tuple-element.13), channel_id=1, source_target_pairs={{0,252},{4,0},{8,4},{12,8},{16,12},{20,16},{24,20},{28,24},{32,28}... | collective-permute-start | bytes 1105928 | tf_op jit(solution)/shard_map/ppermute | solution.py:299
  36.4 1.5 %copy-start.6 = (bf16[180,180]{1,0:T(8,128)(2,1)S(1)}, bf16[180,180]{1,0:T(8,128)(2,1)}, u32[]{:S(2)}) copy-start(bf16[180,180]{1,0:T(8,128)(2,1)} %param.20) | copy-start | bytes 194404
  36.5 2.0 %copy-start.5 = (bf16[360,180]{0,1:T(8,128)(2,1)S(1)}, bf16[360,180]{0,1:T(8,128)(2,1)}, u32[]{:S(2)}) copy-start(bf16[360,180]{0,1:T(8,128)(2,1)} %param.23) | copy-start | bytes 388804
  36.9 15.0 %copy-start.1 = (bf16[4,256,180]{2,1,0:T(8,128)(2,1)S(1)}, bf16[4,256,180]{2,1,0:T(8,128)(2,1)}, u32[]{:S(2)}) copy-start(bf16[4,256,180]{2,1,0:T(8,128)(2,1)} %get-tuple-element.12) | copy-start | bytes 1105924
  58.6 58.5 %all-to-all-start.1 = ((bf16[64,8,384]{2,1,0:T(8,128)(2,1)}), bf16[64,8,384]{2,1,0:T(8,128)(2,1)S(1)}, u32[]{:S(2)}, u32[]{:S(2)}) async-start(bf16[64,8,384]{2,1,0:T(8,128)(2,1)} %route.1), calls=%async_computation.1 | async-start | bytes 786432 | tf_op jit(solution)/shard_map/all_to_all | solution.py:396
  95.2 20.2 %copy-start.2 = (bf16[8,256,180]{2,1,0:T(8,128)(2,1)S(1)}, bf16[8,256,180]{2,1,0:T(8,128)(2,1)}, u32[]{:S(2)}) copy-start(bf16[8,256,180]{2,1,0:T(8,128)(2,1)} %own_path.1) | copy-start | bytes 2211844
  97.3 18.2 %collective-permute-start.1 = (bf16[4,256,180]{2,1,0:T(8,128)(2,1)S(1)}, bf16[4,256,180]{2,1,0:T(8,128)(2,1)S(1)}, u32[]{:S(2)}, u32[]{:S(2)}) collective-permute-start(bf16[4,256,180]{2,1,0:T(8,128)(2,1)S(1)} %fusion.2), channel_id=1, source_target_pairs={{0,4},{4,8},{8,12},{12,16},{16,20},{20,24},{24,28},{28,32},{32,36}... | collective-permute-start | bytes 1105928 | tf_op jit(solution)/shard_map/ppermute | solution.py:299
  117.1 0.8 copy-start.3

commit v2 on v1

v2 whole, which is shorter than its diff:
```python
import jax
import jax.numpy as jnp
from jax import lax
from jax.experimental import pallas as pl
from jax.experimental.pallas import tpu as pltpu
from jax.sharding import PartitionSpec as P


CHAN = 180
HEADS = 6
HEAD_DIM = CHAN // HEADS
HEAD_PAD = 32
WIN = 8
TOKENS = WIN * WIN
TILE = 2
PAIR = TILE * TOKENS
SHIFT = 4
CAP = 8
TAIL = CHAN - 128
EPSILON = 1e-05

F32 = jnp.float32
BF16 = jnp.bfloat16


def dot(left, right, left_dim=1, right_dim=0):
    return lax.dot_general(
        left,
        right,
        (((left_dim,), (right_dim,)), ((), ())),
        preferred_element_type=F32,
    )


def layer_norm(values, gain):
    center = values - jnp.sum(values, axis=-1, keepdims=True) * (1.0 / CHAN)
    spread = jnp.sum(center * center, axis=-1, keepdims=True) * (1.0 / CHAN)
    return center * lax.rsqrt(spread + EPSILON) * gain


def iota(shape, dim):
    return lax.broadcasted_iota(jnp.int32, shape, dim)


def region_mask(row_flags, col_flags):
    shape = (TOKENS, PAIR)
    key, lane = iota(shape, 0), iota(shape, 1)
    first = lane < TOKENS
    row_differs = (((key >> 5) & 1) != ((lane >> 5) & 1)).astype(F32)
    col_differs = (((key >> 2) & 1) != ((lane >> 2) & 1)).astype(F32)
    row_on = jnp.where(first, row_flags[0], row_flags[1])
    col_on = jnp.where(first, col_flags[0], col_flags[1])
    return -100.0 * jnp.maximum(row_differs * row_on, col_differs * col_on)


def attend(x, masks, bias_ref, gain, wqv_ref, wk_ref):
    pairs = len(masks)
    normed = layer_norm(x, gain).astype(BF16)
    qv = dot(wqv_ref[...], normed, 1, 1)
    keys = dot(normed, wk_ref[...])
    key_low = (iota(keys.shape, 1) & 64) != 0
    keys = (keys - jnp.where(key_low, keys.astype(BF16).astype(F32), 0.0)).astype(BF16)
    half = HEADS * HEAD_PAD
    queries = qv[:half] * (HEAD_DIM ** (-0.5))
    high = queries.astype(BF16)
    low = (queries - high.astype(F32)).astype(BF16)
    values = qv[half:].astype(BF16)
    first_lane = iota((TOKENS, PAIR), 1) < TOKENS
    blank = jnp.zeros((PAIR, PAIR), BF16)
    scores = []
    for pair in range(pairs):
        lanes = slice(pair * PAIR, (pair + 1) * PAIR)
        for head in range(0, HEADS, 2):
            fours = []
            for one in (head, head + 1):
                rows = slice(one * HEAD_PAD, (one + 1) * HEAD_PAD)
                h, l = high[rows, lanes], low[rows, lanes]
                fours.append(jnp.concatenate([h, l, h, l], axis=0))
            both = jnp.concatenate(
                [
                    jnp.concatenate([fours[0], blank], axis=1),
                    jnp.concatenate([blank, fours[1]], axis=1),
                ],
                axis=0,
            )
            got = dot(keys[lanes, head * PAIR : (head + 2) * PAIR], both)
            for one in range(2):
                part = got[:, one * PAIR : (one + 1) * PAIR]
                scores.append(jnp.where(first_lane, part[:TOKENS], part[TOKENS:]))
    weights = []
    for pair in range(pairs):
        for head in range(HEADS):
            value = scores[pair * HEADS + head] + bias_ref[head] + masks[pair]
            value = jnp.exp(value - jnp.max(value, axis=0, keepdims=True))
            value = value * (1.0 / jnp.sum(value, axis=0, keepdims=True))
            weights.append(
                jnp.concatenate(
                    [jnp.where(first_lane, value, 0.0), jnp.where(first_lane, 0.0, value)], axis=0
                ).astype(BF16)
            )
    mixed = []
    for pair in range(pairs):
        lanes = slice(pair * PAIR, (pair + 1) * PAIR)
        parts = []
        for head in range(0, HEADS, 2):
            at = pair * HEADS + head
            both = jnp.concatenate([weights[at], weights[at + 1]], axis=1)
            rows = slice(head * HEAD_PAD, (head + 2) * HEAD_PAD)
            got = dot(values[rows, lanes], both)
            parts += [got[:HEAD_PAD, :PAIR], got[HEAD_PAD:, PAIR:]]
        mixed.append(jnp.concatenate(parts, axis=0).astype(BF16))
    return mixed


def feed(states, gain, hidden_ref, output_ref):
    normed = layer_norm(states, gain).astype(BF16)
    inner = jax.nn.gelu(dot(normed, hidden_ref[...]), approximate=True).astype(BF16)
    return states + dot(inner, output_ref[...])


VMEM = pl.BlockSpec(memory_space=pltpu.VMEM)
SMEM = pl.BlockSpec(memory_space=pltpu.SMEM)


def prep_kernel(
    qkv_ref, proj_ref, table_ref, wqv_ref, wk_ref, padded_ref, turned_ref, bias_ref, padded, looked
):
    half = HEADS * HEAD_PAD

    def source(column):
        inner = column & (HEAD_PAD - 1)
        return jnp.where(inner < HEAD_DIM, (column >> 5) * HEAD_DIM + inner, -1000)

    qkv = qkv_ref[...]
    column = iota((2 * half, 3 * CHAN), 0)
    wanted = jnp.where(column < half, source(column), 2 * CHAN + source(column - half))
    pick = (wanted == iota((2 * half, 3 * CHAN), 1)).astype(F32).astype(BF16)
    wqv_ref[...] = dot(pick, qkv, 1, 1).astype(BF16)
    shape = (3 * CHAN, HEADS * PAIR)
    column = iota(shape, 1)
    inner = column & (HEAD_PAD - 1)
    wanted = jnp.where(inner < HEAD_DIM, CHAN + (column >> 7) * HEAD_DIM + inner, -1)
    wk_ref[...] = dot(qkv, (wanted == iota(shape, 0)).astype(F32).astype(BF16)).astype(BF16)
    proj = proj_ref[...]
    pick = (source(iota((half, CHAN), 0)) == iota((half, CHAN), 1)).astype(F32).astype(BF16)
    padded_ref[...] = dot(pick, proj).astype(BF16)
    pick = (source(iota((CHAN, half), 1)) == iota((CHAN, half), 0)).astype(F32).astype(BF16)
    turned_ref[...] = dot(proj, pick, 0, 0).astype(BF16)

    reach = 2 * WIN - 1
    padded[...] = jnp.zeros(padded.shape, F32)
    padded[0:HEADS, 0 : reach * reach] = table_ref[...]
    table = padded[...]
    for key in range(TOKENS):
        shift = 112 - (key // WIN) * reach - key % WIN
        moved = pltpu.roll(table, (256 - shift) % 256, 1)[:, :PAIR]
        looked[key * 8 : (key + 1) * 8, :] = moved
    rest = looked[...]
    query = iota((PAIR, PAIR), 1) & (TOKENS - 1)
    pick = (iota((PAIR, PAIR), 0) == (query >> 3) * reach + (query & 7)).astype(F32).astype(BF16)
    total = None
    for _ in range(3):
        part = rest.astype(BF16)
        rest = rest - part.astype(F32)
        got = dot(part, pick)
        total = got if total is None else total + got
    looked[...] = total
    for head in range(HEADS):
        bias_ref[head] = looked[pl.ds(head, TOKENS, stride=8), :]


def prep(qkv_weight, proj_weight, table):
    half = HEADS * HEAD_PAD
    return pl.pallas_call(
        prep_kernel,
        in_specs=[VMEM] * 3,
        out_specs=[VMEM] * 5,
        out_shape=[
            jax.ShapeDtypeStruct((2 * half, CHAN), BF16),
            jax.ShapeDtypeStruct((CHAN, HEADS * PAIR), BF16),
            jax.ShapeDtypeStruct((half, CHAN), BF16),
            jax.ShapeDtypeStruct((CHAN, half), BF16),
            jax.ShapeDtypeStruct((HEADS, TOKENS, PAIR), F32),
        ],
        scratch_shapes=[pltpu.VMEM((8, 256), F32), pltpu.VMEM((8 * TOKENS, PAIR), F32)],
        cost_estimate=pl.CostEstimate(
            flops=600_000_000, bytes_accessed=1_500_000, transcendentals=0
        ),
        name="prep",
    )(qkv_weight, proj_weight, table)


def own_kernel(
    keep_ref,
    count_ref,
    rest_ref,
    halo_ref,
    bias_ref,
    gain_attn_ref,
    wqv_ref,
    wk_ref,
    proj_ref,
    gain_mlp_ref,
    hidden_ref,
    output_ref,
    out_ref,
    send_ref,
    active,
):
    step = pl.program_id(0)
    steps = pl.num_programs(0)
    pairs = rest_ref.shape[1] // (TILE * WIN)
    row_flag = jnp.where(lax.axis_index("band") == lax.axis_size("band") - 1, 1.0, 0.0)

    @pl.when(step == 0)
    def _():
        position = jnp.int32(-1)
        for w in range(keep_ref.shape[1]):
            keep = keep_ref[0, w]
            position = position + keep
            active[w] = jnp.where((keep == 1) & (position < count_ref[0]), 1, 0)

    tokens, masks = [], []
    for pair in range(pairs):
        columns = pl.ds(pair * TILE * WIN, TILE * WIN)
        upper = rest_ref[:, columns, :].astype(F32)
        lower = halo_ref[:, columns, :].astype(F32)
        for w in range(TILE):
            for part in (upper, lower):
                tokens.append(
                    part[:, w * WIN : (w + 1) * WIN].reshape(SHIFT * WIN, CHAN)
                )
        at_end = jnp.where((step == steps - 1) & (pair == pairs - 1), 1.0, 0.0)
        masks.append(region_mask((row_flag, row_flag), (0.0, at_end)))
    x = jnp.concatenate(tokens, axis=0)
    mixed = attend(x, masks, bias_ref, gain_attn_ref[...], wqv_ref, wk_ref)
    projected = [dot(part, proj_ref[...], 0, 0) for part in mixed]
    attended = x + jnp.concatenate(projected, axis=0)
    attended = attended.astype(BF16).astype(F32)
    done = feed(attended, gain_mlp_ref[...], hidden_ref, output_ref)
    for pair in range(pairs):
        columns = pl.ds(pair * TILE * WIN, TILE * WIN)
        uppers, lowers = [], []
        for w in range(TILE):
            at = pair * TILE + w
            on = active[step * pairs * TILE + at]
            rows = slice(at * TOKENS, (at + 1) * TOKENS)
            kept = jnp.where(on == 1, done[rows], x[rows]).reshape(WIN, WIN, CHAN)
            uppers.append(kept[:SHIFT])
            lowers.append(kept[SHIFT:])
        out_ref[:, columns, :] = jnp.concatenate(uppers, axis=1).astype(BF16)
        send_ref[:, columns, :] = jnp.concatenate(lowers, axis=1).astype(BF16)


def own_path(keep, count, rest, halo, bias, gain_attn, wqv, wk, proj, gain_mlp, hidden, output):
    rows, columns, _ = rest.shape
    per_step = 2 * TILE * WIN
    block = pl.BlockSpec((rows, per_step, CHAN), lambda i: (0, i, 0))
    return pl.pallas_call(
        own_kernel,
        grid=(columns // per_step,),
        in_specs=[SMEM, SMEM, block, block] + [VMEM] * 8,
        out_specs=[block, block],
        out_shape=[jax.ShapeDtypeStruct(rest.shape, BF16)] * 2,
        scratch_shapes=[pltpu.SMEM((columns // WIN,), jnp.int32)],
        cost_estimate=pl.CostEstimate(
            flops=20_000_000_000, bytes_accessed=3_000_000, transcendentals=2_000_000
        ),
        name="own_path",
    )(keep, count, rest, halo, bias, gain_attn, wqv, wk, proj, gain_mlp, hidden, output)


def spread_kernel(
    keep_ref, count_ref, dest_ref, slot_ref, pixels_ref, out_ref, top_ref, rest_ref, heads, tails
):
    rows, columns, _ = pixels_ref.shape
    windows = columns // WIN
    half = windows // 2
    bands = lax.axis_size("band")
    last_band = jnp.where(lax.axis_index("band") == bands - 1, 1.0, 0.0)
    row, lane = iota((half, 128), 0), iota((half, 128), 1) - 2 * TAIL
    codes = jnp.where((lane == 4) | (lane == 6), last_band, 0.0)
    codes = jnp.where((lane == 7) & (row == half - 1), 1.0, codes)
    position = jnp.int32(-1)
    for w in range(windows):
        keep = keep_ref[0, w]
        position = position + keep
        tile = jnp.maximum(position, 0) >> 1
        slot = slot_ref[0, tile]
        placed = (keep == 1) & (position < count_ref[0]) & (slot < CAP)
        dest = jnp.where(placed, dest_ref[0, tile], bands).astype(F32)
        place = jnp.where(placed, slot * TILE + (position & 1), 0).astype(F32)
        first = 2 * (w // half)
        here = row == w % half
        codes = jnp.where(here & (lane == first), dest, codes)
        codes = jnp.where(here & (lane == first + 1), place, codes)

    tails[...] = jnp.zeros(tails.shape, F32)
    for r in range(rows):
        values = pixels_ref[r].astype(F32)
        heads[r, 0:columns, :] = values[:, 0:128]
        tails[r, 0:columns, 0:TAIL] = values[:, 128:CHAN]
        heads[r, columns : columns + WIN, :] = values[0:WIN, 0:128]
        tails[r, columns : columns + WIN, 0:TAIL] = values[0:WIN, 128:CHAN]
    for r in range(rows):
        target = top_ref.at[r] if r < SHIFT else rest_ref.at[r - SHIFT]
        target[:, 0:128] = heads[r, SHIFT : SHIFT + columns, :].astype(BF16)
        target[:, 128:CHAN] = tails[r, SHIFT : SHIFT + columns, 0:TAIL].astype(BF16)
    for token in range(TOKENS):
        r = (token // WIN + SHIFT) % rows
        picked = pl.ds(token % WIN + SHIFT, windows, stride=WIN)
        head = heads[r, picked, :]
        tail = tails[r, picked, :]
        packed = tail[:half] + pltpu.roll(tail[half:], TAIL, 1) + codes
        out_ref[token, :, 0:128] = head[:half].astype(BF16)
        out_ref[token, :, 128:256] = head[half:].astype(BF16)
        out_ref[token, :, 256:384] = packed.astype(BF16)


def spread(keep, count, dest, slot, pixels):
    rows, columns, _ = pixels.shape
    half = columns // WIN // 2
    part = jax.ShapeDtypeStruct((SHIFT, columns, CHAN), BF16)
    return pl.pallas_call(
        spread_kernel,
        in_specs=[SMEM] * 4 + [VMEM],
        out_specs=[VMEM] * 3,
        out_shape=[jax.ShapeDtypeStruct((TOKENS, half, 384), BF16), part, part],
        scratch_shapes=[pltpu.VMEM((rows, columns + WIN, 128), F32)] * 2,
        cost_estimate=pl.CostEstimate(
            flops=100_000_000, bytes_accessed=2_000_000, transcendentals=0
        ),
        name="spread",
    )(keep, count, dest, slot, pixels)


def route_kernel(got_ref, out_ref):
    bands, half, _ = got_ref.shape
    slots = out_ref.shape[0] * out_ref.shape[1]
    sources = bands * half
    got = got_ref[...].reshape(sources, 384)
    tails = got[:, 256:384]
    row = iota((8, 128), 0)
    lane = iota((8, 128), 1) - 2 * TAIL - 2 * row
    pick = jnp.where(row < 2, jnp.where(lane == 0, 16.0, jnp.where(lane == 1, 1.0, 0.0)), 0.0)
    codes = dot(pick.astype(BF16), tails, 1, 1)
    behind = lax.axis_index("band") >= TOKENS // 2
    codes = jnp.where(behind, pltpu.roll(codes, half, 1), codes)
    low, high = codes[0:1].astype(jnp.int32), codes[1:2].astype(jnp.int32)
    chunk = 128
    lane_out = iota((chunk, 128), 1)
    is_kind = (lane_out == 2 * TAIL + 4) | (lane_out == 2 * TAIL + 5)
    first = jnp.concatenate([got[:, 0:128], tails], axis=1)
    second = jnp.concatenate([got[:, 128:256], tails], axis=1)
    for start in range(0, slots, chunk):
        target = (iota((chunk, sources), 0) + start) * TILE
        heads, total = [], None
        for place in range(TILE):
            pick_low = jnp.where(target + place == low, 1.0, 0.0).astype(BF16)
            pick_high = jnp.where(target + place == high, 1.0, 0.0).astype(BF16)
            from_low = dot(pick_low, first)
            from_high = dot(pick_high, second)
            heads.append(from_low[:, 0:128] + from_high[:, 0:128])
            low_tail, high_tail = from_low[:, 128:256], from_high[:, 128:256]
            tail = low_tail + pltpu.roll(high_tail, 128 - TAIL, 1)
            kind = low_tail + pltpu.roll(high_tail, 126, 1)
            tail = jnp.where(lane_out < TAIL, tail, 0.0)
            kind = jnp.where(is_kind, kind, 0.0)
            if place:
                tail = pltpu.roll(tail, TAIL, 1)
                kind = pltpu.roll(kind, 2, 1)
            total = tail + kind if total is None else total + tail + kind
        out = out_ref.at[start // CAP : (start + chunk) // CAP]
        blocks = chunk // CAP
        out[:, :, 0:128] = heads[0].reshape(blocks, CAP, 128).astype(BF16)
        out[:, :, 128:256] = heads[1].reshape(blocks, CAP, 128).astype(BF16)
        out[:, :, 256:384] = total.reshape(blocks, CAP, 128).astype(BF16)


def route(got):
    bands = got.shape[0]
    return pl.pallas_call(
        route_kernel,
        in_specs=[VMEM],
        out_specs=VMEM,
        out_shape=jax.ShapeDtypeStruct((bands, CAP, 384), BF16),
        cost_estimate=pl.CostEstimate(
            flops=1_200_000_000, bytes_accessed=1_200_000, transcendentals=0
        ),
        name="route",
    )(got)


def work_kernel(got_ref, bias_ref, gain_ref, wqv_ref, wk_ref, proj_ref, out_ref, held, done):
    for part in range(held.shape[0]):
        values = got_ref[:, :, part * 128 : (part + 1) * 128].astype(F32)
        held[part] = values.reshape(TOKENS * CAP, 128)
    pairs = 2

    def two_slots(step, carry):
        tokens, masks = [], []
        for index in range(pairs):
            slot = step * pairs + index
            rows = pl.ds(slot, TOKENS, stride=CAP)
            tail = held[TILE, rows, :]
            for place in range(TILE):
                head = held[place, rows, :]
                moved = pltpu.roll(tail, 128 - TAIL, 1) if place else tail
                tokens.append(jnp.concatenate([head, moved], axis=1)[:, :CHAN])
            lane = iota((1, 128), 1) - 2 * TAIL - 4
            flags = [
                jnp.sum(jnp.where(lane == i, tail[0:1], 0.0), axis=1, keepdims=True)
                for i in range(4)
            ]
            masks.append(region_mask(flags[0::2], flags[1::2]))
        x = jnp.concatenate(tokens, axis=0)
        mixed = attend(x, masks, bias_ref, gain_ref[...], wqv_ref, wk_ref)
        for index in range(pairs):
            rows = pl.ds(step * pairs + index, CHAN, stride=CAP)
            own = x[index * PAIR : (index + 1) * PAIR]
            done[rows, :] = own.T + dot(proj_ref[...], mixed[index])
        return carry

    lax.fori_loop(0, CAP // pairs, two_slots, 0)
    out_ref[...] = done[...].reshape(CHAN, CAP, PAIR).astype(BF16)


def work_path(got, bias, gain, wqv, wk, proj):
    return pl.pallas_call(
        work_kernel,
        in_specs=[VMEM] * 6,
        out_specs=VMEM,
        out_shape=jax.ShapeDtypeStruct((CHAN, CAP, PAIR), BF16),
        scratch_shapes=[
            pltpu.VMEM((TILE + 1, TOKENS * CAP, 128), F32),
            pltpu.VMEM((CHAN * CAP, PAIR), F32),
        ],
        cost_estimate=pl.CostEstimate(
            flops=8_000_000_000, bytes_accessed=2_000_000, transcendentals=1_000_000
        ),
        name="work_path",
    )(got, bias, gain, wqv, wk, proj)


def from_behind(value, axis, steps):
    count = lax.axis_size(axis)
    pairs = [(source, (source + steps) % count) for source in range(count)]
    return lax.ppermute(value, axis, pairs)


def shards(
    pixels,
    keep_mask,
    band_counts,
    plan_dest,
    plan_slot,
    bias_table,
    gain_attn,
    qkv_weight,
    proj_weight,
    gain_mlp,
    hidden_weight,
    output_weight,
):
    gain_attn, gain_mlp = gain_attn[None], gain_mlp[None]
    outgoing, top, rest = spread(keep_mask, band_counts, plan_dest, plan_slot, pixels)
    halo = from_behind(top, "band", -1)
    gathered = lax.all_to_all(outgoing, "band", split_axis=0, concat_axis=0, tiled=True)
    wqv, wk, proj, proj_turned, bias = prep(qkv_weight, proj_weight, bias_table.T)
    kept, sent = own_path(
        keep_mask,
        band_counts,
        rest,
        halo,
        bias,
        gain_attn,
        wqv,
        wk,
        proj,
        gain_mlp,
        hidden_weight,
        output_weight,
    )
    upper = from_behind(sent, "band", 1)
    routed = route(gathered)
    incoming = lax.all_to_all(routed, "band", split_axis=0, concat_axis=0, tiled=True)
    restored = jnp.roll(jnp.concatenate([upper, kept], axis=0), SHIFT, axis=1)
    work_tiles = work_path(incoming, bias, gain_attn, wqv, wk, proj_turned)
    work_tiles = jnp.transpose(work_tiles, (1, 2, 0))
    return (restored, work_tiles)


def solution(mesh):
    in_specs = (
        P(("img", "band"), None, None),
        P(("img", "band"), None),
        P(("img", "band")),
        P(("img", "band"), None),
        P(("img", "band"), None),
        P(),
        P(),
        P(),
        P(),
        P(),
        P(),
        P(),
    )
    out_specs = (P(("img", "band"), None, None), P(("img", "band"), None, None))
    return jax.shard_map(shards, mesh=mesh, in_specs=in_specs, out_specs=out_specs, check_vma=False)
```

time: 129 us -> 101 us (0.78)
  local copies, waits for them, and re-layouts: 14.6 us -> 7.08 us
  other arithmetic: 7.76 us -> 0.29 us
  starting transfers between devices: 38.8 us -> 32.5 us
  Pallas kernels: 38 us -> 31.9 us
  matrix products: 2.11 us -> 0 us
    all_to_all x1, waiting for transfers between devices: 0.01 us -> 12.4 us  [shards(): lax.all_to_all(outgoing, 'band', split_axis=0, concat_axis=0, tiled=True)]
    ppermute x2, waiting for transfers between devices: 25.9 us -> 14.7 us  [from_behind(): return lax.ppermute(value, axis, pairs)]
    all_to_all x1, starting transfers between devices: 13.7 us -> 7.53 us  [shards(): lax.all_to_all(routed, 'band', split_axis=0, concat_axis=0, tiled=True)]
    pallas_call x4 -> x5, Pallas kernels: 38 us -> 31.9 us  [the longest x1 15.6 us: own_path(): pl.pallas_call(own_kernel, grid=(columns // per_step,), in_specs=[SMEM, S...]
    concatenate x5 -> x1, other arithmetic: 5.47 us -> 0.29 us  [shards(): restored = jnp.roll(jnp.concatenate([upper, kept], axis=0), SHIFT, axis=1)]
    slice x6 -> x1, local copies, waits for them, and re-layouts: 2.32 us -> 0.01 us  [shards(): restored = jnp.roll(jnp.concatenate([upper, kept], axis=0), SHIFT, axis=1)]
    dot_general x2 -> x0, matrix products: 2.11 us -> none  [the longest x1 1.84 us: position_bias(): jnp.einsum('hkqb,cdb->hkcqd', looked, onehot, precision=lax.Precision.HIG...]
    another operation x11 -> x0, local copies, waits for them, and re-layouts: 1.57 us -> none  [the longest x10 0.79 us: shards(): jnp.stack([dest[:half], place[:half], dest[half:], place[half:], kind[:ha...]
  transfers between devices with their start and end apart: 4 -> 4, of which waited for: 2 -> 2; matrix products, arithmetic and copies ran while one was open for 13% -> 3% of each run, Pallas kernels for 18% -> 22%
where the time goes in v2:
time: 101 us; the launch traced here: 100 us
  starting transfers between devices  32.5 us (32%)
  Pallas kernels  31.9 us (32%)
  waiting for transfers between devices  27.1 us (27%)
  local copies, waits for them, and re-layouts  7.08 us (7%)
  between operations  1.36 us (1%)
    pallas_call x1, Pallas kernels, own_path(): pl.pallas_call(own_kernel, grid=(columns // per_step,), in_specs=[SMEM, S...  15.6 us
    all_to_all x1, starting transfers between devices, shards(): lax.all_to_all(outgoing, 'band', split_axis=0, concat_axis=0, tiled=True)  15.2 us
    ppermute x2, waiting for transfers between devices, from_behind(): return lax.ppermute(value, axis, pairs)  14.7 us
    all_to_all x1, waiting for transfers between devices, shards(): lax.all_to_all(outgoing, 'band', split_axis=0, concat_axis=0, tiled=True)  12.4 us
    ppermute x2, starting transfers between devices, from_behind(): return lax.ppermute(value, axis, pairs)  9.71 us
    all_to_all x1, starting transfers between devices, shards(): lax.all_to_all(routed, 'band', split_axis=0, concat_axis=0, tiled=True)  7.53 us
    unnamed x16, local copies, waits for them, and re-layouts  7.03 us
    pallas_call x1, Pallas kernels, work_path(): pl.pallas_call(work_kernel, in_specs=[VMEM] * 6, out_specs=VMEM, out_shap...  6.86 us
  transfers between devices with their start and end apart: 4, of which 2 were waited for; matrix products, arithmetic and copies ran while one was open for 3% of the time, Pallas kernels for 22%

profile of v2, /device:TPU:1, one launch (start us, length us, event | category | flops | bytes accessed | tf_op | source)
XLA Modules:
  0.0 100.2 jit_solution(8357030329629748647)
XLA Ops:
  1.3 2.4 %copy.14.pixels_ref = bf16[8,256,180]{2,1,0:T(8,128)(2,1)} copy(bf16[8,256,180]{1,0,2:T(8,128)(2,1)} %param.12) | data formatting | bytes 1474560 | tf_op args[0]
  3.6 3.3 %spread.1 = (bf16[64,16,384]{2,1,0:T(8,128)(2,1)}, bf16[4,256,180]{2,1,0:T(8,128)(2,1)}, bf16[4,256,180]{2,1,0:T(8,128)(2,1)}) custom-call(s32[1,32]{1,0:T(1,128)} %keep_ref.3, s32[1]{0:T(128)S(6)} %copy.18.count_ref, s32[1,16]{1,0:T(1,128)} %dest_ref.1, s32[1,16]{1,0:T(1,128)} %slot_ref.1, bf16[8,256,180]{2,1,0:T(8,128)(2,1)} %copy.14.pixels_ref), custom_call_target="tpu_custom_call" | custom-call | flops 100000000 | bytes 2000000 | tf_op jit(solution)/shard_map/spread/pallas_call | solution.py:324
  6.9 0.0 copy-start.4
  6.9 0.0 copy-start.3
  6.9 15.2 %all-to-all-start = ((bf16[64,16,384]{2,1,0:T(8,128)(2,1)}), bf16[64,16,384]{2,1,0:T(8,128)(2,1)S(1)}, u32[]{:S(2)}, u32[]{:S(2)}) async-start(bf16[64,16,384]{2,1,0:T(8,128)(2,1)} %get-tuple-element.20), calls=%async_computation | async-start | bytes 1572864 | tf_op jit(solution)/shard_map/all_to_all | solution.py:468
  22.2 0.0 copy-done.4
  22.2 7.1 %collective-permute-start = (bf16[4,256,180]{2,1,0:T(8,128)(2,1)S(1)}, bf16[4,256,180]{2,1,0:T(8,128)(2,1)S(1)}, u32[]{:S(2)}, u32[]{:S(2)}) collective-permute-start(bf16[4,256,180]{2,1,0:T(8,128)(2,1)S(1)} %copy-done.4), channel_id=1, source_target_pairs={{0,252},{4,0},{8,4},{12,8},{16,12},{20,16},{24,20},{28,24},{32,28}... | collective-permute-start | bytes 1105928 | tf_op jit(solution)/shard_map/ppermute | solution.py:448
  29.3 0.0 copy-done.3
  29.3 0.8 copy.15.output_ref
  30.1 2.6 %prep.1 = (bf16[384,180]{1,0:T(8,128)(2,1)}, bf16[180,768]{1,0:T(8,128)(2,1)}, bf16[192,180]{1,0:T(8,128)(2,1)}, bf16[180,192]{1,0:T(8,128)(2,1)}, f32[6,64,128]{2,1,0:T(8,128)}) custom-call(bf16[180,540]{1,0:T(8,128)(2,1)} %qkv_ref.1, bf16[180,180]{1,0:T(8,128)(2,1)} %proj_ref.1, f32[6,225]{1,0:T(8,128)} %bitcast.6), custom_call_target="tpu_custom_call" | custom-call | flops 600000000 | bytes 1500000 | tf_op jit(solution)/shard_map/prep/pallas_call | solution.py:174
  32.7 12.4 %all-to-all-done.got_ref = bf16[64,16,384]{2,1,0:T(8,128)(2,1)S(1)} async-done(((bf16[64,16,384]{2,1,0:T(8,128)(2,1)}), bf16[64,16,384]{2,1,0:T(8,128)(2,1)S(1)}, u32[]{:S(2)}, u32[]{:S(2)}) %all-to-all-start) | async-done | bytes 786464 | tf_op jit(solution)/shard_map/all_to_all | solution.py:468
  45.1 0.0 copy-start
  45.1 0.9 copy-done
  46.0 3.5 %route.1 = bf16[64,8,384]{2,1,0:T(8,128)(2,1)} custom-call(bf16[64,16,384]{2,1,0:T(8,128)(2,1)} %copy-done), custom_call_target="tpu_custom_call" | custom-call | flops 1200000000 | bytes 1200000 | tf_op jit(solution)/shard_map/route/pallas_call | solution.py:382
  49.6 7.5 %all-to-all-start.1 = ((bf16[64,8,384]{2,1,0:T(8,128)(2,1)}), bf16[64,8,384]{2,1,0:T(8,128)(2,1)S(1)}, u32[]{:S(2)}, u32[]{:S(2)}) async-start(bf16[64,8,384]{2,1,0:T(8,128)(2,1)} %route.1), calls=%async_computation.1 | async-start | bytes 786432 | tf_op jit(solution)/shard_map/all_to_all | solution.py:486
  57.1 0.0 collective-permute-done.halo_ref
  57.1 0.0 copy-start.5
  57.1 0.8 copy-done.5
  57.9 15.6 %own_path.1 = (bf16[4,256,180]{2,1,0:T(8,128)(2,1)}, bf16[4,256,180]{2,1,0:T(8,128)(2,1)}) custom-call(s32[1,32]{1,0:T(1,128)} %keep_ref.3, s32[1]{0:T(128)S(6)} %copy.18.count_ref, bf16[4,256,180]{2,1,0:T(8,128)(2,1)} %get-tuple-element.12.rest_ref, bf16[4,256,180]{2,1,0:T(8,128)(2,1)} %copy-done.5, f32[6,64,128]{2,1,0:T(8,128)} %get-tuple-element.14.bias_ref, ...), custom_call_target="tpu_custom_call" | custom-call | flops 20000000000 | bytes 3000000 | tf_op jit(solution)/shard_map/own_path/pallas_call | solution.py:259
  73.5 0.0 copy-start.1
  73.5 2.6 %collective-permute-start.1 = (bf16[4,256,180]{2,1,0:T(8,128)(2,1)}, bf16[4,256,180]{2,1,0:T(8,128)(2,1)S(1)}, u32[]{:S(2)}, u32[]{:S(2)}) collective-permute-start(bf16[4,256,180]{2,1,0:T(8,128)(2,1)} %get-tuple-element.18), channel_id=1, source_target_pairs={{0,4},{4,8},{8,12},{12,16},{16,20},{20,24},{24,28},{28,32},{32,36}... | collective-permute-start | bytes 1105928 | tf_op jit(solution)/shard_map/ppermute | solution.py:448
  76.1 14.7 %collective-permute-done.1 = bf16[4,256,180]{2,1,0:T(8,128)(2,1)S(1)} collective-permute-done((bf16[4,256,180]{2,1,0:T(8,128)(2,1)}, bf16[4,256,180]{2,1,0:T(8,128)(2,1)S(1)}, u32[]{:S(2)}, u32[]{:S(2)}) %collective-permute-start.1) | collective-permute-done | bytes 368672 | tf_op jit(solution)/shard_map/ppermute | solution.py:448
  90.9 0.0 copy-done.1
  90.9 0.3 pad_maximum_fusion
  91.2 1.4 %copy.16 = bf16[8,256,180]{1,0,2:T(8,128)(2,1)} copy(bf16[8,256,180]{2,1,0:T(8,128)(2,1)S(1)} %pad_maximum_fusion) | data formatting | bytes 1474560
  92.6 0.0 all-to-all-done.1.got_ref
  92.6 0.0 copy-start.2
  92.6 0.7 copy-done.2
  93.3 6.9 %work_path.1 = bf16[180,8,128]{2,1,0:T(8,128)(2,1)} custom-call(bf16[64,8,384]{2,1,0:T(8,128)(2,1)} %copy-done.2, f32[6,64,128]{2,1,0:T(8,128)} %get-tuple-element.14.bias_ref, f32[1,180]{1,0:T(1,128)} %bitcast.9, bf16[384,180]{1,0:T(8,128)(2,1)} %get-tuple-element.15.wqv_ref, bf16[180,768]{1,0:T(8,128)(2,1)} %get-tuple-element.16.wk_ref, ...), custom_call_target="tpu_custom_call" | custom-call | flops 8000000000 | bytes 2000000 | tf_op jit(solution)/shard_map/work_path/pallas_call | solution.py:429
  (3 shorter events, 0.1 us)
Async XLA Ops:
  6.9 15.2 %copy-start.4 = (bf16[4,256,180]{2,1,0:T(8,128)(2,1)S(1)}, bf16[4,256,180]{2,1,0:T(8,128)(2,1)}, u32[]{:S(2)}) copy-start(bf16[4,256,180]{2,1,0:T(8,128)(2,1)} %get-tuple-element.13) | copy-start | bytes 1105924
  6.9 22.4 %copy-start.3 = (bf16[360,180]{0,1:T(8,128)(2,1)S(1)}, bf16[360,180]{0,1:T(8,128)(2,1)}, u32[]{:S(2)}) copy-start(bf16[360,180]{0,1:T(8,128)(2,1)} %param.23) | copy-start | bytes 388804
  6.9 38.2 %all-to-all-start = ((bf16[64,16,384]{2,1,0:T(8,128)(2,1)}), bf16[64,16,384]{2,1,0:T(8,128)(2,1)S(1)}, u32[]{:S(2)}, u32[]{:S(2)}) async-start(bf16[64,16,384]{2,1,0:T(8,128)(2,1)} %get-tuple-element.20), calls=%async_computation | async-start | bytes 1572864 | tf_op jit(solution)/shard_map/all_to_all | solution.py:468
  22.2 34.9 %collective-permute-start = (bf16[4,256,180]{2,1,0:T(8,128)(2,1)S(1)}, bf16[4,256,180]{2,1,0:T(8,128)(2,1)S(1)}, u32[]{:S(2)}, u32[]{:S(2)}) collective-permute-start(bf16[4,256,180]{2,1,0:T(8,128)(2,1)S(1)} %copy-done.4), channel_id=1, source_target_pairs={{0,252},{4,0},{8,4},{12,8},{16,12},{20,16},{24,20},{28,24},{32,28}... | collective-permute-start | bytes 1105928 | tf_op jit(solution)/shard_map/ppermute | solution.py:448
  45.1 0.9 copy-start
  49.6 43.0 %all-to-all-start.1 = ((bf16[64,8,384]{2,1,0:T(8,128)(2,1)}), bf16[64,8,384]{2,1,0:T(8,128)(2,1)S(1)}, u32[]{:S(2)}, u32[]{:S(2)}) async-start(bf16[64,8,384]{2,1,0:T(8,128)(2,1)} %route.1), calls=%async_computation.1 | async-start | bytes 786432 | tf_op jit(solution)/shard_map/all_to_all | solution.py:486
  57.1 0.8 copy-start.5
  73.5 17.3 %copy-start.1 = (bf16[4,256,180]{2,1,0:T(8,128)(2,1)S(1)}, bf16[4,256,180]{2,1,0:T(8,128)(2,1)}, u32[]{:S(2)}) copy-start(bf16[4,256,180]{2,1,0:T(8,128)(2,1)} %get-tuple-element.19) | copy-start | bytes 1105924
  73.5 17.3 %collective-permute-start.1 = (bf16[4,256,180]{2,1,0:T(8,128)(2,1)}, bf16[4,256,180]{2,1,0:T(8,128)(2,1)S(1)}, u32[]{:S(2)}, u32[]{:S(2)}) collective-permute-start(bf16[4,256,180]{2,1,0:T(8,128)(2,1)} %get-tuple-element.18), channel_id=1, source_target_pairs={{0,4},{4,8},{8,12},{12,16},{16,20},{20,24},{24,28},{28,32},{32,36}... | collective-permute-start | bytes 1105928 | tf_op jit(solution)/shard_map/ppermute | solution.py:448
  92.6 0.7 copy-start.2

commit v3 on v2

--- a/solution.py
+++ b/solution.py
@@ -115,7 +115,7 @@
 def feed(states, gain, hidden_ref, output_ref):
     normed = layer_norm(states, gain).astype(BF16)
     inner = jax.nn.gelu(dot(normed, hidden_ref[...]), approximate=True).astype(BF16)
-    return states + dot(inner, output_ref[...])
+    return states + dot(inner, output_ref[...], 1, 1)
 
 
 VMEM = pl.BlockSpec(memory_space=pltpu.VMEM)
@@ -190,6 +190,24 @@
     )(qkv_weight, proj_weight, table)
 
 
+def turned_rows(flat, row, stride):
+    rows = pl.ds(row, 256, stride=stride)
+    return jnp.concatenate([half[rows, :] for half in flat], axis=1).astype(BF16)
+
+
+def hold_channels(block_ref, flat):
+    channels, rows, _ = block_ref.shape
+    for index, half in enumerate(flat):
+        values = block_ref[:, :, index * 128 : (index + 1) * 128].astype(F32)
+        half[0 : channels * rows, :] = values.reshape(channels * rows, 128)
+        half[channels * rows :, :] = jnp.zeros((half.shape[0] - channels * rows, 128), F32)
+
+
+def roll_pick(columns):
+    wanted = (iota((columns, columns), 0) + SHIFT) & (columns - 1)
+    return (wanted == iota((columns, columns), 1)).astype(F32).astype(BF16)
+
+
 def own_kernel(
     keep_ref,
     count_ref,
@@ -204,11 +222,17 @@
     hidden_ref,
     output_ref,
     out_ref,
-    send_ref,
     active,
+    flat0,
+    flat1,
+    lower_rows,
+    finished,
+    turned0,
+    turned1,
 ):
     step = pl.program_id(0)
     steps = pl.num_programs(0)
+    columns_all = out_ref.shape[2]
     pairs = rest_ref.shape[1] // (TILE * WIN)
     row_flag = jnp.where(lax.axis_index("band") == lax.axis_size("band") - 1, 1.0, 0.0)
 
@@ -219,12 +243,18 @@
             keep = keep_ref[0, w]
             position = position + keep
             active[w] = jnp.where((keep == 1) & (position < count_ref[0]), 1, 0)
+        hold_channels(halo_ref, (flat0, flat1))
+        pick = roll_pick(columns_all)
+        for row in range(SHIFT):
+            got = dot(pick, turned_rows((flat0, flat1), row, SHIFT), 1, 1)
+            lower_rows[row] = got[:, :CHAN]
 
     tokens, masks = [], []
     for pair in range(pairs):
         columns = pl.ds(pair * TILE * WIN, TILE * WIN)
+        start = pl.multiple_of((step * pairs + pair) * TILE * WIN, TILE * WIN)
         upper = rest_ref[:, columns, :].astype(F32)
-        lower = halo_ref[:, columns, :].astype(F32)
+        lower = lower_rows[:, pl.ds(start, TILE * WIN), :]
         for w in range(TILE):
             for part in (upper, lower):
                 tokens.append(
@@ -239,30 +269,50 @@
     attended = attended.astype(BF16).astype(F32)
     done = feed(attended, gain_mlp_ref[...], hidden_ref, output_ref)
     for pair in range(pairs):
-        columns = pl.ds(pair * TILE * WIN, TILE * WIN)
-        uppers, lowers = [], []
+        start = pl.multiple_of((step * pairs + pair) * TILE * WIN, TILE * WIN)
+        kept = []
         for w in range(TILE):
             at = pair * TILE + w
             on = active[step * pairs * TILE + at]
             rows = slice(at * TOKENS, (at + 1) * TOKENS)
-            kept = jnp.where(on == 1, done[rows], x[rows]).reshape(WIN, WIN, CHAN)
-            uppers.append(kept[:SHIFT])
-            lowers.append(kept[SHIFT:])
-        out_ref[:, columns, :] = jnp.concatenate(uppers, axis=1).astype(BF16)
-        send_ref[:, columns, :] = jnp.concatenate(lowers, axis=1).astype(BF16)
+            kept.append(jnp.where(on == 1, done[rows], x[rows]).reshape(WIN, WIN, CHAN))
+        kept = jnp.concatenate(kept, axis=1).astype(BF16)
+        finished[:, pl.ds(start, TILE * WIN), :] = kept
+
+    @pl.when(step == steps - 1)
+    def _():
+        same = (iota((CHAN, CHAN), 0) == iota((CHAN, CHAN), 1)).astype(F32).astype(BF16)
+        for row in range(WIN):
+            got = dot(same, finished[(row + SHIFT) % WIN], 1, 1)
+            got = pltpu.roll(got, SHIFT, 1)
+            rows = pl.ds(row, CHAN, stride=WIN)
+            turned0[rows, :] = got[:, :128]
+            turned1[rows, :] = got[:, 128:]
+        out_ref[:, :, 0:128] = turned0[...].reshape(CHAN, WIN, 128).astype(BF16)
+        out_ref[:, :, 128:256] = turned1[...].reshape(CHAN, WIN, 128).astype(BF16)
 
 
 def own_path(keep, count, rest, halo, bias, gain_attn, wqv, wk, proj, gain_mlp, hidden, output):
     rows, columns, _ = rest.shape
     per_step = 2 * TILE * WIN
     block = pl.BlockSpec((rows, per_step, CHAN), lambda i: (0, i, 0))
+    flat = pltpu.VMEM((256 * SHIFT, 128), F32)
+    turned = pltpu.VMEM((CHAN * WIN, 128), F32)
     return pl.pallas_call(
         own_kernel,
         grid=(columns // per_step,),
-        in_specs=[SMEM, SMEM, block, block] + [VMEM] * 8,
-        out_specs=[block, block],
-        out_shape=[jax.ShapeDtypeStruct(rest.shape, BF16)] * 2,
-        scratch_shapes=[pltpu.SMEM((columns // WIN,), jnp.int32)],
+        in_specs=[SMEM, SMEM, block] + [VMEM] * 9,
+        out_specs=VMEM,
+        out_shape=jax.ShapeDtypeStruct((CHAN, WIN, columns), BF16),
+        scratch_shapes=[
+            pltpu.SMEM((columns // WIN,), jnp.int32),
+            flat,
+            flat,
+            pltpu.VMEM((SHIFT, columns, CHAN), F32),
+            pltpu.VMEM((WIN, columns, CHAN), BF16),
+            turned,
+            turned,
+        ],
         cost_estimate=pl.CostEstimate(
             flops=20_000_000_000, bytes_accessed=3_000_000, transcendentals=2_000_000
         ),
@@ -271,9 +321,9 @@
 
 
 def spread_kernel(
-    keep_ref, count_ref, dest_ref, slot_ref, pixels_ref, out_ref, top_ref, rest_ref, heads, tails
+    keep_ref, count_ref, dest_ref, slot_ref, pixels_ref, out_ref, rest_ref, flat0, flat1
 ):
-    rows, columns, _ = pixels_ref.shape
+    _, rows, columns = pixels_ref.shape
     windows = columns // WIN
     half = windows // 2
     bands = lax.axis_size("band")
@@ -295,40 +345,41 @@
         codes = jnp.where(here & (lane == first), dest, codes)
         codes = jnp.where(here & (lane == first + 1), place, codes)
 
-    tails[...] = jnp.zeros(tails.shape, F32)
+    hold_channels(pixels_ref, (flat0, flat1))
+    out_row = iota((columns, columns), 0)
+    wanted = ((out_row & (windows - 1)) * WIN + (out_row >> 5) + SHIFT) & (columns - 1)
+    group = (wanted == iota((columns, columns), 1)).astype(F32).astype(BF16)
+    pick = roll_pick(columns)
     for r in range(rows):
-        values = pixels_ref[r].astype(F32)
-        heads[r, 0:columns, :] = values[:, 0:128]
-        tails[r, 0:columns, 0:TAIL] = values[:, 128:CHAN]
-        heads[r, columns : columns + WIN, :] = values[0:WIN, 0:128]
-        tails[r, columns : columns + WIN, 0:TAIL] = values[0:WIN, 128:CHAN]
-    for r in range(rows):
-        target = top_ref.at[r] if r < SHIFT else rest_ref.at[r - SHIFT]
-        target[:, 0:128] = heads[r, SHIFT : SHIFT + columns, :].astype(BF16)
-        target[:, 128:CHAN] = tails[r, SHIFT : SHIFT + columns, 0:TAIL].astype(BF16)
-    for token in range(TOKENS):
-        r = (token // WIN + SHIFT) % rows
-        picked = pl.ds(token % WIN + SHIFT, windows, stride=WIN)
-        head = heads[r, picked, :]
-        tail = tails[r, picked, :]
-        packed = tail[:half] + pltpu.roll(tail[half:], TAIL, 1) + codes
-        out_ref[token, :, 0:128] = head[:half].astype(BF16)
-        out_ref[token, :, 128:256] = head[half:].astype(BF16)
-        out_ref[token, :, 256:384] = packed.astype(BF16)
+        line = turned_rows((flat0, flat1), r, rows)
+        if r >= SHIFT:
+            rest_ref[r - SHIFT] = dot(pick, line, 1, 1)[:, :CHAN].astype(BF16)
+        got = dot(group, line, 1, 1)
+        for cu in range(WIN):
+            token = (r + SHIFT) % rows * WIN + cu
+            low = got[cu * windows : cu * windows + half]
+            high = got[cu * windows + half : (cu + 1) * windows]
+            packed = low[:, 128:] + pltpu.roll(high[:, 128:], TAIL, 1) + codes
+            out_ref[token, :, 0:128] = low[:, :128].astype(BF16)
+            out_ref[token, :, 128:256] = high[:, :128].astype(BF16)
+            out_ref[token, :, 256:384] = packed.astype(BF16)
 
 
 def spread(keep, count, dest, slot, pixels):
-    rows, columns, _ = pixels.shape
+    _, rows, columns = pixels.shape
     half = columns // WIN // 2
-    part = jax.ShapeDtypeStruct((SHIFT, columns, CHAN), BF16)
+    flat = pltpu.VMEM((256 * rows, 128), F32)
     return pl.pallas_call(
         spread_kernel,
         in_specs=[SMEM] * 4 + [VMEM],
-        out_specs=[VMEM] * 3,
-        out_shape=[jax.ShapeDtypeStruct((TOKENS, half, 384), BF16), part, part],
-        scratch_shapes=[pltpu.VMEM((rows, columns + WIN, 128), F32)] * 2,
+        out_specs=[VMEM] * 2,
+        out_shape=[
+            jax.ShapeDtypeStruct((TOKENS, half, 384), BF16),
+            jax.ShapeDtypeStruct((SHIFT, columns, CHAN), BF16),
+        ],
+        scratch_shapes=[flat, flat],
         cost_estimate=pl.CostEstimate(
-            flops=100_000_000, bytes_accessed=2_000_000, transcendentals=0
+            flops=500_000_000, bytes_accessed=2_000_000, transcendentals=0
         ),
         name="spread",
     )(keep, count, dest, slot, pixels)
@@ -463,11 +514,12 @@
     output_weight,
 ):
     gain_attn, gain_mlp = gain_attn[None], gain_mlp[None]
-    outgoing, top, rest = spread(keep_mask, band_counts, plan_dest, plan_slot, pixels)
-    halo = from_behind(top, "band", -1)
+    pixels = jnp.transpose(pixels, (2, 0, 1))
+    halo = from_behind(pixels[:, :SHIFT], "band", -1)
+    outgoing, rest = spread(keep_mask, band_counts, plan_dest, plan_slot, pixels)
     gathered = lax.all_to_all(outgoing, "band", split_axis=0, concat_axis=0, tiled=True)
     wqv, wk, proj, proj_turned, bias = prep(qkv_weight, proj_weight, bias_table.T)
-    kept, sent = own_path(
+    finished = own_path(
         keep_mask,
         band_counts,
         rest,
@@ -479,12 +531,13 @@
         proj,
         gain_mlp,
         hidden_weight,
-        output_weight,
+        output_weight.T,
     )
-    upper = from_behind(sent, "band", 1)
+    upper = from_behind(finished[:, :SHIFT], "band", 1)
     routed = route(gathered)
     incoming = lax.all_to_all(routed, "band", split_axis=0, concat_axis=0, tiled=True)
-    restored = jnp.roll(jnp.concatenate([upper, kept], axis=0), SHIFT, axis=1)
+    restored = jnp.concatenate([upper, finished[:, SHIFT:]], axis=1)
+    restored = jnp.transpose(restored, (1, 2, 0))
     work_tiles = work_path(incoming, bias, gain_attn, wqv, wk, proj_turned)
     work_tiles = jnp.transpose(work_tiles, (1, 2, 0))
     return (restored, work_tiles)

time: 101 us -> 97.4 us (0.964)
  local copies, waits for them, and re-layouts: 7.08 us -> 4.09 us
  waiting for transfers between devices: 27.1 us -> 24.3 us
  Pallas kernels: 31.9 us -> 33 us
    unnamed x16 -> x8, local copies, waits for them, and re-layouts: 7.03 us -> 2.36 us
    ppermute x2, waiting for transfers between devices: 14.7 us -> 11.2 us  [from_behind(): return lax.ppermute(value, axis, pairs)]
    slice x1 -> x2, local copies, waits for them, and re-layouts: 0.01 us -> 1.72 us  [the longest x1 1.63 us: shards(): upper = from_behind(finished[:, :SHIFT], 'band', 1)]
    pallas_call x1, Pallas kernels: 15.6 us -> 16.9 us  [own_path(): pl.pallas_call(own_kernel, grid=(columns // per_step,), in_specs=[SMEM, S...]
    transpose x0 -> x1, other arithmetic: none -> 1.22 us  [shards(): restored = jnp.transpose(restored, (1, 2, 0))]
  transfers between devices with their start and end apart: 4 -> 4, of which waited for: 2 -> 2; matrix products, arithmetic and copies ran while one was open for 3% -> 3% of each run, Pallas kernels for 22% -> 24%
where the time goes in v3:
time: 97.4 us; the launch traced here: 96.3 us
  Pallas kernels  33 us (34%)
  starting transfers between devices  32.5 us (33%)
  waiting for transfers between devices  24.3 us (25%)
  local copies, waits for them, and re-layouts  4.09 us (4%)
  between operations  1.34 us (1%)
  other arithmetic  1.22 us (1%)
    pallas_call x1, Pallas kernels, own_path(): pl.pallas_call(own_kernel, grid=(columns // per_step,), in_specs=[SMEM, S...  16.9 us
    all_to_all x1, starting transfers between devices, shards(): lax.all_to_all(outgoing, 'band', split_axis=0, concat_axis=0, tiled=True)  15.2 us
    all_to_all x1, waiting for transfers between devices, shards(): lax.all_to_all(outgoing, 'band', split_axis=0, concat_axis=0, tiled=True)  13.1 us
    ppermute x2, waiting for transfers between devices, from_behind(): return lax.ppermute(value, axis, pairs)  11.2 us
    ppermute x2, starting transfers between devices, from_behind(): return lax.ppermute(value, axis, pairs)  9.7 us
    all_to_all x1, starting transfers between devices, shards(): lax.all_to_all(routed, 'band', split_axis=0, concat_axis=0, tiled=True)  7.53 us
    pallas_call x1, Pallas kernels, work_path(): pl.pallas_call(work_kernel, in_specs=[VMEM] * 6, out_specs=VMEM, out_shap...  6.86 us
    pallas_call x1, Pallas kernels, route(): pl.pallas_call(route_kernel, in_specs=[VMEM], out_specs=VMEM, out_shape=j...  3.52 us
  transfers between devices with their start and end apart: 4, of which 2 were waited for; matrix products, arithmetic and copies ran while one was open for 3% of the time, Pallas kernels for 24%

profile of v3, /device:TPU:1, one launch (start us, length us, event | category | flops | bytes accessed | tf_op | source)
XLA Modules:
  0.0 96.3 jit_solution(16464102658226491263)
XLA Ops:
  1.3 3.1 %spread.1 = (bf16[64,16,384]{2,1,0:T(8,128)(2,1)}, bf16[4,256,180]{2,1,0:T(8,128)(2,1)}) custom-call(s32[1,32]{1,0:T(1,128)} %keep_ref.3, s32[1]{0:T(128)S(6)} %copy.14.count_ref, s32[1,16]{1,0:T(1,128)} %dest_ref.1, s32[1,16]{1,0:T(1,128)} %slot_ref.1, bf16[180,8,256]{2,1,0:T(8,128)(2,1)} %bitcast.8), custom_call_target="tpu_custom_call" | custom-call | flops 500000000 | bytes 2000000 | tf_op jit(solution)/shard_map/spread/pallas_call | solution.py:372
  4.4 0.0 copy-start.2
  4.4 15.2 %all-to-all-start = ((bf16[64,16,384]{2,1,0:T(8,128)(2,1)}), bf16[64,16,384]{2,1,0:T(8,128)(2,1)S(1)}, u32[]{:S(2)}, u32[]{:S(2)}) async-start(bf16[64,16,384]{2,1,0:T(8,128)(2,1)} %get-tuple-element.14), calls=%async_computation | async-start | bytes 1572864 | tf_op jit(solution)/shard_map/all_to_all | solution.py:520
  19.6 0.0 copy-done.2
  19.6 0.1 slice.12
  19.7 7.1 %collective-permute-start = (bf16[180,4,256]{2,1,0:T(4,128)(2,1)S(1)}, bf16[180,4,256]{2,1,0:T(4,128)(2,1)S(1)}, u32[]{:S(2)}, u32[]{:S(2)}) collective-permute-start(bf16[180,4,256]{2,1,0:T(4,128)(2,1)S(1)} %slice.12), channel_id=1, source_target_pairs={{0,252},{4,0},{8,4},{12,8},{16,12},{20,16},{24,20},{28,24},{32,28}... | collective-permute-start | bytes 1105928 | tf_op jit(solution)/shard_map/ppermute | solution.py:499
  26.8 2.6 %prep.1 = (bf16[384,180]{1,0:T(8,128)(2,1)}, bf16[180,768]{1,0:T(8,128)(2,1)}, bf16[192,180]{1,0:T(8,128)(2,1)}, bf16[180,192]{1,0:T(8,128)(2,1)}, f32[6,64,128]{2,1,0:T(8,128)}) custom-call(bf16[180,540]{1,0:T(8,128)(2,1)} %qkv_ref.1, bf16[180,180]{1,0:T(8,128)(2,1)} %proj_ref.1, f32[6,225]{1,0:T(8,128)} %bitcast.11), custom_call_target="tpu_custom_call" | custom-call | flops 600000000 | bytes 1500000 | tf_op jit(solution)/shard_map/prep/pallas_call | solution.py:174
  29.4 13.1 %all-to-all-done.got_ref = bf16[64,16,384]{2,1,0:T(8,128)(2,1)S(1)} async-done(((bf16[64,16,384]{2,1,0:T(8,128)(2,1)}), bf16[64,16,384]{2,1,0:T(8,128)(2,1)S(1)}, u32[]{:S(2)}, u32[]{:S(2)}) %all-to-all-start) | async-done | bytes 786464 | tf_op jit(solution)/shard_map/all_to_all | solution.py:520
  42.6 0.0 copy-start
  42.6 0.9 copy-done
  43.4 3.5 %route.1 = bf16[64,8,384]{2,1,0:T(8,128)(2,1)} custom-call(bf16[64,16,384]{2,1,0:T(8,128)(2,1)} %copy-done), custom_call_target="tpu_custom_call" | custom-call | flops 1200000000 | bytes 1200000 | tf_op jit(solution)/shard_map/route/pallas_call | solution.py:433
  47.0 7.5 %all-to-all-start.1 = ((bf16[64,8,384]{2,1,0:T(8,128)(2,1)}), bf16[64,8,384]{2,1,0:T(8,128)(2,1)S(1)}, u32[]{:S(2)}, u32[]{:S(2)}) async-start(bf16[64,8,384]{2,1,0:T(8,128)(2,1)} %route.1), calls=%async_computation.1 | async-start | bytes 786432 | tf_op jit(solution)/shard_map/all_to_all | solution.py:538
  54.5 0.0 collective-permute-done.halo_ref
  54.5 0.0 copy-start.3
  54.5 0.7 copy-done.3
  55.2 16.9 %own_path.1 = bf16[180,8,256]{2,1,0:T(8,128)(2,1)} custom-call(s32[1,32]{1,0:T(1,128)} %keep_ref.3, s32[1]{0:T(128)S(6)} %copy.14.count_ref, bf16[4,256,180]{2,1,0:T(8,128)(2,1)} %get-tuple-element.9.rest_ref, bf16[180,4,256]{2,1,0:T(4,128)(2,1)} %copy-done.3, f32[6,64,128]{2,1,0:T(8,128)} %get-tuple-element.10.bias_ref, f32[1,180]{1,0:T(1,128)} %bitcast.13, ...), custom_call_target="tpu_custom_call" | custom-call | flops 20000000000 | bytes 3000000 | tf_op jit(solution)/shard_map/own_path/pallas_call | solution.py:301
  72.2 1.6 %fusion = (bf16[180,4,256]{2,1,0:T(4,128)(2,1)S(1)}, bf16[180,4,256]{2,1,0:T(4,128)(2,1)S(1)}) fusion(bf16[180,8,256]{2,1,0:T(8,128)(2,1)} %own_path.1), kind=kLoop, calls=%fused_computation.1 | loop fusion | bytes 1474560 | tf_op jit(solution)/shard_map/slice | solution.py:536
  73.8 2.6 %collective-permute-start.1 = (bf16[180,4,256]{2,1,0:T(4,128)(2,1)S(1)}, bf16[180,4,256]{2,1,0:T(4,128)(2,1)S(1)}, u32[]{:S(2)}, u32[]{:S(2)}) collective-permute-start(bf16[180,4,256]{2,1,0:T(4,128)(2,1)S(1)} %get-tuple-element.16), channel_id=1, source_target_pairs={{0,4},{4,8},{8,12},{12,16},{16,20},{20,24},{24,28},{28,32},{32,36}... | collective-permute-start | bytes 1105928 | tf_op jit(solution)/shard_map/ppermute | solution.py:499
  76.4 11.2 %collective-permute-done.1 = bf16[180,4,256]{2,1,0:T(4,128)(2,1)S(1)} collective-permute-done((bf16[180,4,256]{2,1,0:T(4,128)(2,1)S(1)}, bf16[180,4,256]{2,1,0:T(4,128)(2,1)S(1)}, u32[]{:S(2)}, u32[]{:S(2)}) %collective-permute-start.1) | collective-permute-done | bytes 368672 | tf_op jit(solution)/shard_map/ppermute | solution.py:499
  87.5 1.2 %maximum_bitcast_fusion = bf16[8,256,180]{1,0,2:T(8,128)(2,1)} fusion(bf16[180,4,256]{2,1,0:T(4,128)(2,1)S(1)} %get-tuple-element.17, bf16[180,4,256]{2,1,0:T(4,128)(2,1)S(1)} %collective-permute-done.1), kind=kLoop, calls=%fused_computation | loop fusion | flops 1474560 | bytes 1474560 | tf_op jit(solution)/shard_map/transpose | solution.py:540
  88.7 0.0 all-to-all-done.1.got_ref
  88.7 0.0 copy-start.1
  88.7 0.7 copy-done.1
  89.5 6.9 %work_path.1 = bf16[180,8,128]{2,1,0:T(8,128)(2,1)} custom-call(bf16[64,8,384]{2,1,0:T(8,128)(2,1)} %copy-done.1, f32[6,64,128]{2,1,0:T(8,128)} %get-tuple-element.10.bias_ref, f32[1,180]{1,0:T(1,128)} %bitcast.14, bf16[384,180]{1,0:T(8,128)(2,1)} %get-tuple-element.11.wqv_ref, bf16[180,768]{1,0:T(8,128)(2,1)} %get-tuple-element.12.wk_ref, ...), custom_call_target="tpu_custom_call" | custom-call | flops 8000000000 | bytes 2000000 | tf_op jit(solution)/shard_map/work_path/pallas_call | solution.py:480
Async XLA Ops:
  4.4 15.2 %copy-start.2 = (bf16[8,256,180]{1,0,2:T(8,128)(2,1)S(1)}, bf16[8,256,180]{1,0,2:T(8,128)(2,1)}, u32[]{:S(2)}) copy-start(bf16[8,256,180]{1,0,2:T(8,128)(2,1)} %param.12) | copy-start | bytes 2211844
  4.4 38.2 %all-to-all-start = ((bf16[64,16,384]{2,1,0:T(8,128)(2,1)}), bf16[64,16,384]{2,1,0:T(8,128)(2,1)S(1)}, u32[]{:S(2)}, u32[]{:S(2)}) async-start(bf16[64,16,384]{2,1,0:T(8,128)(2,1)} %get-tuple-element.14), calls=%async_computation | async-start | bytes 1572864 | tf_op jit(solution)/shard_map/all_to_all | solution.py:520
  19.7 34.8 %collective-permute-start = (bf16[180,4,256]{2,1,0:T(4,128)(2,1)S(1)}, bf16[180,4,256]{2,1,0:T(4,128)(2,1)S(1)}, u32[]{:S(2)}, u32[]{:S(2)}) collective-permute-start(bf16[180,4,256]{2,1,0:T(4,128)(2,1)S(1)} %slice.12), channel_id=1, source_target_pairs={{0,252},{4,0},{8,4},{12,8},{16,12},{20,16},{24,20},{28,24},{32,28}... | collective-permute-start | bytes 1105928 | tf_op jit(solution)/shard_map/ppermute | solution.py:499
  42.6 0.9 copy-start
  47.0 41.8 %all-to-all-start.1 = ((bf16[64,8,384]{2,1,0:T(8,128)(2,1)}), bf16[64,8,384]{2,1,0:T(8,128)(2,1)S(1)}, u32[]{:S(2)}, u32[]{:S(2)}) async-start(bf16[64,8,384]{2,1,0:T(8,128)(2,1)} %route.1), calls=%async_computation.1 | async-start | bytes 786432 | tf_op jit(solution)/shard_map/all_to_all | solution.py:538
  54.5 0.7 copy-start.3
  73.8 13.7 %collective-permute-start.1 = (bf16[180,4,256]{2,1,0:T(4,128)(2,1)S(1)}, bf16[180,4,256]{2,1,0:T(4,128)(2,1)S(1)}, u32[]{:S(2)}, u32[]{:S(2)}) collective-permute-start(bf16[180,4,256]{2,1,0:T(4,128)(2,1)S(1)} %get-tuple-element.16), channel_id=1, source_target_pairs={{0,4},{4,8},{8,12},{12,16},{16,20},{20,24},{24,28},{28,32},{32,36}... | collective-permute-start | bytes 1105928 | tf_op jit(solution)/shard_map/ppermute | solution.py:499
  88.7 0.7 copy-start.1

commit v4 on v3

--- a/solution.py
+++ b/solution.py
@@ -118,13 +118,15 @@
     return states + dot(inner, output_ref[...], 1, 1)
 
 
+def in_vmem(value):
+    return pltpu.with_memory_space_constraint(value, pltpu.VMEM)
+
+
 VMEM = pl.BlockSpec(memory_space=pltpu.VMEM)
 SMEM = pl.BlockSpec(memory_space=pltpu.SMEM)
 
 
-def prep_kernel(
-    qkv_ref, proj_ref, table_ref, wqv_ref, wk_ref, padded_ref, turned_ref, bias_ref, padded, looked
-):
+def pad_weights(qkv_ref, proj_ref, wqv_ref, wk_ref, padded_ref, turned_ref):
     half = HEADS * HEAD_PAD
 
     def source(column):
@@ -147,6 +149,8 @@
     pick = (source(iota((CHAN, half), 1)) == iota((CHAN, half), 0)).astype(F32).astype(BF16)
     turned_ref[...] = dot(proj, pick, 0, 0).astype(BF16)
 
+
+def spread_bias(table_ref, bias_ref, padded, looked):
     reach = 2 * WIN - 1
     padded[...] = jnp.zeros(padded.shape, F32)
     padded[0:HEADS, 0 : reach * reach] = table_ref[...]
@@ -169,27 +173,6 @@
         bias_ref[head] = looked[pl.ds(head, TOKENS, stride=8), :]
 
 
-def prep(qkv_weight, proj_weight, table):
-    half = HEADS * HEAD_PAD
-    return pl.pallas_call(
-        prep_kernel,
-        in_specs=[VMEM] * 3,
-        out_specs=[VMEM] * 5,
-        out_shape=[
-            jax.ShapeDtypeStruct((2 * half, CHAN), BF16),
-            jax.ShapeDtypeStruct((CHAN, HEADS * PAIR), BF16),
-            jax.ShapeDtypeStruct((half, CHAN), BF16),
-            jax.ShapeDtypeStruct((CHAN, half), BF16),
-            jax.ShapeDtypeStruct((HEADS, TOKENS, PAIR), F32),
-        ],
-        scratch_shapes=[pltpu.VMEM((8, 256), F32), pltpu.VMEM((8 * TOKENS, PAIR), F32)],
-        cost_estimate=pl.CostEstimate(
-            flops=600_000_000, bytes_accessed=1_500_000, transcendentals=0
-        ),
-        name="prep",
-    )(qkv_weight, proj_weight, table)
-
-
 def turned_rows(flat, row, stride):
     rows = pl.ds(row, 256, stride=stride)
     return jnp.concatenate([half[rows, :] for half in flat], axis=1).astype(BF16)
@@ -213,111 +196,124 @@
     count_ref,
     rest_ref,
     halo_ref,
-    bias_ref,
+    table_ref,
+    qkv_ref,
+    proj_ref,
     gain_attn_ref,
-    wqv_ref,
-    wk_ref,
-    proj_ref,
     gain_mlp_ref,
     hidden_ref,
     output_ref,
-    out_ref,
+    sent_ref,
+    kept_ref,
+    wqv_ref,
+    wk_ref,
+    turned_ref,
+    bias_ref,
     active,
+    padded_proj,
+    padded_table,
+    looked,
     flat0,
     flat1,
     lower_rows,
     finished,
-    turned0,
-    turned1,
 ):
-    step = pl.program_id(0)
-    steps = pl.num_programs(0)
-    columns_all = out_ref.shape[2]
-    pairs = rest_ref.shape[1] // (TILE * WIN)
+    columns_all = rest_ref.shape[1]
+    pairs = 8
+    steps = columns_all // (pairs * TILE * WIN)
     row_flag = jnp.where(lax.axis_index("band") == lax.axis_size("band") - 1, 1.0, 0.0)
 
-    @pl.when(step == 0)
-    def _():
-        position = jnp.int32(-1)
-        for w in range(keep_ref.shape[1]):
-            keep = keep_ref[0, w]
-            position = position + keep
-            active[w] = jnp.where((keep == 1) & (position < count_ref[0]), 1, 0)
-        hold_channels(halo_ref, (flat0, flat1))
-        pick = roll_pick(columns_all)
+    position = jnp.int32(-1)
+    for w in range(keep_ref.shape[1]):
+        keep = keep_ref[0, w]
+        position = position + keep
+        active[w] = jnp.where((keep == 1) & (position < count_ref[0]), 1, 0)
+    pad_weights(qkv_ref, proj_ref, wqv_ref, wk_ref, padded_proj, turned_ref)
+    spread_bias(table_ref, bias_ref, padded_table, looked)
+    hold_channels(halo_ref, (flat0, flat1))
+    pick = roll_pick(columns_all)
+    for row in range(SHIFT):
+        got = dot(pick, turned_rows((flat0, flat1), row, SHIFT), 1, 1)
+        lower_rows[row] = got[:, :CHAN]
+
+    def some_pairs(step, carry):
+        tokens, masks = [], []
+        for pair in range(pairs):
+            start = pl.multiple_of((step * pairs + pair) * TILE * WIN, TILE * WIN)
+            columns = pl.ds(start, TILE * WIN)
+            upper = rest_ref[:, columns, :].astype(F32)
+            lower = lower_rows[:, columns, :]
+            for w in range(TILE):
+                for part in (upper, lower):
+                    tokens.append(
+                        part[:, w * WIN : (w + 1) * WIN].reshape(SHIFT * WIN, CHAN)
+                    )
+            at_end = jnp.where((step == steps - 1) & (pair == pairs - 1), 1.0, 0.0)
+            masks.append(region_mask((row_flag, row_flag), (0.0, at_end)))
+        x = jnp.concatenate(tokens, axis=0)
+        mixed = attend(x, masks, bias_ref, gain_attn_ref[...], wqv_ref, wk_ref)
+        projected = [dot(part, padded_proj[...], 0, 0) for part in mixed]
+        attended = x + jnp.concatenate(projected, axis=0)
+        attended = attended.astype(BF16).astype(F32)
+        done = feed(attended, gain_mlp_ref[...], hidden_ref, output_ref)
+        for pair in range(pairs):
+            start = pl.multiple_of((step * pairs + pair) * TILE * WIN, TILE * WIN)
+            kept = []
+            for w in range(TILE):
+                at = pair * TILE + w
+                on = active[step * pairs * TILE + at]
+                rows = slice(at * TOKENS, (at + 1) * TOKENS)
+                kept.append(jnp.where(on == 1, done[rows], x[rows]).reshape(WIN, WIN, CHAN))
+            kept = jnp.concatenate(kept, axis=1).astype(BF16)
+            finished[:, pl.ds(start, TILE * WIN), :] = kept
+        return carry
+
+    lax.fori_loop(0, steps, some_pairs, 0)
+
+    same = (iota((CHAN, CHAN), 0) == iota((CHAN, CHAN), 1)).astype(F32).astype(BF16)
+    for first, out_ref in ((0, kept_ref), (SHIFT, sent_ref)):
         for row in range(SHIFT):
-            got = dot(pick, turned_rows((flat0, flat1), row, SHIFT), 1, 1)
-            lower_rows[row] = got[:, :CHAN]
-
-    tokens, masks = [], []
-    for pair in range(pairs):
-        columns = pl.ds(pair * TILE * WIN, TILE * WIN)
-        start = pl.multiple_of((step * pairs + pair) * TILE * WIN, TILE * WIN)
-        upper = rest_ref[:, columns, :].astype(F32)
-        lower = lower_rows[:, pl.ds(start, TILE * WIN), :]
-        for w in range(TILE):
-            for part in (upper, lower):
-                tokens.append(
-                    part[:, w * WIN : (w + 1) * WIN].reshape(SHIFT * WIN, CHAN)
-                )
-        at_end = jnp.where((step == steps - 1) & (pair == pairs - 1), 1.0, 0.0)
-        masks.append(region_mask((row_flag, row_flag), (0.0, at_end)))
-    x = jnp.concatenate(tokens, axis=0)
-    mixed = attend(x, masks, bias_ref, gain_attn_ref[...], wqv_ref, wk_ref)
-    projected = [dot(part, proj_ref[...], 0, 0) for part in mixed]
-    attended = x + jnp.concatenate(projected, axis=0)
-    attended = attended.astype(BF16).astype(F32)
-    done = feed(attended, gain_mlp_ref[...], hidden_ref, output_ref)
-    for pair in range(pairs):
-        start = pl.multiple_of((step * pairs + pair) * TILE * WIN, TILE * WIN)
-        kept = []
-        for w in range(TILE):
-            at = pair * TILE + w
-            on = active[step * pairs * TILE + at]
-            rows = slice(at * TOKENS, (at + 1) * TOKENS)
-            kept.append(jnp.where(on == 1, done[rows], x[rows]).reshape(WIN, WIN, CHAN))
-        kept = jnp.concatenate(kept, axis=1).astype(BF16)
-        finished[:, pl.ds(start, TILE * WIN), :] = kept
-
-    @pl.when(step == steps - 1)
-    def _():
-        same = (iota((CHAN, CHAN), 0) == iota((CHAN, CHAN), 1)).astype(F32).astype(BF16)
-        for row in range(WIN):
-            got = dot(same, finished[(row + SHIFT) % WIN], 1, 1)
-            got = pltpu.roll(got, SHIFT, 1)
-            rows = pl.ds(row, CHAN, stride=WIN)
-            turned0[rows, :] = got[:, :128]
-            turned1[rows, :] = got[:, 128:]
-        out_ref[:, :, 0:128] = turned0[...].reshape(CHAN, WIN, 128).astype(BF16)
-        out_ref[:, :, 128:256] = turned1[...].reshape(CHAN, WIN, 128).astype(BF16)
-
-
-def own_path(keep, count, rest, halo, bias, gain_attn, wqv, wk, proj, gain_mlp, hidden, output):
-    rows, columns, _ = rest.shape
-    per_step = 2 * TILE * WIN
-    block = pl.BlockSpec((rows, per_step, CHAN), lambda i: (0, i, 0))
+            got = pltpu.roll(dot(same, finished[first + row], 1, 1), SHIFT, 1)
+            rows = pl.ds(row, CHAN, stride=SHIFT)
+            flat0[rows, :] = got[:, :128]
+            flat1[rows, :] = got[:, 128:]
+        for index, flat in enumerate((flat0, flat1)):
+            values = flat[0 : CHAN * SHIFT, :].reshape(CHAN, SHIFT, 128)
+            out_ref[:, :, index * 128 : (index + 1) * 128] = values.astype(BF16)
+
+
+def own_path(keep, count, rest, halo, table, qkv, proj, gain_attn, gain_mlp, hidden, output):
+    _, columns, _ = rest.shape
+    half = HEADS * HEAD_PAD
     flat = pltpu.VMEM((256 * SHIFT, 128), F32)
-    turned = pltpu.VMEM((CHAN * WIN, 128), F32)
+    part = jax.ShapeDtypeStruct((CHAN, SHIFT, columns), BF16)
     return pl.pallas_call(
         own_kernel,
-        grid=(columns // per_step,),
-        in_specs=[SMEM, SMEM, block] + [VMEM] * 9,
-        out_specs=VMEM,
-        out_shape=jax.ShapeDtypeStruct((CHAN, WIN, columns), BF16),
+        in_specs=[SMEM, SMEM] + [VMEM] * 9,
+        out_specs=[VMEM] * 6,
+        out_shape=[
+            part,
+            part,
+            jax.ShapeDtypeStruct((2 * half, CHAN), BF16),
+            jax.ShapeDtypeStruct((CHAN, HEADS * PAIR), BF16),
+            jax.ShapeDtypeStruct((CHAN, half), BF16),
+            jax.ShapeDtypeStruct((HEADS, TOKENS, PAIR), F32),
+        ],
         scratch_shapes=[
             pltpu.SMEM((columns // WIN,), jnp.int32),
+            pltpu.VMEM((half, CHAN), BF16),
+            pltpu.VMEM((8, 256), F32),
+            pltpu.VMEM((8 * TOKENS, PAIR), F32),
             flat,
             flat,
             pltpu.VMEM((SHIFT, columns, CHAN), F32),
             pltpu.VMEM((WIN, columns, CHAN), BF16),
-            turned,
-            turned,
         ],
         cost_estimate=pl.CostEstimate(
             flops=20_000_000_000, bytes_accessed=3_000_000, transcendentals=2_000_000
         ),
         name="own_path",
-    )(keep, count, rest, halo, bias, gain_attn, wqv, wk, proj, gain_mlp, hidden, output)
+    )(keep, count, rest, in_vmem(halo), table, qkv, proj, gain_attn, gain_mlp, hidden, output)
 
 
 def spread_kernel(
@@ -398,7 +394,7 @@
     behind = lax.axis_index("band") >= TOKENS // 2
     codes = jnp.where(behind, pltpu.roll(codes, half, 1), codes)
     low, high = codes[0:1].astype(jnp.int32), codes[1:2].astype(jnp.int32)
-    chunk = 128
+    chunk = 256
     lane_out = iota((chunk, 128), 1)
     is_kind = (lane_out == 2 * TAIL + 4) | (lane_out == 2 * TAIL + 5)
     first = jnp.concatenate([got[:, 0:128], tails], axis=1)
@@ -439,16 +435,16 @@
             flops=1_200_000_000, bytes_accessed=1_200_000, transcendentals=0
         ),
         name="route",
-    )(got)
+    )(in_vmem(got))
 
 
 def work_kernel(got_ref, bias_ref, gain_ref, wqv_ref, wk_ref, proj_ref, out_ref, held, done):
     for part in range(held.shape[0]):
         values = got_ref[:, :, part * 128 : (part + 1) * 128].astype(F32)
         held[part] = values.reshape(TOKENS * CAP, 128)
-    pairs = 2
-
-    def two_slots(step, carry):
+    pairs = 8
+
+    def some_slots(step, carry):
         tokens, masks = [], []
         for index in range(pairs):
             slot = step * pairs + index
@@ -472,7 +468,7 @@
             done[rows, :] = own.T + dot(proj_ref[...], mixed[index])
         return carry
 
-    lax.fori_loop(0, CAP // pairs, two_slots, 0)
+    lax.fori_loop(0, CAP // pairs, some_slots, 0)
     out_ref[...] = done[...].reshape(CHAN, CAP, PAIR).astype(BF16)
 
 
@@ -490,7 +486,7 @@
             flops=8_000_000_000, bytes_accessed=2_000_000, transcendentals=1_000_000
         ),
         name="work_path",
-    )(got, bias, gain, wqv, wk, proj)
+    )(in_vmem(got), bias, gain, wqv, wk, proj)
 
 
 def from_behind(value, axis, steps):
@@ -518,27 +514,25 @@
     halo = from_behind(pixels[:, :SHIFT], "band", -1)
     outgoing, rest = spread(keep_mask, band_counts, plan_dest, plan_slot, pixels)
     gathered = lax.all_to_all(outgoing, "band", split_axis=0, concat_axis=0, tiled=True)
-    wqv, wk, proj, proj_turned, bias = prep(qkv_weight, proj_weight, bias_table.T)
-    finished = own_path(
+    sent, kept, wqv, wk, proj, bias = own_path(
         keep_mask,
         band_counts,
         rest,
         halo,
-        bias,
+        bias_table.T,
+        qkv_weight,
+        proj_weight,
         gain_attn,
-        wqv,
-        wk,
-        proj,
         gain_mlp,
         hidden_weight,
         output_weight.T,
     )
-    upper = from_behind(finished[:, :SHIFT], "band", 1)
+    upper = from_behind(sent, "band", 1)
     routed = route(gathered)
     incoming = lax.all_to_all(routed, "band", split_axis=0, concat_axis=0, tiled=True)
-    restored = jnp.concatenate([upper, finished[:, SHIFT:]], axis=1)
+    restored = jnp.concatenate([upper, kept], axis=1)
     restored = jnp.transpose(restored, (1, 2, 0))
-    work_tiles = work_path(incoming, bias, gain_attn, wqv, wk, proj_turned)
+    work_tiles = work_path(incoming, bias, gain_attn, wqv, wk, proj)
     work_tiles = jnp.transpose(work_tiles, (1, 2, 0))
     return (restored, work_tiles)
 

time: 97.4 us -> 86.3 us (0.89)
  Pallas kernels: 33 us -> 21.8 us
  local copies, waits for them, and re-layouts: 4.09 us -> 0.1 us
  waiting for transfers between devices: 24.3 us -> 27.1 us
  other arithmetic: 1.22 us -> 2.21 us
    pallas_call x2 -> x1, Pallas kernels: 19.5 us -> 11.5 us  [own_path(): pl.pallas_call(own_kernel, in_specs=[SMEM, SMEM] + [VMEM] * 9, out_specs=...]
    all_to_all x1, waiting for transfers between devices: 13.1 us -> 15.7 us  [shards(): lax.all_to_all(outgoing, 'band', split_axis=0, concat_axis=0, tiled=True)]
    unnamed x8 -> x2, local copies, waits for them, and re-layouts: 2.36 us -> 0.01 us
    pallas_call x1, Pallas kernels: 6.86 us -> 4.92 us  [work_path(): pl.pallas_call(work_kernel, in_specs=[VMEM] * 6, out_specs=VMEM, out_shap...]
    slice x1 -> x0, local copies, waits for them, and re-layouts: 1.63 us -> none  [shards(): upper = from_behind(finished[:, :SHIFT], 'band', 1)]
    pallas_call x1, Pallas kernels: 3.52 us -> 2.36 us  [route(): pl.pallas_call(route_kernel, in_specs=[VMEM], out_specs=VMEM, out_shape=j...]
    transpose x1, other arithmetic: 1.22 us -> 2.21 us  [shards(): restored = jnp.transpose(restored, (1, 2, 0))]
  transfers between devices with their start and end apart: 4 -> 4, of which waited for: 2 -> 2; matrix products, arithmetic and copies ran while one was open for 3% -> 3% of each run, Pallas kernels for 24% -> 16%
where the time goes in v4:
time: 86.3 us; the launch traced here: 85.2 us
  starting transfers between devices  32.7 us (38%)
  waiting for transfers between devices  27.1 us (31%)
  Pallas kernels  21.8 us (25%)
  other arithmetic  2.21 us (3%)
  between operations  1.32 us (2%)
    all_to_all x1, waiting for transfers between devices, shards(): lax.all_to_all(outgoing, 'band', split_axis=0, concat_axis=0, tiled=True)  15.7 us
    all_to_all x1, starting transfers between devices, shards(): lax.all_to_all(outgoing, 'band', split_axis=0, concat_axis=0, tiled=True)  15.2 us
    pallas_call x1, Pallas kernels, own_path(): pl.pallas_call(own_kernel, in_specs=[SMEM, SMEM] + [VMEM] * 9, out_specs=...  11.5 us
    ppermute x2, waiting for transfers between devices, from_behind(): return lax.ppermute(value, axis, pairs)  11.3 us
    ppermute x2, starting transfers between devices, from_behind(): return lax.ppermute(value, axis, pairs)  9.9 us
    all_to_all x1, starting transfers between devices, shards(): lax.all_to_all(routed, 'band', split_axis=0, concat_axis=0, tiled=True)  7.54 us
    pallas_call x1, Pallas kernels, work_path(): pl.pallas_call(work_kernel, in_specs=[VMEM] * 6, out_specs=VMEM, out_shap...  4.92 us
    pallas_call x1, Pallas kernels, spread(): pl.pallas_call(spread_kernel, in_specs=[SMEM] * 4 + [VMEM], out_specs=[VM...  3.06 us
  transfers between devices with their start and end apart: 4, of which 2 were waited for; matrix products, arithmetic and copies ran while one was open for 3% of the time, Pallas kernels for 16%

profile of v4, /device:TPU:1, one launch (start us, length us, event | category | flops | bytes accessed | tf_op | source)
XLA Modules:
  0.0 85.2 jit_solution(2294574441960726945)
XLA Ops:
  1.3 3.1 %spread.1 = (bf16[64,16,384]{2,1,0:T(8,128)(2,1)}, bf16[4,256,180]{2,1,0:T(8,128)(2,1)}) custom-call(s32[1,32]{1,0:T(1,128)} %keep_ref.3, s32[1]{0:T(128)S(6)} %copy.14.count_ref, s32[1,16]{1,0:T(1,128)} %dest_ref.1, s32[1,16]{1,0:T(1,128)} %slot_ref.1, bf16[180,8,256]{2,1,0:T(8,128)(2,1)} %bitcast.8), custom_call_target="tpu_custom_call" | custom-call | flops 500000000 | bytes 2000000 | tf_op jit(solution)/shard_map/spread/pallas_call | solution.py:368
  4.3 0.0 copy-start
  4.3 15.2 %all-to-all-start = ((bf16[64,16,384]{2,1,0:T(8,128)(2,1)}), bf16[64,16,384]{2,1,0:T(8,128)(2,1)S(1)}, u32[]{:S(2)}, u32[]{:S(2)}) async-start(bf16[64,16,384]{2,1,0:T(8,128)(2,1)} %get-tuple-element.13), calls=%async_computation | async-start | bytes 1572864 | tf_op jit(solution)/shard_map/all_to_all | solution.py:516
  19.6 0.0 copy-done
  19.6 0.1 slice.4
  19.7 7.1 %collective-permute-start = (bf16[180,4,256]{2,1,0:T(4,128)(2,1)S(1)}, bf16[180,4,256]{2,1,0:T(4,128)(2,1)S(1)}, u32[]{:S(2)}, u32[]{:S(2)}) collective-permute-start(bf16[180,4,256]{2,1,0:T(4,128)(2,1)S(1)} %slice.4), channel_id=1, source_target_pairs={{0,252},{4,0},{8,4},{12,8},{16,12},{20,16},{24,20},{28,24},{32,28}... | collective-permute-start | bytes 1105928 | tf_op jit(solution)/shard_map/ppermute | solution.py:495
  26.8 15.7 %all-to-all-done.got_ref = bf16[64,16,384]{2,1,0:T(8,128)(2,1)S(1)} async-done(((bf16[64,16,384]{2,1,0:T(8,128)(2,1)}), bf16[64,16,384]{2,1,0:T(8,128)(2,1)S(1)}, u32[]{:S(2)}, u32[]{:S(2)}) %all-to-all-start) | async-done | bytes 786464 | tf_op jit(solution)/shard_map/all_to_all | solution.py:516
  42.5 2.4 %route.1 = bf16[64,8,384]{2,1,0:T(8,128)(2,1)} custom-call(bf16[64,16,384]{2,1,0:T(8,128)(2,1)S(1)} %all-to-all-done.got_ref), custom_call_target="tpu_custom_call" | custom-call | flops 1200000000 | bytes 1200000 | tf_op jit(solution)/shard_map/route/pallas_call | solution.py:429
  44.9 7.5 %all-to-all-start.1 = ((bf16[64,8,384]{2,1,0:T(8,128)(2,1)}), bf16[64,8,384]{2,1,0:T(8,128)(2,1)S(1)}, u32[]{:S(2)}, u32[]{:S(2)}) async-start(bf16[64,8,384]{2,1,0:T(8,128)(2,1)} %route.1), calls=%async_computation.1 | async-start | bytes 786432 | tf_op jit(solution)/shard_map/all_to_all | solution.py:532
  52.4 0.0 collective-permute-done.halo_ref
  52.5 11.5 %own_path.1 = (bf16[180,4,256]{2,1,0:T(4,128)(2,1)}, bf16[180,4,256]{2,1,0:T(4,128)(2,1)}, bf16[384,180]{1,0:T(8,128)(2,1)}, bf16[180,768]{1,0:T(8,128)(2,1)}, b...) custom-call(s32[1,32]{1,0:T(1,128)} %keep_ref.3, s32[1]{0:T(128)S(6)} %copy.14.count_ref, ...), custom_call_target="tpu_custom_call" | custom-call | flops 20000000000 | bytes 3000000 | tf_op jit(solution)/shard_map/own_path/pallas_call | solution.py:290
  64.0 2.8 %collective-permute-start.1 = (bf16[180,4,256]{2,1,0:T(4,128)(2,1)}, bf16[180,4,256]{2,1,0:T(4,128)(2,1)S(1)}, u32[]{:S(2)}, u32[]{:S(2)}) collective-permute-start(bf16[180,4,256]{2,1,0:T(4,128)(2,1)} %get-tuple-element.11), channel_id=1, source_target_pairs={{0,4},{4,8},{8,12},{12,16},{16,20},{20,24},{24,28},{28,32},{32,36}... | collective-permute-start | bytes 1105928 | tf_op jit(solution)/shard_map/ppermute | solution.py:495
  66.7 11.3 %collective-permute-done.1 = bf16[180,4,256]{2,1,0:T(4,128)(2,1)S(1)} collective-permute-done((bf16[180,4,256]{2,1,0:T(4,128)(2,1)}, bf16[180,4,256]{2,1,0:T(4,128)(2,1)S(1)}, u32[]{:S(2)}, u32[]{:S(2)}) %collective-permute-start.1) | collective-permute-done | bytes 368672 | tf_op jit(solution)/shard_map/ppermute | solution.py:495
  78.1 2.2 %maximum_bitcast_fusion = bf16[8,256,180]{1,0,2:T(8,128)(2,1)} fusion(bf16[180,4,256]{2,1,0:T(4,128)(2,1)} %get-tuple-element.12, bf16[180,4,256]{2,1,0:T(4,128)(2,1)S(1)} %collective-permute-done.1), kind=kLoop, calls=%fused_computation | loop fusion | flops 1474560 | bytes 1474560 | tf_op jit(solution)/shard_map/transpose | solution.py:534
  80.3 0.0 all-to-all-done.1.got_ref
  80.3 4.9 %work_path.1 = bf16[180,8,128]{2,1,0:T(8,128)(2,1)} custom-call(bf16[64,8,384]{2,1,0:T(8,128)(2,1)S(1)} %all-to-all-done.1.got_ref, f32[6,64,128]{2,1,0:T(8,128)} %get-tuple-element.14.bias_ref, f32[1,180]{1,0:T(1,128)} %bitcast.14, bf16[384,180]{1,0:T(8,128)(2,1)} %get-tuple-element.15.wqv_ref, bf16[180,768]{1,0:T(8,128)(2,1)} %get-tuple-element.16.wk_ref, ...), custom_call_target="tpu_custom_call" | custom-call | flops 8000000000 | bytes 2000000 | tf_op jit(solution)/shard_map/work_path/pallas_call | solution.py:476
Async XLA Ops:
  4.3 15.2 %copy-start = (bf16[8,256,180]{1,0,2:T(8,128)(2,1)S(1)}, bf16[8,256,180]{1,0,2:T(8,128)(2,1)}, u32[]{:S(2)}) copy-start(bf16[8,256,180]{1,0,2:T(8,128)(2,1)} %param.12) | copy-start | bytes 2211844
  4.3 38.2 %all-to-all-start = ((bf16[64,16,384]{2,1,0:T(8,128)(2,1)}), bf16[64,16,384]{2,1,0:T(8,128)(2,1)S(1)}, u32[]{:S(2)}, u32[]{:S(2)}) async-start(bf16[64,16,384]{2,1,0:T(8,128)(2,1)} %get-tuple-element.13), calls=%async_computation | async-start | bytes 1572864 | tf_op jit(solution)/shard_map/all_to_all | solution.py:516
  19.7 32.7 %collective-permute-start = (bf16[180,4,256]{2,1,0:T(4,128)(2,1)S(1)}, bf16[180,4,256]{2,1,0:T(4,128)(2,1)S(1)}, u32[]{:S(2)}, u32[]{:S(2)}) collective-permute-start(bf16[180,4,256]{2,1,0:T(4,128)(2,1)S(1)} %slice.4), channel_id=1, source_target_pairs={{0,252},{4,0},{8,4},{12,8},{16,12},{20,16},{24,20},{28,24},{32,28}... | collective-permute-start | bytes 1105928 | tf_op jit(solution)/shard_map/ppermute | solution.py:495
  44.9 35.4 %all-to-all-start.1 = ((bf16[64,8,384]{2,1,0:T(8,128)(2,1)}), bf16[64,8,384]{2,1,0:T(8,128)(2,1)S(1)}, u32[]{:S(2)}, u32[]{:S(2)}) async-start(bf16[64,8,384]{2,1,0:T(8,128)(2,1)} %route.1), calls=%async_computation.1 | async-start | bytes 786432 | tf_op jit(solution)/shard_map/all_to_all | solution.py:532
  64.0 14.1 %collective-permute-start.1 = (bf16[180,4,256]{2,1,0:T(4,128)(2,1)}, bf16[180,4,256]{2,1,0:T(4,128)(2,1)S(1)}, u32[]{:S(2)}, u32[]{:S(2)}) collective-permute-start(bf16[180,4,256]{2,1,0:T(4,128)(2,1)} %get-tuple-element.11), channel_id=1, source_target_pairs={{0,4},{4,8},{8,12},{12,16},{16,20},{20,24},{24,28},{28,32},{32,36}... | collective-permute-start | bytes 1105928 | tf_op jit(solution)/shard_map/ppermute | solution.py:495

commit v5 on v4

--- a/solution.py
+++ b/solution.py
@@ -194,7 +194,7 @@
 def own_kernel(
     keep_ref,
     count_ref,
-    rest_ref,
+    pixels_ref,
     halo_ref,
     table_ref,
     qkv_ref,
@@ -215,10 +215,13 @@
     looked,
     flat0,
     flat1,
+    wide0,
+    wide1,
     lower_rows,
+    upper_rows,
     finished,
 ):
-    columns_all = rest_ref.shape[1]
+    columns_all = pixels_ref.shape[2]
     pairs = 8
     steps = columns_all // (pairs * TILE * WIN)
     row_flag = jnp.where(lax.axis_index("band") == lax.axis_size("band") - 1, 1.0, 0.0)
@@ -235,13 +238,17 @@
     for row in range(SHIFT):
         got = dot(pick, turned_rows((flat0, flat1), row, SHIFT), 1, 1)
         lower_rows[row] = got[:, :CHAN]
+    hold_channels(pixels_ref, (wide0, wide1))
+    for row in range(SHIFT):
+        got = dot(pick, turned_rows((wide0, wide1), SHIFT + row, WIN), 1, 1)
+        upper_rows[row] = got[:, :CHAN]
 
     def some_pairs(step, carry):
         tokens, masks = [], []
         for pair in range(pairs):
             start = pl.multiple_of((step * pairs + pair) * TILE * WIN, TILE * WIN)
             columns = pl.ds(start, TILE * WIN)
-            upper = rest_ref[:, columns, :].astype(F32)
+            upper = upper_rows[:, columns, :]
             lower = lower_rows[:, columns, :]
             for w in range(TILE):
                 for part in (upper, lower):
@@ -282,10 +289,12 @@
             out_ref[:, :, index * 128 : (index + 1) * 128] = values.astype(BF16)
 
 
-def own_path(keep, count, rest, halo, table, qkv, proj, gain_attn, gain_mlp, hidden, output):
-    _, columns, _ = rest.shape
+def own_path(keep, count, pixels, halo, table, qkv, proj, gain_attn, gain_mlp, hidden, output):
+    columns = pixels.shape[2]
     half = HEADS * HEAD_PAD
     flat = pltpu.VMEM((256 * SHIFT, 128), F32)
+    wide = pltpu.VMEM((256 * WIN, 128), F32)
+    rows = pltpu.VMEM((SHIFT, columns, CHAN), F32)
     part = jax.ShapeDtypeStruct((CHAN, SHIFT, columns), BF16)
     return pl.pallas_call(
         own_kernel,
@@ -294,10 +303,10 @@
         out_shape=[
             part,
             part,
-            jax.ShapeDtypeStruct((2 * half, CHAN), BF16),
-            jax.ShapeDtypeStruct((CHAN, HEADS * PAIR), BF16),
-            jax.ShapeDtypeStruct((CHAN, half), BF16),
-            jax.ShapeDtypeStruct((HEADS, TOKENS, PAIR), F32),
+            pltpu.VMEM((2 * half, CHAN), BF16),
+            pltpu.VMEM((CHAN, HEADS * PAIR), BF16),
+            pltpu.VMEM((CHAN, half), BF16),
+            pltpu.VMEM((HEADS, TOKENS, PAIR), F32),
         ],
         scratch_shapes=[
             pltpu.SMEM((columns // WIN,), jnp.int32),
@@ -306,18 +315,29 @@
             pltpu.VMEM((8 * TOKENS, PAIR), F32),
             flat,
             flat,
-            pltpu.VMEM((SHIFT, columns, CHAN), F32),
+            wide,
+            wide,
+            rows,
+            rows,
             pltpu.VMEM((WIN, columns, CHAN), BF16),
         ],
         cost_estimate=pl.CostEstimate(
             flops=20_000_000_000, bytes_accessed=3_000_000, transcendentals=2_000_000
         ),
         name="own_path",
-    )(keep, count, rest, in_vmem(halo), table, qkv, proj, gain_attn, gain_mlp, hidden, output)
+    )(keep, count, pixels, in_vmem(halo), table, qkv, proj, gain_attn, gain_mlp, hidden, output)
 
 
 def spread_kernel(
-    keep_ref, count_ref, dest_ref, slot_ref, pixels_ref, out_ref, rest_ref, flat0, flat1
+    keep_ref,
+    count_ref,
+    dest_ref,
+    slot_ref,
+    pixels_ref,
+    out_ref,
+    top_ref,
+    flat0,
+    flat1,
 ):
     _, rows, columns = pixels_ref.shape
     windows = columns // WIN
@@ -334,23 +354,20 @@
         tile = jnp.maximum(position, 0) >> 1
         slot = slot_ref[0, tile]
         placed = (keep == 1) & (position < count_ref[0]) & (slot < CAP)
-        dest = jnp.where(placed, dest_ref[0, tile], bands).astype(F32)
+        dest = jnp.where(placed, bands - 1 - dest_ref[0, tile], bands).astype(F32)
         place = jnp.where(placed, slot * TILE + (position & 1), 0).astype(F32)
         first = 2 * (w // half)
         here = row == w % half
         codes = jnp.where(here & (lane == first), dest, codes)
         codes = jnp.where(here & (lane == first + 1), place, codes)
 
+    top_ref[...] = pixels_ref[:, 0:SHIFT, :]
     hold_channels(pixels_ref, (flat0, flat1))
     out_row = iota((columns, columns), 0)
     wanted = ((out_row & (windows - 1)) * WIN + (out_row >> 5) + SHIFT) & (columns - 1)
     group = (wanted == iota((columns, columns), 1)).astype(F32).astype(BF16)
-    pick = roll_pick(columns)
     for r in range(rows):
-        line = turned_rows((flat0, flat1), r, rows)
-        if r >= SHIFT:
-            rest_ref[r - SHIFT] = dot(pick, line, 1, 1)[:, :CHAN].astype(BF16)
-        got = dot(group, line, 1, 1)
+        got = dot(group, turned_rows((flat0, flat1), r, rows), 1, 1)
         for cu in range(WIN):
             token = (r + SHIFT) % rows * WIN + cu
             low = got[cu * windows : cu * windows + half]
@@ -362,7 +379,7 @@
 
 
 def spread(keep, count, dest, slot, pixels):
-    _, rows, columns = pixels.shape
+    channels, rows, columns = pixels.shape
     half = columns // WIN // 2
     flat = pltpu.VMEM((256 * rows, 128), F32)
     return pl.pallas_call(
@@ -371,7 +388,7 @@
         out_specs=[VMEM] * 2,
         out_shape=[
             jax.ShapeDtypeStruct((TOKENS, half, 384), BF16),
-            jax.ShapeDtypeStruct((SHIFT, columns, CHAN), BF16),
+            jax.ShapeDtypeStruct((channels, SHIFT, columns), BF16),
         ],
         scratch_shapes=[flat, flat],
         cost_estimate=pl.CostEstimate(
@@ -391,8 +408,8 @@
     lane = iota((8, 128), 1) - 2 * TAIL - 2 * row
     pick = jnp.where(row < 2, jnp.where(lane == 0, 16.0, jnp.where(lane == 1, 1.0, 0.0)), 0.0)
     codes = dot(pick.astype(BF16), tails, 1, 1)
-    behind = lax.axis_index("band") >= TOKENS // 2
-    codes = jnp.where(behind, pltpu.roll(codes, half, 1), codes)
+    behind = bands - 1 - lax.axis_index("band") >= TOKENS // 2
+    codes = jnp.where(behind, pltpu.roll(codes, sources - half, 1), codes)
     low, high = codes[0:1].astype(jnp.int32), codes[1:2].astype(jnp.int32)
     chunk = 256
     lane_out = iota((chunk, 128), 1)
@@ -486,13 +503,20 @@
             flops=8_000_000_000, bytes_accessed=2_000_000, transcendentals=1_000_000
         ),
         name="work_path",
-    )(in_vmem(got), bias, gain, wqv, wk, proj)
+    )(in_vmem(got), in_vmem(bias), gain, in_vmem(wqv), in_vmem(wk), in_vmem(proj))
 
 
 def from_behind(value, axis, steps):
     count = lax.axis_size(axis)
     pairs = [(source, (source + steps) % count) for source in range(count)]
     return lax.ppermute(value, axis, pairs)
+
+
+def exchange(value):
+    order = tuple(range(lax.axis_size("band")))[::-1]
+    return lax.all_to_all(
+        value, "band", split_axis=0, concat_axis=0, axis_index_groups=[order], tiled=True
+    )
 
 
 def shards(
@@ -511,13 +535,13 @@
 ):
     gain_attn, gain_mlp = gain_attn[None], gain_mlp[None]
     pixels = jnp.transpose(pixels, (2, 0, 1))
-    halo = from_behind(pixels[:, :SHIFT], "band", -1)
-    outgoing, rest = spread(keep_mask, band_counts, plan_dest, plan_slot, pixels)
-    gathered = lax.all_to_all(outgoing, "band", split_axis=0, concat_axis=0, tiled=True)
+    outgoing, top = spread(keep_mask, band_counts, plan_dest, plan_slot, pixels)
+    halo = from_behind(top, "band", -1)
+    gathered = exchange(outgoing)
     sent, kept, wqv, wk, proj, bias = own_path(
         keep_mask,
         band_counts,
-        rest,
+        pixels,
         halo,
         bias_table.T,
         qkv_weight,
@@ -529,7 +553,7 @@
     )
     upper = from_behind(sent, "band", 1)
     routed = route(gathered)
-    incoming = lax.all_to_all(routed, "band", split_axis=0, concat_axis=0, tiled=True)
+    incoming = exchange(routed)
     restored = jnp.concatenate([upper, kept], axis=1)
     restored = jnp.transpose(restored, (1, 2, 0))
     work_tiles = work_path(incoming, bias, gain_attn, wqv, wk, proj)

time: 86.3 us -> 87.2 us (1.010)
  waiting for transfers between devices: 27.1 us -> 32.1 us
  starting transfers between devices: 32.7 us -> 28.4 us
    ppermute x2, starting transfers between devices: 9.9 us -> 0.49 us  [from_behind(): return lax.ppermute(value, axis, pairs)]
    all_to_all x2, starting transfers between devices: 22.8 us -> 27.9 us  [exchange(): lax.all_to_all(value, 'band', split_axis=0, concat_axis=0, axis_index_gro...]
    all_to_all x2, waiting for transfers between devices: 15.7 us -> 18.2 us  [exchange(): lax.all_to_all(value, 'band', split_axis=0, concat_axis=0, axis_index_gro...]
    ppermute x2, waiting for transfers between devices: 11.3 us -> 13.9 us  [from_behind(): return lax.ppermute(value, axis, pairs)]
  transfers between devices with their start and end apart: 4 -> 4, of which waited for: 2 -> 2; matrix products, arithmetic and copies ran while one was open for 3% -> 3% of each run, Pallas kernels for 16% -> 17%
where the time goes in v5:
time: 87.2 us; the launch traced here: 85.8 us
  waiting for transfers between devices  32.1 us (37%)
  starting transfers between devices  28.4 us (33%)
  Pallas kernels  21.8 us (25%)
  other arithmetic  2.21 us (3%)
  between operations  1.31 us (2%)
    all_to_all x2, starting transfers between devices, exchange(): lax.all_to_all(value, 'band', split_axis=0, concat_axis=0, axis_index_gro...  27.9 us
    all_to_all x2, waiting for transfers between devices, exchange(): lax.all_to_all(value, 'band', split_axis=0, concat_axis=0, axis_index_gro...  18.2 us
    ppermute x2, waiting for transfers between devices, from_behind(): return lax.ppermute(value, axis, pairs)  13.9 us
    pallas_call x1, Pallas kernels, own_path(): pl.pallas_call(own_kernel, in_specs=[SMEM, SMEM] + [VMEM] * 9, out_specs=...  12 us
    pallas_call x1, Pallas kernels, work_path(): pl.pallas_call(work_kernel, in_specs=[VMEM] * 6, out_specs=VMEM, out_shap...  4.49 us
    pallas_call x1, Pallas kernels, spread(): pl.pallas_call(spread_kernel, in_specs=[SMEM] * 4 + [VMEM], out_specs=[VM...  2.99 us
    pallas_call x1, Pallas kernels, route(): pl.pallas_call(route_kernel, in_specs=[VMEM], out_specs=VMEM, out_shape=j...  2.33 us
    transpose x1, other arithmetic, shards(): restored = jnp.transpose(restored, (1, 2, 0))  2.21 us
  transfers between devices with their start and end apart: 4, of which 2 were waited for; matrix products, arithmetic and copies ran while one was open for 3% of the time, Pallas kernels for 17%

profile of v5, /device:TPU:1, one launch (start us, length us, event | category | flops | bytes accessed | tf_op | source)
XLA Modules:
  0.0 85.8 jit_solution(7602205155149080181)
XLA Ops:
  1.3 3.0 %spread.1 = (bf16[64,16,384]{2,1,0:T(8,128)(2,1)}, bf16[180,4,256]{2,1,0:T(4,128)(2,1)}) custom-call(s32[1,32]{1,0:T(1,128)} %keep_ref.3, s32[1]{0:T(128)S(6)} %copy.14.count_ref, s32[1,16]{1,0:T(1,128)} %dest_ref.1, s32[1,16]{1,0:T(1,128)} %slot_ref.1, bf16[180,8,256]{2,1,0:T(8,128)(2,1)} %bitcast.8), custom_call_target="tpu_custom_call" | custom-call | flops 500000000 | bytes 2000000 | tf_op jit(solution)/shard_map/spread/pallas_call | solution.py:385
  4.3 0.0 copy-start
  4.3 16.0 %all-to-all-start = ((bf16[64,16,384]{2,1,0:T(8,128)(2,1)}), bf16[64,16,384]{2,1,0:T(8,128)(2,1)S(1)}, u32[]{:S(2)}, u32[]{:S(2)}) async-start(bf16[64,16,384]{2,1,0:T(8,128)(2,1)} %get-tuple-element.13), calls=%async_computation | async-start | bytes 1572864 | tf_op jit(solution)/shard_map/all_to_all | solution.py:517
  20.2 0.0 copy-done
  20.3 0.2 collective-permute-start
  20.5 18.2 %all-to-all-done.got_ref = bf16[64,16,384]{2,1,0:T(8,128)(2,1)S(1)} async-done(((bf16[64,16,384]{2,1,0:T(8,128)(2,1)}), bf16[64,16,384]{2,1,0:T(8,128)(2,1)S(1)}, u32[]{:S(2)}, u32[]{:S(2)}) %all-to-all-start) | async-done | bytes 786464 | tf_op jit(solution)/shard_map/all_to_all | solution.py:517
  38.7 2.3 %route.1 = bf16[64,8,384]{2,1,0:T(8,128)(2,1)} custom-call(bf16[64,16,384]{2,1,0:T(8,128)(2,1)S(1)} %all-to-all-done.got_ref), custom_call_target="tpu_custom_call" | custom-call | flops 1200000000 | bytes 1200000 | tf_op jit(solution)/shard_map/route/pallas_call | solution.py:446
  41.0 11.9 %all-to-all-start.1 = ((bf16[64,8,384]{2,1,0:T(8,128)(2,1)}), bf16[64,8,384]{2,1,0:T(8,128)(2,1)S(1)}, u32[]{:S(2)}, u32[]{:S(2)}) async-start(bf16[64,8,384]{2,1,0:T(8,128)(2,1)} %route.1), calls=%async_computation.1 | async-start | bytes 786432 | tf_op jit(solution)/shard_map/all_to_all | solution.py:517
  52.9 0.0 collective-permute-done.halo_ref
  53.0 12.0 %own_path.1 = (bf16[180,4,256]{2,1,0:T(4,128)(2,1)}, bf16[180,4,256]{2,1,0:T(4,128)(2,1)}, bf16[384,180]{1,0:T(8,128)(2,1)S(1)}, bf16[180,768]{1,0:T(8,128)(2,1)...) custom-call(s32[1,32]{1,0:T(1,128)} %keep_ref.3, s32[1]{0:T(128)S(6)} %copy.14.count_ref, ...), custom_call_target="tpu_custom_call" | custom-call | flops 20000000000 | bytes 3000000 | tf_op jit(solution)/shard_map/own_path/pallas_call | solution.py:299
  64.9 0.3 collective-permute-start.1
  65.2 13.9 %collective-permute-done.1 = bf16[180,4,256]{2,1,0:T(4,128)(2,1)S(1)} collective-permute-done((bf16[180,4,256]{2,1,0:T(4,128)(2,1)}, bf16[180,4,256]{2,1,0:T(4,128)(2,1)S(1)}, u32[]{:S(2)}, u32[]{:S(2)}) %collective-permute-start.1) | collective-permute-done | bytes 368672 | tf_op jit(solution)/shard_map/ppermute | solution.py:512
  79.1 2.2 %maximum_bitcast_fusion = bf16[8,256,180]{1,0,2:T(8,128)(2,1)} fusion(bf16[180,4,256]{2,1,0:T(4,128)(2,1)} %get-tuple-element.12, bf16[180,4,256]{2,1,0:T(4,128)(2,1)S(1)} %collective-permute-done.1), kind=kLoop, calls=%fused_computation | loop fusion | flops 1474560 | bytes 1474560 | tf_op jit(solution)/shard_map/transpose | solution.py:558
  81.3 0.0 all-to-all-done.1.got_ref
  81.3 4.5 %work_path.1 = bf16[180,8,128]{2,1,0:T(8,128)(2,1)} custom-call(bf16[64,8,384]{2,1,0:T(8,128)(2,1)S(1)} %all-to-all-done.1.got_ref, f32[6,64,128]{2,1,0:T(8,128)S(1)} %get-tuple-element.14.bias_ref, f32[1,180]{1,0:T(1,128)} %bitcast.14, bf16[384,180]{1,0:T(8,128)(2,1)S(1)} %get-tuple-element.15.wqv_ref, bf16[180,768]{1,0:T(8,128)(2,1)S(1)} %get-tuple-element.16.wk_ref, ...), custom_call_target="tpu_custom_call" | custom-call | flops 8000000000 | bytes 2000000 | tf_op jit(solution)/shard_map/work_path/pallas_call | solution.py:493
Async XLA Ops:
  4.3 16.0 %copy-start = (bf16[180,4,256]{2,1,0:T(4,128)(2,1)S(1)}, bf16[180,4,256]{2,1,0:T(4,128)(2,1)}, u32[]{:S(2)}) copy-start(bf16[180,4,256]{2,1,0:T(4,128)(2,1)} %get-tuple-element.10) | copy-start | bytes 1105924
  4.3 34.4 %all-to-all-start = ((bf16[64,16,384]{2,1,0:T(8,128)(2,1)}), bf16[64,16,384]{2,1,0:T(8,128)(2,1)S(1)}, u32[]{:S(2)}, u32[]{:S(2)}) async-start(bf16[64,16,384]{2,1,0:T(8,128)(2,1)} %get-tuple-element.13), calls=%async_computation | async-start | bytes 1572864 | tf_op jit(solution)/shard_map/all_to_all | solution.py:517
  20.3 32.7 %collective-permute-start = (bf16[180,4,256]{2,1,0:T(4,128)(2,1)S(1)}, bf16[180,4,256]{2,1,0:T(4,128)(2,1)S(1)}, u32[]{:S(2)}, u32[]{:S(2)}) collective-permute-start(bf16[180,4,256]{2,1,0:T(4,128)(2,1)S(1)} %copy-done), channel_id=1, source_target_pairs={{0,252},{4,0},{8,4},{12,8},{16,12},{20,16},{24,20},{28,24},{32,28}... | collective-permute-start | bytes 1105928 | tf_op jit(solution)/shard_map/ppermute | solution.py:512
  41.0 40.2 %all-to-all-start.1 = ((bf16[64,8,384]{2,1,0:T(8,128)(2,1)}), bf16[64,8,384]{2,1,0:T(8,128)(2,1)S(1)}, u32[]{:S(2)}, u32[]{:S(2)}) async-start(bf16[64,8,384]{2,1,0:T(8,128)(2,1)} %route.1), calls=%async_computation.1 | async-start | bytes 786432 | tf_op jit(solution)/shard_map/all_to_all | solution.py:517
  64.9 14.1 %collective-permute-start.1 = (bf16[180,4,256]{2,1,0:T(4,128)(2,1)}, bf16[180,4,256]{2,1,0:T(4,128)(2,1)S(1)}, u32[]{:S(2)}, u32[]{:S(2)}) collective-permute-start(bf16[180,4,256]{2,1,0:T(4,128)(2,1)} %get-tuple-element.11), channel_id=1, source_target_pairs={{0,4},{4,8},{8,12},{12,16},{16,20},{20,24},{24,28},{28,32},{32,36}... | collective-permute-start | bytes 1105928 | tf_op jit(solution)/shard_map/ppermute | solution.py:512

commit v6 on v5

--- a/solution.py
+++ b/solution.py
@@ -192,8 +192,6 @@
 
 
 def own_kernel(
-    keep_ref,
-    count_ref,
     pixels_ref,
     halo_ref,
     table_ref,
@@ -209,7 +207,6 @@
     wk_ref,
     turned_ref,
     bias_ref,
-    active,
     padded_proj,
     padded_table,
     looked,
@@ -219,29 +216,25 @@
     wide1,
     lower_rows,
     upper_rows,
+    marks,
     finished,
 ):
     columns_all = pixels_ref.shape[2]
     pairs = 8
     steps = columns_all // (pairs * TILE * WIN)
-    row_flag = jnp.where(lax.axis_index("band") == lax.axis_size("band") - 1, 1.0, 0.0)
-
-    position = jnp.int32(-1)
-    for w in range(keep_ref.shape[1]):
-        keep = keep_ref[0, w]
-        position = position + keep
-        active[w] = jnp.where((keep == 1) & (position < count_ref[0]), 1, 0)
+    row_flag = jnp.where(lax.axis_index("band") == 0, 1.0, 0.0)
     pad_weights(qkv_ref, proj_ref, wqv_ref, wk_ref, padded_proj, turned_ref)
     spread_bias(table_ref, bias_ref, padded_table, looked)
     hold_channels(halo_ref, (flat0, flat1))
+    hold_channels(pixels_ref, (wide0, wide1))
     pick = roll_pick(columns_all)
     for row in range(SHIFT):
         got = dot(pick, turned_rows((flat0, flat1), row, SHIFT), 1, 1)
+        upper_rows[row] = got[:, :CHAN]
+        if row == 0:
+            marks[...] = got[:, 128:]
+        got = dot(pick, turned_rows((wide0, wide1), row, WIN), 1, 1)
         lower_rows[row] = got[:, :CHAN]
-    hold_channels(pixels_ref, (wide0, wide1))
-    for row in range(SHIFT):
-        got = dot(pick, turned_rows((wide0, wide1), SHIFT + row, WIN), 1, 1)
-        upper_rows[row] = got[:, :CHAN]
 
     def some_pairs(step, carry):
         tokens, masks = [], []
@@ -268,9 +261,9 @@
             kept = []
             for w in range(TILE):
                 at = pair * TILE + w
-                on = active[step * pairs * TILE + at]
                 rows = slice(at * TOKENS, (at + 1) * TOKENS)
-                kept.append(jnp.where(on == 1, done[rows], x[rows]).reshape(WIN, WIN, CHAN))
+                on = marks[pl.ds(start + w * WIN, WIN), :][0:1, TAIL : TAIL + 1] > 0.5
+                kept.append(jnp.where(on, done[rows], x[rows]).reshape(WIN, WIN, CHAN))
             kept = jnp.concatenate(kept, axis=1).astype(BF16)
             finished[:, pl.ds(start, TILE * WIN), :] = kept
         return carry
@@ -278,7 +271,7 @@
     lax.fori_loop(0, steps, some_pairs, 0)
 
     same = (iota((CHAN, CHAN), 0) == iota((CHAN, CHAN), 1)).astype(F32).astype(BF16)
-    for first, out_ref in ((0, kept_ref), (SHIFT, sent_ref)):
+    for first, out_ref in ((0, sent_ref), (SHIFT, kept_ref)):
         for row in range(SHIFT):
             got = pltpu.roll(dot(same, finished[first + row], 1, 1), SHIFT, 1)
             rows = pl.ds(row, CHAN, stride=SHIFT)
@@ -289,7 +282,7 @@
             out_ref[:, :, index * 128 : (index + 1) * 128] = values.astype(BF16)
 
 
-def own_path(keep, count, pixels, halo, table, qkv, proj, gain_attn, gain_mlp, hidden, output):
+def own_path(pixels, halo, table, qkv, proj, gain_attn, gain_mlp, hidden, output):
     columns = pixels.shape[2]
     half = HEADS * HEAD_PAD
     flat = pltpu.VMEM((256 * SHIFT, 128), F32)
@@ -298,7 +291,7 @@
     part = jax.ShapeDtypeStruct((CHAN, SHIFT, columns), BF16)
     return pl.pallas_call(
         own_kernel,
-        in_specs=[SMEM, SMEM] + [VMEM] * 9,
+        in_specs=[VMEM] * 9,
         out_specs=[VMEM] * 6,
         out_shape=[
             part,
@@ -309,7 +302,6 @@
             pltpu.VMEM((HEADS, TOKENS, PAIR), F32),
         ],
         scratch_shapes=[
-            pltpu.SMEM((columns // WIN,), jnp.int32),
             pltpu.VMEM((half, CHAN), BF16),
             pltpu.VMEM((8, 256), F32),
             pltpu.VMEM((8 * TOKENS, PAIR), F32),
@@ -319,13 +311,14 @@
             wide,
             rows,
             rows,
+            pltpu.VMEM((columns, 128), F32),
             pltpu.VMEM((WIN, columns, CHAN), BF16),
         ],
         cost_estimate=pl.CostEstimate(
             flops=20_000_000_000, bytes_accessed=3_000_000, transcendentals=2_000_000
         ),
         name="own_path",
-    )(keep, count, pixels, in_vmem(halo), table, qkv, proj, gain_attn, gain_mlp, hidden, output)
+    )(pixels, in_vmem(halo), table, qkv, proj, gain_attn, gain_mlp, hidden, output)
 
 
 def spread_kernel(
@@ -335,11 +328,11 @@
     slot_ref,
     pixels_ref,
     out_ref,
-    top_ref,
+    edge_ref,
     flat0,
     flat1,
 ):
-    _, rows, columns = pixels_ref.shape
+    channels, rows, columns = pixels_ref.shape
     windows = columns // WIN
     half = windows // 2
     bands = lax.axis_size("band")
@@ -347,13 +340,17 @@
     row, lane = iota((half, 128), 0), iota((half, 128), 1) - 2 * TAIL
     codes = jnp.where((lane == 4) | (lane == 6), last_band, 0.0)
     codes = jnp.where((lane == 7) & (row == half - 1), 1.0, codes)
+    window_of = ((iota((SHIFT, columns), 1) - SHIFT) & (columns - 1)) >> 3
+    running = jnp.zeros((SHIFT, columns), F32)
     position = jnp.int32(-1)
     for w in range(windows):
         keep = keep_ref[0, w]
         position = position + keep
         tile = jnp.maximum(position, 0) >> 1
         slot = slot_ref[0, tile]
-        placed = (keep == 1) & (position < count_ref[0]) & (slot < CAP)
+        active = (keep == 1) & (position < count_ref[0])
+        running = jnp.where(window_of == w, jnp.where(active, 1.0, 0.0), running)
+        placed = active & (slot < CAP)
         dest = jnp.where(placed, bands - 1 - dest_ref[0, tile], bands).astype(F32)
         place = jnp.where(placed, slot * TILE + (position & 1), 0).astype(F32)
         first = 2 * (w // half)
@@ -361,7 +358,10 @@
         codes = jnp.where(here & (lane == first), dest, codes)
         codes = jnp.where(here & (lane == first + 1), place, codes)
 
-    top_ref[...] = pixels_ref[:, 0:SHIFT, :]
+    edge_ref[0:channels] = pixels_ref[:, SHIFT:, :]
+    edge_ref[channels] = running.astype(BF16)
+    extra = edge_ref.shape[0] - channels - 1
+    edge_ref[channels + 1 :] = jnp.zeros((extra, SHIFT, columns), BF16)
     hold_channels(pixels_ref, (flat0, flat1))
     out_row = iota((columns, columns), 0)
     wanted = ((out_row & (windows - 1)) * WIN + (out_row >> 5) + SHIFT) & (columns - 1)
@@ -388,7 +388,7 @@
         out_specs=[VMEM] * 2,
         out_shape=[
             jax.ShapeDtypeStruct((TOKENS, half, 384), BF16),
-            jax.ShapeDtypeStruct((channels, SHIFT, columns), BF16),
+            jax.ShapeDtypeStruct((channels + 4, SHIFT, columns), BF16),
         ],
         scratch_shapes=[flat, flat],
         cost_estimate=pl.CostEstimate(
@@ -535,12 +535,10 @@
 ):
     gain_attn, gain_mlp = gain_attn[None], gain_mlp[None]
     pixels = jnp.transpose(pixels, (2, 0, 1))
-    outgoing, top = spread(keep_mask, band_counts, plan_dest, plan_slot, pixels)
-    halo = from_behind(top, "band", -1)
+    outgoing, edge = spread(keep_mask, band_counts, plan_dest, plan_slot, pixels)
+    halo = from_behind(edge, "band", 1)
     gathered = exchange(outgoing)
     sent, kept, wqv, wk, proj, bias = own_path(
-        keep_mask,
-        band_counts,
         pixels,
         halo,
         bias_table.T,
@@ -551,10 +549,10 @@
         hidden_weight,
         output_weight.T,
     )
-    upper = from_behind(sent, "band", 1)
+    lower = from_behind(sent, "band", -1)
     routed = route(gathered)
     incoming = exchange(routed)
-    restored = jnp.concatenate([upper, kept], axis=1)
+    restored = jnp.concatenate([kept, lower], axis=1)
     restored = jnp.transpose(restored, (1, 2, 0))
     work_tiles = work_path(incoming, bias, gain_attn, wqv, wk, proj)
     work_tiles = jnp.transpose(work_tiles, (1, 2, 0))

time: 87.2 us -> 83.3 us (0.955)
  the two profiles are of different devices: /device:TPU:1 before, /device:TPU:8 now
where the time goes in v6:
time: 83.3 us; the launch traced here: 82.9 us
  waiting for transfers between devices  30.1 us (36%)
  starting transfers between devices  27.3 us (33%)
  Pallas kernels  21.9 us (26%)
  other arithmetic  2.21 us (3%)
  between operations  1.31 us (2%)
    all_to_all x2, starting transfers between devices, exchange(): lax.all_to_all(value, 'band', split_axis=0, concat_axis=0, axis_index_gro...  26.5 us
    all_to_all x2, waiting for transfers between devices, exchange(): lax.all_to_all(value, 'band', split_axis=0, concat_axis=0, axis_index_gro...  20 us
    pallas_call x1, Pallas kernels, own_path(): pl.pallas_call(own_kernel, in_specs=[VMEM] * 9, out_specs=[VMEM] * 6, out...  12.1 us
    ppermute x2, waiting for transfers between devices, from_behind(): return lax.ppermute(value, axis, pairs)  10.1 us
    pallas_call x1, Pallas kernels, work_path(): pl.pallas_call(work_kernel, in_specs=[VMEM] * 6, out_specs=VMEM, out_shap...  4.48 us
    pallas_call x1, Pallas kernels, spread(): pl.pallas_call(spread_kernel, in_specs=[SMEM] * 4 + [VMEM], out_specs=[VM...  3.02 us
    pallas_call x1, Pallas kernels, route(): pl.pallas_call(route_kernel, in_specs=[VMEM], out_specs=VMEM, out_shape=j...  2.32 us
    transpose x1, other arithmetic, shards(): restored = jnp.transpose(restored, (1, 2, 0))  2.21 us
  transfers between devices with their start and end apart: 4, of which 2 were waited for; matrix products, arithmetic and copies ran while one was open for 3% of the time, Pallas kernels for 17%

profile of v6, /device:TPU:8, one launch (start us, length us, event | category | flops | bytes accessed | tf_op | source)
XLA Modules:
  0.0 82.9 jit_solution(17041129354457899671)
XLA Ops:
  1.3 3.0 %spread.1 = (bf16[64,16,384]{2,1,0:T(8,128)(2,1)}, bf16[184,4,256]{2,1,0:T(4,128)(2,1)}) custom-call(s32[1,32]{1,0:T(1,128)} %keep_ref.1, s32[1]{0:T(128)S(6)} %copy.14.count_ref, s32[1,16]{1,0:T(1,128)} %dest_ref.1, s32[1,16]{1,0:T(1,128)} %slot_ref.1, bf16[180,8,256]{2,1,0:T(8,128)(2,1)} %bitcast.8), custom_call_target="tpu_custom_call" | custom-call | flops 500000000 | bytes 2000000 | tf_op jit(solution)/shard_map/spread/pallas_call | solution.py:385
  4.3 0.0 copy-start
  4.3 15.5 %all-to-all-start = ((bf16[64,16,384]{2,1,0:T(8,128)(2,1)}), bf16[64,16,384]{2,1,0:T(8,128)(2,1)S(1)}, u32[]{:S(2)}, u32[]{:S(2)}) async-start(bf16[64,16,384]{2,1,0:T(8,128)(2,1)} %get-tuple-element.13), calls=%async_computation | async-start | bytes 1572864 | tf_op jit(solution)/shard_map/all_to_all | solution.py:517
  19.8 0.0 copy-done
  19.8 0.6 collective-permute-start
  20.4 20.0 %all-to-all-done.got_ref = bf16[64,16,384]{2,1,0:T(8,128)(2,1)S(1)} async-done(((bf16[64,16,384]{2,1,0:T(8,128)(2,1)}), bf16[64,16,384]{2,1,0:T(8,128)(2,1)S(1)}, u32[]{:S(2)}, u32[]{:S(2)}) %all-to-all-start) | async-done | bytes 786464 | tf_op jit(solution)/shard_map/all_to_all | solution.py:517
  40.4 2.3 %route.1 = bf16[64,8,384]{2,1,0:T(8,128)(2,1)} custom-call(bf16[64,16,384]{2,1,0:T(8,128)(2,1)S(1)} %all-to-all-done.got_ref), custom_call_target="tpu_custom_call" | custom-call | flops 1200000000 | bytes 1200000 | tf_op jit(solution)/shard_map/route/pallas_call | solution.py:446
  42.8 11.1 %all-to-all-start.1 = ((bf16[64,8,384]{2,1,0:T(8,128)(2,1)}), bf16[64,8,384]{2,1,0:T(8,128)(2,1)S(1)}, u32[]{:S(2)}, u32[]{:S(2)}) async-start(bf16[64,8,384]{2,1,0:T(8,128)(2,1)} %route.1), calls=%async_computation.1 | async-start | bytes 786432 | tf_op jit(solution)/shard_map/all_to_all | solution.py:517
  53.8 0.0 collective-permute-done.halo_ref
  53.9 12.1 %own_path.1 = (bf16[180,4,256]{2,1,0:T(4,128)(2,1)}, bf16[180,4,256]{2,1,0:T(4,128)(2,1)}, bf16[384,180]{1,0:T(8,128)(2,1)S(1)}, bf16[180,768]{1,0:T(8,128)(2,1)...) custom-call(bf16[180,8,256]{2,1,0:T(8,128)(2,1)} %bitcast.9, ...), custom_call_target="tpu_custom_call" | custom-call | flops 20000000000 | bytes 3000000 | tf_op jit(solution)/shard_map/own_path/pallas_call | solution.py:292
  66.0 0.1 collective-permute-start.1
  66.1 10.1 %collective-permute-done.1 = bf16[180,4,256]{2,1,0:T(4,128)(2,1)S(1)} collective-permute-done((bf16[180,4,256]{2,1,0:T(4,128)(2,1)}, bf16[180,4,256]{2,1,0:T(4,128)(2,1)S(1)}, u32[]{:S(2)}, u32[]{:S(2)}) %collective-permute-start.1) | collective-permute-done | bytes 368672 | tf_op jit(solution)/shard_map/ppermute | solution.py:512
  76.2 2.2 %maximum_bitcast_fusion = bf16[8,256,180]{1,0,2:T(8,128)(2,1)} fusion(bf16[180,4,256]{2,1,0:T(4,128)(2,1)S(1)} %collective-permute-done.1, bf16[180,4,256]{2,1,0:T(4,128)(2,1)} %get-tuple-element.11), kind=kLoop, calls=%fused_computation | loop fusion | flops 1474560 | bytes 1474560 | tf_op jit(solution)/shard_map/transpose | solution.py:556
  78.4 0.0 all-to-all-done.1.got_ref
  78.4 4.5 %work_path.1 = bf16[180,8,128]{2,1,0:T(8,128)(2,1)} custom-call(bf16[64,8,384]{2,1,0:T(8,128)(2,1)S(1)} %all-to-all-done.1.got_ref, f32[6,64,128]{2,1,0:T(8,128)S(1)} %get-tuple-element.14.bias_ref, f32[1,180]{1,0:T(1,128)} %bitcast.14, bf16[384,180]{1,0:T(8,128)(2,1)S(1)} %get-tuple-element.15.wqv_ref, bf16[180,768]{1,0:T(8,128)(2,1)S(1)} %get-tuple-element.16.wk_ref, ...), custom_call_target="tpu_custom_call" | custom-call | flops 8000000000 | bytes 2000000 | tf_op jit(solution)/shard_map/work_path/pallas_call | solution.py:493
Async XLA Ops:
  4.3 15.5 %copy-start = (bf16[184,4,256]{2,1,0:T(4,128)(2,1)S(1)}, bf16[184,4,256]{2,1,0:T(4,128)(2,1)}, u32[]{:S(2)}) copy-start(bf16[184,4,256]{2,1,0:T(4,128)(2,1)} %get-tuple-element.10) | copy-start | bytes 1130500
  4.3 36.1 %all-to-all-start = ((bf16[64,16,384]{2,1,0:T(8,128)(2,1)}), bf16[64,16,384]{2,1,0:T(8,128)(2,1)S(1)}, u32[]{:S(2)}, u32[]{:S(2)}) async-start(bf16[64,16,384]{2,1,0:T(8,128)(2,1)} %get-tuple-element.13), calls=%async_computation | async-start | bytes 1572864 | tf_op jit(solution)/shard_map/all_to_all | solution.py:517
  19.8 34.1 %collective-permute-start = (bf16[184,4,256]{2,1,0:T(4,128)(2,1)S(1)}, bf16[184,4,256]{2,1,0:T(4,128)(2,1)S(1)}, u32[]{:S(2)}, u32[]{:S(2)}) collective-permute-start(bf16[184,4,256]{2,1,0:T(4,128)(2,1)S(1)} %copy-done), channel_id=1, source_target_pairs={{0,4},{4,8},{8,12},{12,16},{16,20},{20,24},{24,28},{28,32},{32,36}... | collective-permute-start | bytes 1130504 | tf_op jit(solution)/shard_map/ppermute | solution.py:512
  42.8 35.7 %all-to-all-start.1 = ((bf16[64,8,384]{2,1,0:T(8,128)(2,1)}), bf16[64,8,384]{2,1,0:T(8,128)(2,1)S(1)}, u32[]{:S(2)}, u32[]{:S(2)}) async-start(bf16[64,8,384]{2,1,0:T(8,128)(2,1)} %route.1), calls=%async_computation.1 | async-start | bytes 786432 | tf_op jit(solution)/shard_map/all_to_all | solution.py:517
  66.0 10.2 %collective-permute-start.1 = (bf16[180,4,256]{2,1,0:T(4,128)(2,1)}, bf16[180,4,256]{2,1,0:T(4,128)(2,1)S(1)}, u32[]{:S(2)}, u32[]{:S(2)}) collective-permute-start(bf16[180,4,256]{2,1,0:T(4,128)(2,1)} %get-tuple-element.12), channel_id=1, source_target_pairs={{0,252},{4,0},{8,4},{12,8},{16,12},{20,16},{24,20},{28,24},{32,28}... | collective-permute-start | bytes 1105928 | tf_op jit(solution)/shard_map/ppermute | solution.py:512

commit v7 on v6

--- a/solution.py
+++ b/solution.py
@@ -17,6 +17,7 @@
 SHIFT = 4
 CAP = 8
 TAIL = CHAN - 128
+LEAD = 41
 EPSILON = 1e-05
 
 F32 = jnp.float32
@@ -351,7 +352,7 @@
         active = (keep == 1) & (position < count_ref[0])
         running = jnp.where(window_of == w, jnp.where(active, 1.0, 0.0), running)
         placed = active & (slot < CAP)
-        dest = jnp.where(placed, bands - 1 - dest_ref[0, tile], bands).astype(F32)
+        dest = jnp.where(placed, (LEAD - dest_ref[0, tile]) & (bands - 1), bands).astype(F32)
         place = jnp.where(placed, slot * TILE + (position & 1), 0).astype(F32)
         first = 2 * (w // half)
         here = row == w % half
@@ -388,7 +389,7 @@
         out_specs=[VMEM] * 2,
         out_shape=[
             jax.ShapeDtypeStruct((TOKENS, half, 384), BF16),
-            jax.ShapeDtypeStruct((channels + 4, SHIFT, columns), BF16),
+            pltpu.VMEM((channels + 4, SHIFT, columns), BF16),
         ],
         scratch_shapes=[flat, flat],
         cost_estimate=pl.CostEstimate(
@@ -408,7 +409,7 @@
     lane = iota((8, 128), 1) - 2 * TAIL - 2 * row
     pick = jnp.where(row < 2, jnp.where(lane == 0, 16.0, jnp.where(lane == 1, 1.0, 0.0)), 0.0)
     codes = dot(pick.astype(BF16), tails, 1, 1)
-    behind = bands - 1 - lax.axis_index("band") >= TOKENS // 2
+    behind = (LEAD - lax.axis_index("band")) & (bands - 1) >= TOKENS // 2
     codes = jnp.where(behind, pltpu.roll(codes, sources - half, 1), codes)
     low, high = codes[0:1].astype(jnp.int32), codes[1:2].astype(jnp.int32)
     chunk = 256
@@ -486,7 +487,7 @@
         return carry
 
     lax.fori_loop(0, CAP // pairs, some_slots, 0)
-    out_ref[...] = done[...].reshape(CHAN, CAP, PAIR).astype(BF16)
+    out_ref[...] = done[0 : CHAN * CAP, :].reshape(CHAN, CAP, PAIR).astype(BF16)
 
 
 def work_path(got, bias, gain, wqv, wk, proj):
@@ -497,7 +498,7 @@
         out_shape=jax.ShapeDtypeStruct((CHAN, CAP, PAIR), BF16),
         scratch_shapes=[
             pltpu.VMEM((TILE + 1, TOKENS * CAP, 128), F32),
-            pltpu.VMEM((CHAN * CAP, PAIR), F32),
+            pltpu.VMEM((-(-CHAN // 8) * 8 * CAP, PAIR), F32),
         ],
         cost_estimate=pl.CostEstimate(
             flops=8_000_000_000, bytes_accessed=2_000_000, transcendentals=1_000_000
@@ -513,7 +514,7 @@
 
 
 def exchange(value):
-    order = tuple(range(lax.axis_size("band")))[::-1]
+    order = tuple((LEAD - j) % lax.axis_size("band") for j in range(lax.axis_size("band")))
     return lax.all_to_all(
         value, "band", split_axis=0, concat_axis=0, axis_index_groups=[order], tiled=True
     )
@@ -536,7 +537,7 @@
     gain_attn, gain_mlp = gain_attn[None], gain_mlp[None]
     pixels = jnp.transpose(pixels, (2, 0, 1))
     outgoing, edge = spread(keep_mask, band_counts, plan_dest, plan_slot, pixels)
-    halo = from_behind(edge, "band", 1)
+    halo = from_behind(in_vmem(edge), "band", 1)
     gathered = exchange(outgoing)
     sent, kept, wqv, wk, proj, bias = own_path(
         pixels,

time: 83.3 us -> 83.3 us (level)
  the two profiles are of different devices: /device:TPU:8 before, /device:TPU:1 now
where the time goes in v7:
time: 83.3 us; the launch traced here: 81.9 us
  starting transfers between devices  30.9 us (37%)
  waiting for transfers between devices  25.8 us (31%)
  Pallas kernels  21.7 us (26%)
  other arithmetic  2.21 us (3%)
  between operations  1.31 us (2%)
    all_to_all x2, starting transfers between devices, exchange(): lax.all_to_all(value, 'band', split_axis=0, concat_axis=0, axis_index_gro...  30.2 us
    all_to_all x2, waiting for transfers between devices, exchange(): lax.all_to_all(value, 'band', split_axis=0, concat_axis=0, axis_index_gro...  16.5 us
    pallas_call x1, Pallas kernels, own_path(): pl.pallas_call(own_kernel, in_specs=[VMEM] * 9, out_specs=[VMEM] * 6, out...  12 us
    ppermute x2, waiting for transfers between devices, from_behind(): return lax.ppermute(value, axis, pairs)  9.32 us
    pallas_call x1, Pallas kernels, work_path(): pl.pallas_call(work_kernel, in_specs=[VMEM] * 6, out_specs=VMEM, out_shap...  4.42 us
    pallas_call x1, Pallas kernels, spread(): pl.pallas_call(spread_kernel, in_specs=[SMEM] * 4 + [VMEM], out_specs=[VM...  2.93 us
    pallas_call x1, Pallas kernels, route(): pl.pallas_call(route_kernel, in_specs=[VMEM], out_specs=VMEM, out_shape=j...  2.33 us
    transpose x1, other arithmetic, shards(): restored = jnp.transpose(restored, (1, 2, 0))  2.21 us
  transfers between devices with their start and end apart: 4, of which 2 were waited for; matrix products, arithmetic and copies ran while one was open for 3% of the time, Pallas kernels for 18%

profile of v7, /device:TPU:1, one launch (start us, length us, event | category | flops | bytes accessed | tf_op | source)
XLA Modules:
  0.0 81.9 jit_solution(4883978734906823524)
XLA Ops:
  1.3 2.9 %spread.1 = (bf16[64,16,384]{2,1,0:T(8,128)(2,1)}, bf16[184,4,256]{2,1,0:T(4,128)(2,1)S(1)}) custom-call(s32[1,32]{1,0:T(1,128)} %keep_ref.1, s32[1]{0:T(128)S(6)} %copy.14.count_ref, s32[1,16]{1,0:T(1,128)} %dest_ref.1, s32[1,16]{1,0:T(1,128)} %slot_ref.1, bf16[180,8,256]{2,1,0:T(8,128)(2,1)} %bitcast.8), custom_call_target="tpu_custom_call" | custom-call | flops 500000000 | bytes 2000000 | tf_op jit(solution)/shard_map/spread/pallas_call | solution.py:386
  4.2 17.2 %all-to-all-start = ((bf16[64,16,384]{2,1,0:T(8,128)(2,1)}), bf16[64,16,384]{2,1,0:T(8,128)(2,1)S(1)}, u32[]{:S(2)}, u32[]{:S(2)}) async-start(bf16[64,16,384]{2,1,0:T(8,128)(2,1)} %get-tuple-element.13), calls=%async_computation | async-start | bytes 1572864 | tf_op jit(solution)/shard_map/all_to_all | solution.py:518
  21.4 0.4 collective-permute-start
  21.7 16.5 %all-to-all-done.got_ref = bf16[64,16,384]{2,1,0:T(8,128)(2,1)S(1)} async-done(((bf16[64,16,384]{2,1,0:T(8,128)(2,1)}), bf16[64,16,384]{2,1,0:T(8,128)(2,1)S(1)}, u32[]{:S(2)}, u32[]{:S(2)}) %all-to-all-start) | async-done | bytes 786464 | tf_op jit(solution)/shard_map/all_to_all | solution.py:518
  38.2 2.3 %route.1 = bf16[64,8,384]{2,1,0:T(8,128)(2,1)} custom-call(bf16[64,16,384]{2,1,0:T(8,128)(2,1)S(1)} %all-to-all-done.got_ref), custom_call_target="tpu_custom_call" | custom-call | flops 1200000000 | bytes 1200000 | tf_op jit(solution)/shard_map/route/pallas_call | solution.py:447
  40.5 13.1 %all-to-all-start.1 = ((bf16[64,8,384]{2,1,0:T(8,128)(2,1)}), bf16[64,8,384]{2,1,0:T(8,128)(2,1)S(1)}, u32[]{:S(2)}, u32[]{:S(2)}) async-start(bf16[64,8,384]{2,1,0:T(8,128)(2,1)} %route.1), calls=%async_computation.1 | async-start | bytes 786432 | tf_op jit(solution)/shard_map/all_to_all | solution.py:518
  53.6 0.0 collective-permute-done.halo_ref
  53.6 12.0 %own_path.1 = (bf16[180,4,256]{2,1,0:T(4,128)(2,1)}, bf16[180,4,256]{2,1,0:T(4,128)(2,1)}, bf16[384,180]{1,0:T(8,128)(2,1)S(1)}, bf16[180,768]{1,0:T(8,128)(2,1)...) custom-call(bf16[180,8,256]{2,1,0:T(8,128)(2,1)} %bitcast.9, ...), custom_call_target="tpu_custom_call" | custom-call | flops 20000000000 | bytes 3000000 | tf_op jit(solution)/shard_map/own_path/pallas_call | solution.py:293
  65.6 0.3 collective-permute-start.1
  65.9 9.3 %collective-permute-done.1 = bf16[180,4,256]{2,1,0:T(4,128)(2,1)S(1)} collective-permute-done((bf16[180,4,256]{2,1,0:T(4,128)(2,1)}, bf16[180,4,256]{2,1,0:T(4,128)(2,1)S(1)}, u32[]{:S(2)}, u32[]{:S(2)}) %collective-permute-start.1) | collective-permute-done | bytes 368672 | tf_op jit(solution)/shard_map/ppermute | solution.py:513
  75.2 2.2 %maximum_bitcast_fusion = bf16[8,256,180]{1,0,2:T(8,128)(2,1)} fusion(bf16[180,4,256]{2,1,0:T(4,128)(2,1)S(1)} %collective-permute-done.1, bf16[180,4,256]{2,1,0:T(4,128)(2,1)} %get-tuple-element.11), kind=kLoop, calls=%fused_computation | loop fusion | flops 1474560 | bytes 1474560 | tf_op jit(solution)/shard_map/transpose | solution.py:557
  77.5 0.0 all-to-all-done.1.got_ref
  77.5 4.4 %work_path.1 = bf16[180,8,128]{2,1,0:T(8,128)(2,1)} custom-call(bf16[64,8,384]{2,1,0:T(8,128)(2,1)S(1)} %all-to-all-done.1.got_ref, f32[6,64,128]{2,1,0:T(8,128)S(1)} %get-tuple-element.14.bias_ref, f32[1,180]{1,0:T(1,128)} %bitcast.14, bf16[384,180]{1,0:T(8,128)(2,1)S(1)} %get-tuple-element.15.wqv_ref, bf16[180,768]{1,0:T(8,128)(2,1)S(1)} %get-tuple-element.16.wk_ref, ...), custom_call_target="tpu_custom_call" | custom-call | flops 8000000000 | bytes 2000000 | tf_op jit(solution)/shard_map/work_path/pallas_call | solution.py:494
Async XLA Ops:
  4.2 34.0 %all-to-all-start = ((bf16[64,16,384]{2,1,0:T(8,128)(2,1)}), bf16[64,16,384]{2,1,0:T(8,128)(2,1)S(1)}, u32[]{:S(2)}, u32[]{:S(2)}) async-start(bf16[64,16,384]{2,1,0:T(8,128)(2,1)} %get-tuple-element.13), calls=%async_computation | async-start | bytes 1572864 | tf_op jit(solution)/shard_map/all_to_all | solution.py:518
  21.4 32.2 %collective-permute-start = (bf16[184,4,256]{2,1,0:T(4,128)(2,1)S(1)}, bf16[184,4,256]{2,1,0:T(4,128)(2,1)S(1)}, u32[]{:S(2)}, u32[]{:S(2)}) collective-permute-start(bf16[184,4,256]{2,1,0:T(4,128)(2,1)S(1)} %get-tuple-element.10), channel_id=1, source_target_pairs={{0,4},{4,8},{8,12},{12,16},{16,20},{20,24},{24,28},{28,32},{32,36}... | collective-permute-start | bytes 1130504 | tf_op jit(solution)/shard_map/ppermute | solution.py:513
  40.5 36.9 %all-to-all-start.1 = ((bf16[64,8,384]{2,1,0:T(8,128)(2,1)}), bf16[64,8,384]{2,1,0:T(8,128)(2,1)S(1)}, u32[]{:S(2)}, u32[]{:S(2)}) async-start(bf16[64,8,384]{2,1,0:T(8,128)(2,1)} %route.1), calls=%async_computation.1 | async-start | bytes 786432 | tf_op jit(solution)/shard_map/all_to_all | solution.py:518
  65.6 9.6 %collective-permute-start.1 = (bf16[180,4,256]{2,1,0:T(4,128)(2,1)}, bf16[180,4,256]{2,1,0:T(4,128)(2,1)S(1)}, u32[]{:S(2)}, u32[]{:S(2)}) collective-permute-start(bf16[180,4,256]{2,1,0:T(4,128)(2,1)} %get-tuple-element.12), channel_id=1, source_target_pairs={{0,252},{4,0},{8,4},{12,8},{16,12},{20,16},{24,20},{28,24},{32,28}... | collective-permute-start | bytes 1105928 | tf_op jit(solution)/shard_map/ppermute | solution.py:513
